TPU v7x, 16 devices: a whole 2x2x2 slice. The times are simulated.
16 devices in a mesh: etp: 4 (over z, y), ep: 4 (over x, core).
Axes of the slice: x: 2, y: 2, z: 2, core: 2. Of those that a mesh axis runs over, the one named last changes fastest.
Arguments:
- hidden: bfloat16 [32768, 768], P(('ep', 'etp'))
- w_router: float32 [768, 8], replicated
- expert_ids: int32 [32768, 2], P(('ep', 'etp'))
- d_out: bfloat16 [32768, 768], P(('ep', 'etp'))
- w_gate: bfloat16 [8, 768, 4096], P('ep', None, 'etp')
- w_up: bfloat16 [8, 768, 4096], P('ep', None, 'etp')
- w_down: bfloat16 [8, 4096, 768], P('ep', 'etp')
Outputs:
- output 1: bfloat16 [32768, 768], P(('ep', 'etp'))
- output 2: bfloat16 [32768, 768], P(('ep', 'etp'))
- output 3: float32 [768, 8], replicated
- output 4: float32 [], replicated
- output 5: float32 [8, 768, 4096], P('ep', None, 'etp')
- output 6: float32 [8, 768, 4096], P('ep', None, 'etp')
- output 7: float32 [8, 4096, 768], P('ep', 'etp')
All inputs are finite; a program needn't handle non-finite values.
Results may differ from a plain program's by a relative error of at most 0.0089382.
Values are sent between devices in bfloat16 or wider.
A program may use at most 1 GiB of HBM per device.

v0:
```python
import functools
import jax
import jax.numpy as jnp
from jax import lax
from jax.experimental import pallas as pl
from jax.experimental.pallas import tpu as pltpu
from jax.sharding import PartitionSpec as P


AUX_COEF = 0.01
OUT_SCALE = 2.0
BF16 = jnp.bfloat16
F32 = jnp.float32
I32 = jnp.int32
VMEM_LIMIT = 62 * 1024 * 1024


N_SHIFT = 8
TOK_TILE = 256
ROW_TILE = 512
ALIGN = 16
WIN = TOK_TILE + ALIGN


def coords(i):
    return (i >> 3) & 1, (i >> 2) & 1, (i >> 1) & 1, i & 1


def index_of(z, y, x, c):
    return (z << 3) | (y << 2) | (x << 1) | c


def shift_dest(i, s):
    z, y, x, c = coords(i)
    x, c, d = x ^ ((s >> 2) & 1), c ^ ((s >> 1) & 1), s & 1
    return index_of(z, y ^ d, x, c) if c == 0 else index_of(z ^ d, y, x, c)


def split_partner(i):
    z, y, x, c = coords(i)
    return index_of(z, y ^ 1, x, c) if c == 0 else index_of(z ^ 1, y, x, c)


def twin_partner(i):
    z, y, x, c = coords(i)
    return index_of(z ^ 1, y, x, c) if c == 0 else index_of(z, y ^ 1, x, c)


def dot_nn(a, b):
    return lax.dot_general(a, b, (((1,), (0,)), ((), ())), preferred_element_type=F32)


def dot_nt(a, b):
    return lax.dot_general(a, b, (((1,), (1,)), ((), ())), preferred_element_type=F32)


def dot_tn(a, b):
    return lax.dot_general(a, b, (((0,), (0,)), ((), ())), preferred_element_type=F32)


def iota(shape, dim):
    return lax.broadcasted_iota(I32, shape, dim)


def tile_columns(ids_t, starts, limits, n_experts, upper):
    tokens = ids_t.shape[1]
    e_iota = iota((n_experts, tokens), 0)
    hot0 = ids_t[0:1, :] == e_iota
    hot1 = ids_t[1:2, :] == e_iota
    either = jnp.where(hot0 | hot1, 1.0, 0.0).astype(BF16)
    before = dot_nn(either, upper).astype(I32)
    offset = jnp.zeros((n_experts, tokens), I32)
    bound = jnp.zeros((n_experts, tokens), I32)
    for e in range(n_experts):
        offset = jnp.where(e_iota == e, e * WIN + (starts[e] & (ALIGN - 1)), offset)
        if limits is not None:
            bound = jnp.where(e_iota == e, limits[e] - starts[e], bound)
    column = before + offset
    if limits is not None:
        column = jnp.where(before < bound, column, -1)
    return [jnp.sum(jnp.where(hot, column, 0), axis=0, keepdims=True) for hot in (hot0, hot1)]


def strict_upper(n):
    return jnp.where(iota((n, n), 0) < iota((n, n), 1), 1.0, 0.0).astype(BF16)


def add_windows(buf, value, starts, n_experts):
    for e in range(n_experts):
        rows = pl.ds(pl.multiple_of(starts[e] - (starts[e] & (ALIGN - 1)), ALIGN), WIN)
        buf[e, rows, :] = buf[e, rows, :] + value[e * WIN:(e + 1) * WIN, :]


def slots_out(buf, order_ref, outs, sem):
    slots = outs[0].shape[0]
    copies = [pltpu.make_async_copy(buf.at[order_ref[s], pl.ds(0, slots), :], outs[s], sem.at[s]) for s in range(N_SHIFT)]
    for copy in copies:
        copy.start()
    for copy in copies:
        copy.wait()


def counts_kernel(n_dev, etp_size, ids_ref, table_ref, mine_ref, send_sem, recv_sem):
    etp, ep = lax.axis_index("etp"), lax.axis_index("ep")
    ep_size = n_dev // etp_size
    me = ep * etp_size + etp
    tokens = ids_ref.shape[1]
    e_iota = iota((128, tokens), 0)
    hot = (ids_ref[0:1, :] == e_iota) | (ids_ref[1:2, :] == e_iota)
    counts = dot_nt(jnp.ones((8, tokens), BF16), jnp.where(hot, 1.0, 0.0).astype(BF16)).astype(I32)
    mine_ref[...] = counts
    table_ref[me] = counts

    def peer(k):
        return {"ep": lax.rem(ep + k // etp_size, ep_size), "etp": lax.rem(etp + k % etp_size, etp_size)}

    barrier = pltpu.get_barrier_semaphore()
    for k in range(1, n_dev):
        pl.semaphore_signal(barrier, inc=1, device_id=peer(k), device_id_type=pl.DeviceIdType.MESH)
    pl.semaphore_wait(barrier, n_dev - 1)
    copies = [pltpu.make_async_remote_copy(
        src_ref=mine_ref, dst_ref=table_ref.at[me], send_sem=send_sem.at[k], recv_sem=recv_sem.at[k],
        device_id=peer(k), device_id_type=pl.DeviceIdType.MESH) for k in range(1, n_dev)]
    for copy in copies:
        copy.start()
    for copy in copies:
        copy.wait()


def x_slots_kernel(order_ref, ids_ref, h_ref, base_ref, *rest):
    outs, (buf, base_s, sem, base_sem) = rest[:N_SHIFT], rest[N_SHIFT:]
    n_experts, tokens = base_ref.shape[0], ids_ref.shape[1]
    e_iota = iota((n_experts, tokens), 0)
    hot = (ids_ref[0:1, :] == e_iota) | (ids_ref[1:2, :] == e_iota)
    earlier = jnp.where(iota((tokens, 128), 0) < TOK_TILE * iota((tokens, 128), 1), 1.0, 0.0).astype(BF16)
    base_ref[...] = dot_nn(jnp.where(hot, 1.0, 0.0).astype(BF16), earlier).astype(I32)
    copy = pltpu.make_async_copy(base_ref, base_s, base_sem)
    copy.start()
    buf[...] = jnp.zeros_like(buf)
    copy.wait()
    upper = strict_upper(TOK_TILE)

    @pl.loop(0, tokens // TOK_TILE)
    def _(t):
        here = pl.ds(pl.multiple_of(t * TOK_TILE, TOK_TILE), TOK_TILE)
        starts = [base_s[e, t] for e in range(n_experts)]
        col0, col1 = tile_columns(ids_ref[:, here], starts, None, n_experts, upper)
        row = iota((n_experts * WIN, TOK_TILE), 0)
        pick = jnp.where((row == col0) | (row == col1), 1.0, 0.0).astype(BF16)
        add_windows(buf, dot_nn(pick, h_ref[here, :]).astype(BF16), starts, n_experts)

    slots_out(buf, order_ref, outs, sem)


def c_slots_kernel(order_ref, base_s, limit_s, ids_ref, h_ref, dy_ref, wr3_ref, info_ref, psum_ref, *rest):
    outs, (buf, prob_buf, sem) = rest[:N_SHIFT], rest[N_SHIFT:]
    n_experts, tokens = psum_ref.shape[0], ids_ref.shape[1]
    parts = dot_nt(wr3_ref[...], h_ref[...])
    logits = parts[2 * n_experts:3 * n_experts] + parts[n_experts:2 * n_experts] + parts[0:n_experts]
    top = jnp.max(logits, axis=0, keepdims=True)
    expo = jnp.exp(logits - top)
    prob = expo / jnp.sum(expo, axis=0, keepdims=True)
    prob_buf[...] = prob
    psum_ref[...] = jnp.broadcast_to(jnp.sum(prob, axis=1, keepdims=True), psum_ref.shape)
    buf[...] = jnp.zeros_like(buf)
    upper = strict_upper(TOK_TILE)
    limits = [limit_s[e] for e in range(n_experts)]

    @pl.loop(0, tokens // TOK_TILE)
    def _(t):
        here = pl.ds(pl.multiple_of(t * TOK_TILE, TOK_TILE), TOK_TILE)
        starts = [base_s[e, t] for e in range(n_experts)]
        ids_t = ids_ref[:, here]
        p_t = prob_buf[:, here]
        e_iota = iota((n_experts, TOK_TILE), 0)
        p0 = jnp.sum(jnp.where(ids_t[0:1, :] == e_iota, p_t, 0.0), axis=0, keepdims=True)
        p1 = jnp.sum(jnp.where(ids_t[1:2, :] == e_iota, p_t, 0.0), axis=0, keepdims=True)
        total = p0 + p1
        g0, g1 = p0 / total, p1 / total
        col0, col1 = tile_columns(ids_t, starts, limits, n_experts, upper)
        row = iota((n_experts * WIN, TOK_TILE), 0)
        is0, is1 = row == col0, row == col1
        pick = jnp.where(is0 | is1, 1.0, 0.0).astype(BF16)
        gate = jnp.sum(jnp.where(is0, g0, jnp.where(is1, g1, 0.0)), axis=1, keepdims=True)
        mixed = OUT_SCALE * dot_nn(pick, dy_ref[here, :])
        add_windows(buf, (gate * mixed).astype(BF16), starts, n_experts)
        group = iota((8, TOK_TILE), 0)
        extra = jnp.zeros((8, TOK_TILE), F32)
        for k, v in enumerate((g0, g1, col0.astype(F32), col1.astype(F32), ids_t[0:1, :].astype(F32), ids_t[1:2, :].astype(F32))):
            extra = jnp.where(group == k, v, extra)
        table = jnp.concatenate([p_t] * 6 + [extra, jnp.zeros((128 - 6 * n_experts - 8, TOK_TILE), F32)], axis=0)
        info_ref[here, :] = table.T

    slots_out(buf, order_ref, outs, sem)


def pack_kernel(count_s, offset_s, *refs):
    ins, out_ref, (buf, sem, out_sem) = refs[:N_SHIFT], refs[N_SHIFT], refs[N_SHIFT + 1:]
    sizes = [512, 256, 128, 64, 32, 16]

    def for_parts(act):
        for s in range(N_SHIFT):
            count, offset = count_s[s], offset_s[s]
            done = jnp.int32(0)
            for j, size in enumerate(sizes):
                has = (count & size) != 0
                start = pl.multiple_of(done, ALIGN)
                dest = pl.multiple_of(offset + done, ALIGN)

                @pl.when(has)
                def _(s=s, j=j, size=size, start=start, dest=dest):
                    act(pltpu.make_async_copy(ins[s].at[pl.ds(start, size), :], buf.at[pl.ds(dest, size), :], sem.at[s, j]))

                done = done + jnp.where(has, size, 0)

    for_parts(lambda copy: copy.start())
    total = pl.multiple_of(offset_s[N_SHIFT], ALIGN)
    buf[pl.ds(total, ROW_TILE), :] = jnp.zeros((ROW_TILE, buf.shape[1]), buf.dtype)
    for_parts(lambda copy: copy.wait())
    copy = pltpu.make_async_copy(buf.at[pl.ds(0, out_ref.shape[0]), :], out_ref, out_sem)
    copy.start()
    copy.wait()


def rows_out(buf, offset_s, outs, sem):
    slots = outs[0].shape[0]
    copies = [pltpu.make_async_copy(buf.at[pl.ds(pl.multiple_of(offset_s[s], ALIGN), slots), :], outs[s], sem.at[s]) for s in range(N_SHIFT)]
    for copy in copies:
        copy.start()
    for copy in copies:
        copy.wait()


def forward_kernel(n_ref, offset_s, x_ref, w1_ref, w3_ref, w2_ref, *rest, first, last):
    rest = list(rest)
    y_in = None if first else rest.pop(0)
    a_ref, b_ref = rest.pop(0), rest.pop(0)
    if last:
        outs, (buf, sem) = rest[:N_SHIFT], rest[N_SHIFT:]
    else:
        (y_out,) = rest
    i = pl.program_id(0)

    @pl.when(i < n_ref[0])
    def _():
        a = dot_nn(x_ref[...], w1_ref[...])
        b = dot_nn(x_ref[...], w3_ref[...])
        a_ref[...] = a
        b_ref[...] = b
        y = dot_nn((a * jax.nn.sigmoid(a) * b).astype(BF16), w2_ref[...])
        if not first:
            y = y_in[...] + y
        if last:
            buf[pl.ds(pl.multiple_of(i * ROW_TILE, ROW_TILE), ROW_TILE), :] = y.astype(BF16)
        else:
            y_out[...] = y

    if last:
        @pl.when(i == pl.num_programs(0) - 1)
        def _():
            rows_out(buf, offset_s, outs, sem)


def clear(refs):
    @pl.when(pl.program_id(0) == 0)
    def _():
        for ref in refs:
            ref[...] = jnp.zeros_like(ref)


def act_grads(c_ref, a_ref, b_ref, w2_ref):
    du = dot_nt(c_ref[...], w2_ref[...])
    a, b = a_ref[...], b_ref[...]
    sig = jax.nn.sigmoid(a)
    silu = a * sig
    da = (du * b * sig * (1.0 + a * (1.0 - sig))).astype(BF16)
    return da, (du * silu).astype(BF16), (silu * b).astype(BF16)


def add_weight_grads(x, c, da, db, u, g1_ref, g3_ref, g2_ref):
    g1_ref[...] += dot_tn(x, da)
    g3_ref[...] += dot_tn(x, db)
    g2_ref[...] += dot_tn(u, c)


def backward_kernel(n_ref, offset_s, x_ref, c_ref, a_ref, b_ref, w1_ref, w3_ref, w2_ref, *rest, first):
    dx_in = None if first else rest[0]
    g1_ref, g3_ref, g2_ref, dx_out = rest[-4:]
    clear((g1_ref, g3_ref, g2_ref))

    @pl.when(pl.program_id(0) < n_ref[0])
    def _():
        da, db, u = act_grads(c_ref, a_ref, b_ref, w2_ref)
        dx = dot_nt(da, w1_ref[...]) + dot_nt(db, w3_ref[...])
        dx_out[...] = dx if first else dx_in[...] + dx
        add_weight_grads(x_ref[...], c_ref[...], da, db, u, g1_ref, g3_ref, g2_ref)


def backward_rows_kernel(n_ref, offset_s, c_ref, a_ref, b_ref, w1_ref, w3_ref, w2_ref, dx_in, da_ref, db_ref, u_ref, *rest):
    outs, (buf, sem) = rest[:N_SHIFT], rest[N_SHIFT:]
    i = pl.program_id(0)

    @pl.when(i < n_ref[0])
    def _():
        da, db, u = act_grads(c_ref, a_ref, b_ref, w2_ref)
        da_ref[...] = da
        db_ref[...] = db
        u_ref[...] = u
        dx = dx_in[...] + (dot_nt(da, w1_ref[...]) + dot_nt(db, w3_ref[...]))
        buf[pl.ds(pl.multiple_of(i * ROW_TILE, ROW_TILE), ROW_TILE), :] = dx.astype(BF16)

    @pl.when(i == pl.num_programs(0) - 1)
    def _():
        rows_out(buf, offset_s, outs, sem)


def weight_grads_kernel(n_ref, offset_s, x_ref, c_ref, da_ref, db_ref, u_ref, g1_ref, g3_ref, g2_ref):
    clear((g1_ref, g3_ref, g2_ref))

    @pl.when(pl.program_id(0) < n_ref[0])
    def _():
        add_weight_grads(x_ref[...], c_ref[...], da_ref[...], db_ref[...], u_ref[...], g1_ref, g3_ref, g2_ref)


def load_slots(order_ref, ins, buf, sem):
    slots = ins[0].shape[0]
    copies = [pltpu.make_async_copy(ins[s], buf.at[order_ref[s], pl.ds(0, slots), :], sem.at[s]) for s in range(N_SHIFT)]
    for copy in copies:
        copy.start()
    for copy in copies:
        copy.wait()


def gather_windows(buf, window, base_s, kept_s, t, n_experts):
    for e in range(n_experts):
        start = base_s[e, t] - (base_s[e, t] & (ALIGN - 1))
        rows = buf[e, pl.ds(pl.multiple_of(start, ALIGN), WIN), :]
        valid = iota(rows.shape, 0) < kept_s[e] - start
        window[e * WIN:(e + 1) * WIN, :] = jnp.where(valid, rows, jnp.zeros_like(rows))


def y_combine_kernel(order_ref, base_s, kept_s, *refs):
    ins, refs = refs[:N_SHIFT], refs[N_SHIFT:]
    info_ref, h_ref, dy_ref, w_ref, out_ref, dz_ref, dwr_ref, buf, window, sem = refs
    n_experts = buf.shape[0]
    t = pl.program_id(0)

    @pl.when(t == 0)
    def _():
        load_slots(order_ref, ins, buf, sem)
        dwr_ref[...] = jnp.zeros_like(dwr_ref)

    gather_windows(buf, window, base_s, kept_s, t, n_experts)
    info = info_ref[...]
    k0 = 6 * n_experts
    g0, g1, col0, col1, e0, e1 = [info[:, k0 + k:k0 + k + 1] for k in range(6)]
    col = iota((TOK_TILE, n_experts * WIN), 1)
    pick0 = jnp.where(col == col0.astype(I32), 1.0, 0.0).astype(BF16)
    pick1 = jnp.where(col == col1.astype(I32), 1.0, 0.0).astype(BF16)
    y0 = dot_nn(pick0, window[...])
    y1 = dot_nn(pick1, window[...])
    h = h_ref[...]
    mix = OUT_SCALE * dy_ref[...].astype(F32)
    out_ref[...] = (h.astype(F32) + OUT_SCALE * (g0 * y0 + g1 * y1)).astype(BF16)
    dg0 = jnp.sum(mix * y0, axis=1, keepdims=True)
    dg1 = jnp.sum(mix * y1, axis=1, keepdims=True)
    lane = iota(info.shape, 1)
    prob = jnp.where(lane < k0, info, 0.0)
    weight = w_ref[...]
    mean_w = jnp.sum(jnp.where(lane < n_experts, prob * weight, 0.0), axis=1, keepdims=True)
    expert = (lane & (n_experts - 1)).astype(F32)
    sign = jnp.where(expert == e0, 1.0, 0.0) - jnp.where(expert == e1, 1.0, 0.0)
    dz = prob * (weight - mean_w) + g0 * g1 * (dg0 - dg1) * jnp.where(lane < k0, sign, 0.0)
    d1 = dz.astype(BF16)
    rem1 = dz - d1.astype(F32)
    d2 = rem1.astype(BF16)
    d3 = (rem1 - d2.astype(F32)).astype(BF16)
    group = lane // n_experts
    first = (group == 0) | (group == 1) | (group == 3)
    second = (group == 2) | (group == 4)
    dzp = jnp.where(first, d1.astype(F32), jnp.where(second, d2.astype(F32), d3.astype(F32))).astype(BF16)
    dz_ref[...] = dzp
    dwr_ref[...] += dot_tn(dzp, h)


def dx_combine_kernel(order_ref, base_s, kept_s, *refs):
    ins, refs = refs[:N_SHIFT], refs[N_SHIFT:]
    info_ref, dz_ref, dy_ref, wr_ref, out_ref, buf, window, sem = refs
    n_experts = buf.shape[0]
    t = pl.program_id(0)

    @pl.when(t == 0)
    def _():
        load_slots(order_ref, ins, buf, sem)

    gather_windows(buf, window, base_s, kept_s, t, n_experts)
    info = info_ref[...]
    k0 = 6 * n_experts
    col0, col1 = info[:, k0 + 2:k0 + 3].astype(I32), info[:, k0 + 3:k0 + 4].astype(I32)
    col = iota((TOK_TILE, n_experts * WIN), 1)
    pick = jnp.where((col == col0) | (col == col1), 1.0, 0.0).astype(BF16)
    total = dy_ref[...].astype(F32) + dot_nn(pick, window[...]) + dot_nn(dz_ref[...], wr_ref[...])
    out_ref[...] = total.astype(BF16)


def finish_kernel(j_ref, own_ref, part_ref, other_ref, out_ref):
    own = pl.program_id(0) == 0

    @pl.when(own)
    def _():
        out_ref[0] = own_ref[...] + part_ref[...]

    @pl.when(jnp.logical_not(own))
    def _():
        out_ref[0] = other_ref[...]


def params(*semantics):
    return pltpu.CompilerParams(dimension_semantics=semantics or None, vmem_limit_bytes=VMEM_LIMIT)


def hbm():
    return pl.BlockSpec(memory_space=pl.ANY)


def smem():
    return pl.BlockSpec(memory_space=pltpu.SMEM)


def vmem():
    return pl.BlockSpec(memory_space=pltpu.VMEM)


def cost(flops, nbytes):
    return pl.CostEstimate(flops=int(flops), bytes_accessed=int(nbytes), transcendentals=0)


def split3(v):
    p1 = v.astype(BF16)
    r1 = v - p1.astype(F32)
    p2 = r1.astype(BF16)
    return p1, p2, (r1 - p2.astype(F32)).astype(BF16)


def solution(mesh):
    ep_size = mesh.shape["ep"]
    etp_size = mesh.shape["etp"]
    n_dev = ep_size * etp_size
    all_axes = ("ep", "etp")
    dev_axes = ("etp", "ep")
    tok_spec = P(all_axes, None)
    gate_spec = P("ep", None, "etp")
    down_spec = P("ep", "etp", None)

    def layer(hidden, w_router, expert_ids, d_out, w_gate, w_up, w_down):
        tok_rows, d_model = hidden.shape
        n_experts = w_router.shape[1]
        n_tokens = tok_rows * n_dev
        capacity = (5 * n_tokens + 2 * n_experts - 1) // (2 * n_experts)
        slots = 7 * tok_rows // (2 * n_experts)
        width = w_gate.shape[2]
        rows = N_SHIFT * slots
        buf_rows = slots + WIN + ALIGN
        etp, ep = lax.axis_index("etp"), lax.axis_index("ep")
        z, y, x, c = etp >> 1, etp & 1, ep >> 1, ep & 1
        mine = jnp.where(c == 0, y, z)

        def permute(values, pairs):
            return [lax.ppermute(v, dev_axes, pairs) for v in values]

        def exchange(parts, pairs):
            out = [parts[0]]
            for s in range(1, N_SHIFT):
                out.append(lax.ppermute(parts[s], dev_axes, pairs[s]))
            return out

        forth = [[(i, shift_dest(i, s)) for i in range(n_dev)] for s in range(N_SHIFT)]
        back = [[(b, a) for a, b in pairs] for pairs in forth]
        split_pairs = [(i, split_partner(i)) for i in range(n_dev)]
        twin_pairs = [(i, twin_partner(i)) for i in range(n_dev)]

        order = []
        source = []
        for s in range(N_SHIFT):
            dx, dc, d = (s >> 2) & 1, (s >> 1) & 1, s & 1
            order.append(4 * (x ^ dx) + 2 * (c ^ dc) + (jnp.where((c ^ dc) == 0, y, z) ^ d))
            sx, sc = x ^ dx, c ^ dc
            sz = jnp.where(c == 0, z, z ^ d)
            sy = jnp.where(c == 0, y ^ d, y)
            source.append((sx * 2 + sc) * etp_size + sz * 2 + sy)
        order = jnp.stack(order).astype(I32)
        source = jnp.stack(source).astype(I32)

        ids_t = expert_ids.T
        slot_shape = jax.ShapeDtypeStruct((slots, d_model), BF16)
        slot_buf = pltpu.VMEM((n_experts, buf_rows, d_model), BF16)
        dma8 = pltpu.SemaphoreType.DMA((N_SHIFT,))
        spread_flops = 2 * tok_rows * n_experts * WIN * d_model

        count_table = pl.pallas_call(
            functools.partial(counts_kernel, n_dev, etp_size),
            in_specs=[vmem()], out_specs=vmem(),
            out_shape=jax.ShapeDtypeStruct((n_dev, 8, 128), I32),
            scratch_shapes=[pltpu.VMEM((8, 128), I32), pltpu.SemaphoreType.DMA((n_dev,)), pltpu.SemaphoreType.DMA((n_dev,))],
            compiler_params=pltpu.CompilerParams(collective_id=0, has_side_effects=True), name="counts",
        )(ids_t)[:, 0, :n_experts]

        x_slots = pl.pallas_call(
            x_slots_kernel,
            in_specs=[smem(), vmem(), vmem()],
            out_specs=[vmem()] + [hbm()] * N_SHIFT,
            out_shape=[jax.ShapeDtypeStruct((n_experts, 128), I32)] + [slot_shape] * N_SHIFT,
            scratch_shapes=[slot_buf, pltpu.SMEM((n_experts, 128), I32), dma8, pltpu.SemaphoreType.DMA],
            compiler_params=params(), cost_estimate=cost(spread_flops, 2 * rows * d_model), name="x_slots",
        )
        base, *x_send = x_slots(order + jnp.minimum(count_table[0, 0], 0), ids_t, hidden)
        x_recv = exchange(x_send, forth)

        running = jnp.cumsum(count_table, axis=0) - count_table
        total_count = jnp.sum(count_table, axis=0)
        block_idx = ep * etp_size + etp
        limit = jnp.clip(capacity - running, 0, None)
        kept_table = jnp.minimum(count_table, limit)
        my_limit, my_kept = limit[block_idx], kept_table[block_idx]
        my_expert = order[0]
        part = (kept_table[source, my_expert] + ALIGN - 1) // ALIGN * ALIGN
        offset = jnp.concatenate([jnp.zeros((1,), I32), jnp.cumsum(part)]).astype(I32)
        n_tiles = (offset[N_SHIFT:] + ROW_TILE - 1) // ROW_TILE

        wr_t = split3(w_router.T)
        wr3 = jnp.concatenate(wr_t + (jnp.zeros_like(wr_t[0]),), axis=0)
        wr6 = jnp.concatenate([wr_t[0], wr_t[1], wr_t[0], wr_t[2], wr_t[1], wr_t[0], jnp.zeros((128 - 6 * n_experts, d_model), BF16)], axis=0)
        c_slots = pl.pallas_call(
            c_slots_kernel,
            in_specs=[smem()] * 3 + [vmem()] * 4,
            out_specs=[vmem()] * 2 + [hbm()] * N_SHIFT,
            out_shape=[jax.ShapeDtypeStruct((tok_rows, 128), F32), jax.ShapeDtypeStruct((n_experts, 128), F32)] + [slot_shape] * N_SHIFT,
            scratch_shapes=[slot_buf, pltpu.VMEM((n_experts, tok_rows), F32), dma8],
            compiler_params=params(), cost_estimate=cost(spread_flops, 2 * rows * d_model), name="c_slots",
        )
        info, prob_sum, *c_send = c_slots(order, base, my_limit, ids_t, hidden, d_out, wr3)

        def take(w, j):
            return lax.dynamic_index_in_dim(w, j, 0, keepdims=False)

        weights = (w_gate, w_up, w_down)
        early = mine + jnp.minimum(count_table[0, 0], 0)
        later = mine + jnp.minimum(prob_sum[0, 0], 0.0).astype(I32)
        when = (later, later, early)
        q_own = [take(w, j) for w, j in zip(weights, when)]
        q_other = [take(w, 1 - j) for w, j in zip(weights, when)]
        q_split = permute(q_other[:2], split_pairs) + permute(q_other[2:], split_pairs)
        q_twin = permute(q_own[:2], twin_pairs) + permute(q_own[2:], twin_pairs)
        q_far = permute(q_split, twin_pairs)

        def after(value, earlier):
            return lax.optimization_barrier((value, earlier))[0]

        c_recv = exchange(c_send, forth)

        def pack(parts):
            return pl.pallas_call(
                pack_kernel,
                in_specs=[smem()] * 2 + [hbm()] * N_SHIFT,
                out_specs=hbm(),
                out_shape=jax.ShapeDtypeStruct((rows, d_model), BF16),
                scratch_shapes=[pltpu.VMEM((rows + ROW_TILE, d_model), BF16), pltpu.SemaphoreType.DMA((N_SHIFT, 6)), pltpu.SemaphoreType.DMA],
                compiler_params=params(), cost_estimate=cost(10**9, 4 * rows * d_model),
            )(part, offset, *parts)

        def row_spec(w):
            return pl.BlockSpec((ROW_TILE, w), lambda i, n, o: (jnp.clip(n[0] - 1, 0, i), 0))

        def full_spec(shape):
            return pl.BlockSpec(shape, lambda i, n, o: (0, 0), pipeline_mode=pl.Buffered(1))

        grid = (rows // ROW_TILE,)
        up_shape, down_shape = (d_model, width), (width, d_model)
        row_f32 = jax.ShapeDtypeStruct((rows, d_model), F32)
        act_shape = jax.ShapeDtypeStruct((rows, width), F32)
        row_buf = pltpu.VMEM((rows + slots, d_model), BF16)
        mm = 2 * rows * d_model * width

        def forward(quarter, y_acc, first, last):
            n_in = 4 + (not first)
            out = pl.pallas_call(
                functools.partial(forward_kernel, first=first, last=last),
                grid_spec=pltpu.PrefetchScalarGridSpec(
                    num_scalar_prefetch=2, grid=grid,
                    in_specs=[row_spec(d_model), full_spec(up_shape), full_spec(up_shape), full_spec(down_shape)] + [row_spec(d_model)] * (not first),
                    out_specs=[row_spec(width)] * 2 + ([hbm()] * N_SHIFT if last else [row_spec(d_model)]),
                    scratch_shapes=[row_buf, dma8] if last else []),
                out_shape=[act_shape] * 2 + ([slot_shape] * N_SHIFT if last else [row_f32]),
                input_output_aliases={} if first or last else {2 + n_in - 1: 2},
                compiler_params=params("arbitrary"), cost_estimate=cost(3 * mm, 20 * rows * d_model), name="forward",
            )(n_tiles, offset, x_rows, *quarter, *([] if first else [y_acc]))
            return out[0], out[1], (out[2:] if last else out[2])

        grad_shapes = [jax.ShapeDtypeStruct(up_shape, F32)] * 2 + [jax.ShapeDtypeStruct(down_shape, F32)]
        grad_specs = [full_spec(up_shape), full_spec(up_shape), full_spec(down_shape)]

        def backward(quarter, acts, dx_acc):
            first = dx_acc is None
            out = pl.pallas_call(
                functools.partial(backward_kernel, first=first),
                grid_spec=pltpu.PrefetchScalarGridSpec(
                    num_scalar_prefetch=2, grid=grid,
                    in_specs=[row_spec(d_model)] * 2 + [row_spec(width)] * 2 + grad_specs + [row_spec(d_model)] * (not first),
                    out_specs=grad_specs + [row_spec(d_model)]),
                out_shape=grad_shapes + [row_f32],
                input_output_aliases={} if first else {9: 3},
                compiler_params=params("arbitrary"), cost_estimate=cost(6 * mm, 20 * rows * d_model), name="backward",
            )(n_tiles, offset, x_rows, c_rows, *acts, *quarter, *([] if first else [dx_acc]))
            return out[:3], out[3]

        def backward_rows(quarter, acts, dx_acc):
            out = pl.pallas_call(
                backward_rows_kernel,
                grid_spec=pltpu.PrefetchScalarGridSpec(
                    num_scalar_prefetch=2, grid=grid,
                    in_specs=[row_spec(d_model)] + [row_spec(width)] * 2 + grad_specs + [row_spec(d_model)],
                    out_specs=[row_spec(width)] * 3 + [hbm()] * N_SHIFT,
                    scratch_shapes=[row_buf, dma8]),
                out_shape=[jax.ShapeDtypeStruct((rows, width), BF16)] * 3 + [slot_shape] * N_SHIFT,
                compiler_params=params("arbitrary"), cost_estimate=cost(3 * mm, 20 * rows * d_model), name="backward_rows",
            )(n_tiles, offset, c_rows, *acts, *quarter, dx_acc)
            return out[:3], out[3:]

        def weight_grads(grads):
            return pl.pallas_call(
                weight_grads_kernel,
                grid_spec=pltpu.PrefetchScalarGridSpec(
                    num_scalar_prefetch=2, grid=grid,
                    in_specs=[row_spec(d_model)] * 2 + [row_spec(width)] * 3,
                    out_specs=grad_specs),
                out_shape=grad_shapes,
                compiler_params=params("arbitrary"), cost_estimate=cost(3 * mm, 20 * rows * d_model), name="weight_grads",
            )(n_tiles, offset, x_rows, c_rows, *grads)

        x_rows = pack(x_recv)
        a0, b0, acc = forward(q_own, None, True, False)
        a1, b1, acc = forward(q_twin, acc, False, False)
        a2, b2, acc = forward(q_split, acc, False, False)
        a3, b3, y_send = forward(q_far, acc, False, True)
        y_recv = exchange(y_send, back)

        c_rows = pack([after(c_recv[0], y_send[0])] + c_recv[1:])
        g_far, acc = backward(q_far, (a3, b3), None)
        g_far = permute(g_far, twin_pairs)
        g_twin, acc = backward(q_twin, (a1, b1), acc)
        g_twin = permute(g_twin, twin_pairs)
        g_split, acc = backward(q_split, (a2, b2), acc)
        g_split = permute([a + b for a, b in zip(g_split, g_far)], split_pairs)
        grads, dx_send = backward_rows(q_own, (a0, b0), acc)
        dx_recv = exchange(dx_send, back)

        route_frac = total_count.astype(F32) / (2 * n_tokens)
        aux_weight = (AUX_COEF * n_experts / n_tokens) * route_frac
        weight_row = jnp.concatenate([jnp.tile(aux_weight, 6), jnp.zeros((128 - 6 * n_experts,), F32)])[None, :]

        def tok_block(w):
            return pl.BlockSpec((TOK_TILE, w), lambda t: (t, 0))

        def whole(shape):
            return pl.BlockSpec(shape, lambda t: (0, 0))

        combine_scratch = [slot_buf, pltpu.VMEM((n_experts * WIN, d_model), BF16), dma8]
        y_combine = pl.pallas_call(
            y_combine_kernel, grid=(tok_rows // TOK_TILE,),
            in_specs=[smem()] * 3 + [hbm()] * N_SHIFT + [tok_block(128), tok_block(d_model), tok_block(d_model), whole((1, 128))],
            out_specs=[tok_block(d_model), tok_block(128), whole((128, d_model))],
            out_shape=[jax.ShapeDtypeStruct((tok_rows, d_model), BF16), jax.ShapeDtypeStruct((tok_rows, 128), BF16), jax.ShapeDtypeStruct((128, d_model), F32)],
            scratch_shapes=combine_scratch,
            compiler_params=params("arbitrary"), cost_estimate=cost(2 * spread_flops, 4 * rows * d_model), name="y_combine",
        )
        output, dz, dwr = y_combine(order, base, my_kept, *y_recv, after(info, dx_send[0]), hidden, d_out, weight_row)
        dwr_t = dwr[0:n_experts] + dwr[2 * n_experts:3 * n_experts] + dwr[5 * n_experts:6 * n_experts]
        shared = jnp.concatenate([dwr_t, jnp.pad(prob_sum, ((0, 0), (0, d_model - 128)))], axis=0)

        def flip(value, bits):
            return lax.ppermute(value, dev_axes, [(i, i ^ bits) for i in range(n_dev)])

        shared = shared + flip(shared, 1)
        across_x = flip(shared, 2)

        def finish(own, got, other):
            r, w = own.shape
            tile = r // 4
            own_spec = pl.BlockSpec((tile, w), lambda e, i, j: (jnp.where(e == 0, i, 3), 0))
            other_spec = pl.BlockSpec((tile, w), lambda e, i, j: (jnp.where(e == 0, 0, i), 0))
            return pl.pallas_call(
                finish_kernel,
                grid_spec=pltpu.PrefetchScalarGridSpec(
                    num_scalar_prefetch=1, grid=(2, 4),
                    in_specs=[own_spec, own_spec, other_spec], out_specs=pl.BlockSpec((1, tile, w), lambda e, i, j: (e ^ j[0], i, 0))),
                out_shape=jax.ShapeDtypeStruct((2, r, w), F32),
                compiler_params=params("arbitrary", "arbitrary"), cost_estimate=cost(10**9, 24 * r * w), name="finish",
            )(mine[None].astype(I32), own, got, other)

        g_own = weight_grads([after(grads[0], dz)] + list(grads[1:]))
        d_gate, d_up, d_down = [finish(own, got, other) for own, got, other in zip(g_own, g_twin, g_split)]
        shared = shared + after(across_x, (d_gate, d_up, d_down))
        across = [flip(shared, bits) for bits in (4, 8, 12)]

        d_hidden = pl.pallas_call(
            dx_combine_kernel, grid=(tok_rows // TOK_TILE,),
            in_specs=[smem()] * 3 + [hbm()] * N_SHIFT + [tok_block(128), tok_block(128), tok_block(d_model), whole((128, d_model))],
            out_specs=tok_block(d_model),
            out_shape=jax.ShapeDtypeStruct((tok_rows, d_model), BF16),
            scratch_shapes=combine_scratch,
            compiler_params=params("arbitrary"), cost_estimate=cost(spread_flops, 4 * rows * d_model), name="dx_combine",
        )(order, base, my_kept, *dx_recv, after(info, (d_gate, d_up, d_down)), dz, d_out, wr6)

        across = [after(v, d_hidden) for v in across]
        shared = (shared + across[0]) + (across[1] + across[2])
        d_router = shared[:n_experts].T
        prob_total = shared[n_experts:, 0]
        aux_loss = AUX_COEF * n_experts * jnp.sum(route_frac * (prob_total / n_tokens))
        return output, d_hidden, d_router, aux_loss, d_gate, d_up, d_down

    return jax.shard_map(layer, mesh=mesh, in_specs=(tok_spec, P(), tok_spec, tok_spec, gate_spec, gate_spec, down_spec), out_specs=(tok_spec, tok_spec, P(), P(), gate_spec, gate_spec, down_spec), check_vma=False)
```

profile of v0, /device:TPU:0, one launch (start us, length us, event | category | flops | bytes accessed | tf_op | source)
XLA Modules:
  0.0 1091.3 jit_solution(7512252246089432813)
XLA Ops:
  0.6 9.4 counts.1
  12.2 3.2 dynamic-slice_bitcast_fusion
  17.5 19.8 %x_slots.1 = (s32[8,128]{1,0:T(8,128)}, bf16[896,768]{1,0:T(8,128)(2,1)}, bf16[896,768]{1,0:T(8,128)(2,1)}, bf16[896,768]{1,0:T(8,128)(2,1)}, bf16[896,768]{1,0:...) custom-call(s32[8]{0:T(128)} %broadcast_add_fusion.order_ref, ...), custom_call_target="tpu_custom_call" | custom-call | flops 6845104128 | bytes 11010048 | tf_op jit(solution)/shard_map/x_slots/pallas_call | solution.py:516
  44.8 26.7 %c_slots.1 = (f32[2048,128]{1,0:T(8,128)}, f32[8,128]{1,0:T(8,128)}, bf16[896,768]{1,0:T(8,128)(2,1)}, bf16[896,768]{1,0:T(8,128)(2,1)}, bf16[896,768]{1,0:T(8,1...) custom-call(s32[8]{0:T(128)} %copy-done.15, ...), custom_call_target="tpu_custom_call" | custom-call | flops 6845104128 | bytes 11010048 | tf_op jit(solution)/shard_map/c_slots/pallas_call | solution.py:541
  80.7 4.0 dynamic-slice_bitcast_fusion.1
  88.7 17.8 %collective-permute-done.4.refs_5_ = bf16[896,768]{1,0:T(8,128)(2,1)} collective-permute-done((bf16[896,768]{1,0:T(8,128)(2,1)}, bf16[896,768]{1,0:T(8,128)(2,1)}, u32[]{:S(2)}, u32[]{:S(2)}) %collective-permute-start.4) | collective-permute-done | bytes 1376288 | tf_op jit(solution)/shard_map/ppermute | solution.py:474
  108.0 26.1 %collective-permute-done.5.refs_6_ = bf16[896,768]{1,0:T(8,128)(2,1)} collective-permute-done((bf16[896,768]{1,0:T(8,128)(2,1)}, bf16[896,768]{1,0:T(8,128)(2,1)}, u32[]{:S(2)}, u32[]{:S(2)}) %collective-permute-start.5) | collective-permute-done | bytes 1376288 | tf_op jit(solution)/shard_map/ppermute | solution.py:474
  134.7 28.2 %collective-permute-done.6.refs_7_ = bf16[896,768]{1,0:T(8,128)(2,1)} collective-permute-done((bf16[896,768]{1,0:T(8,128)(2,1)}, bf16[896,768]{1,0:T(8,128)(2,1)}, u32[]{:S(2)}, u32[]{:S(2)}) %collective-permute-start.6) | collective-permute-done | bytes 1376288 | tf_op jit(solution)/shard_map/ppermute | solution.py:474
  164.3 7.8 shard_map.126.x_ref
  173.3 28.6 %forward.4 = (f32[7168,1024]{1,0:T(8,128)}, f32[7168,1024]{1,0:T(8,128)}, f32[7168,768]{1,0:T(8,128)}) custom-call(s32[1]{0:T(128)S(6)} %select_n.94.n_ref, s32[9]{0:T(128)} %pad_add_fusion.offset_s, bf16[7168,768]{1,0:T(8,128)(2,1)} %shard_map.126.x_ref, bf16[768,1024]{1,0:T(8,128)(2,1)} %get-tuple-element.167.w1_ref, ...), custom_call_target="tpu_custom_call" | custom-call | flops 33822867456 | bytes 110100480 | tf_op jit(solution)/shard_map/forward/pallas_call | solution.py:586
  201.9 3.3 collective-permute-start.23
  208.6 31.4 %forward.5 = (f32[7168,1024]{1,0:T(8,128)}, f32[7168,1024]{1,0:T(8,128)}, f32[7168,768]{1,0:T(8,128)}) custom-call(s32[1]{0:T(128)S(6)} %select_n.94.n_ref, s32[9]{0:T(128)} %pad_add_fusion.offset_s, bf16[7168,768]{1,0:T(8,128)(2,1)} %shard_map.126.x_ref, bf16[768,1024]{1,0:T(8,128)(2,1)} %collective-permute-done.13.w1_ref, ...), custom_call_target="tpu_custom_call", output_to_operand_aliasing={{2}: (6, {})} | custom-call | flops 33822867456 | bytes 110100480 | tf_op jit(solution)/shard_map/forward/pallas_call | solution.py:586
  239.9 31.6 %forward.6 = (f32[7168,1024]{1,0:T(8,128)}, f32[7168,1024]{1,0:T(8,128)}, f32[7168,768]{1,0:T(8,128)}) custom-call(s32[1]{0:T(128)S(6)} %select_n.94.n_ref, s32[9]{0:T(128)} %pad_add_fusion.offset_s, bf16[7168,768]{1,0:T(8,128)(2,1)} %shard_map.126.x_ref, bf16[768,1024]{1,0:T(8,128)(2,1)} %collective-permute-done.7.w1_ref, ...), custom_call_target="tpu_custom_call", output_to_operand_aliasing={{2}: (6, {})} | custom-call | flops 33822867456 | bytes 110100480 | tf_op jit(solution)/shard_map/forward/pallas_call | solution.py:586
  271.6 6.4 collective-permute-start.25
  278.0 17.0 %collective-permute-start.27 = (bf16[896,768]{1,0:T(8,128)(2,1)}, bf16[896,768]{1,0:T(8,128)(2,1)}, u32[]{:S(2)}, u32[]{:S(2)}) collective-permute-start(bf16[896,768]{1,0:T(8,128)(2,1)} %get-tuple-element.110), channel_id=1, source_target_pairs={{0,6},{1,11},{2,4},{3,9},{4,2},{5,15},{6,0},{7,13},{8,14},{9,3},{1... | collective-permute-start | bytes 4128776 | tf_op jit(solution)/shard_map/ppermute | solution.py:474
  297.9 34.1 %forward.7 = (f32[7168,1024]{1,0:T(8,128)}, f32[7168,1024]{1,0:T(8,128)}, bf16[896,768]{1,0:T(8,128)(2,1)}, bf16[896,768]{1,0:T(8,128)(2,1)}, bf16[896,768]{1,0:...) custom-call(s32[1]{0:T(128)S(6)} %select_n.94.n_ref, ...), custom_call_target="tpu_custom_call" | custom-call | flops 33822867456 | bytes 110100480 | tf_op jit(solution)/shard_map/forward/pallas_call | solution.py:586
  331.9 4.4 collective-permute-start.16
  336.5 19.2 %collective-permute-done.27.refs_5_ = bf16[896,768]{1,0:T(8,128)(2,1)} collective-permute-done((bf16[896,768]{1,0:T(8,128)(2,1)}, bf16[896,768]{1,0:T(8,128)(2,1)}, u32[]{:S(2)}, u32[]{:S(2)}) %collective-permute-start.27) | collective-permute-done | bytes 1376288 | tf_op jit(solution)/shard_map/ppermute | solution.py:474
  355.7 27.3 %collective-permute-done.28.refs_6_ = bf16[896,768]{1,0:T(8,128)(2,1)} collective-permute-done((bf16[896,768]{1,0:T(8,128)(2,1)}, bf16[896,768]{1,0:T(8,128)(2,1)}, u32[]{:S(2)}, u32[]{:S(2)}) %collective-permute-start.28) | collective-permute-done | bytes 1376288 | tf_op jit(solution)/shard_map/ppermute | solution.py:474
  383.0 3.4 collective-permute-start.19
  386.5 17.7 %collective-permute-done.29.refs_7_ = bf16[896,768]{1,0:T(8,128)(2,1)} collective-permute-done((bf16[896,768]{1,0:T(8,128)(2,1)}, bf16[896,768]{1,0:T(8,128)(2,1)}, u32[]{:S(2)}, u32[]{:S(2)}) %collective-permute-start.29) | collective-permute-done | bytes 1376288 | tf_op jit(solution)/shard_map/ppermute | solution.py:474
  404.2 10.1 collective-permute-start.20
  414.2 8.0 shard_map.127.c_ref
  422.2 53.6 %backward.3 = (f32[768,1024]{1,0:T(8,128)}, f32[768,1024]{1,0:T(8,128)}, f32[1024,768]{1,0:T(8,128)}, f32[7168,768]{1,0:T(8,128)}) custom-call(s32[1]{0:T(128)S(6)} %select_n.94.n_ref, s32[9]{0:T(128)} %pad_add_fusion.offset_s, bf16[7168,768]{1,0:T(8,128)(2,1)} %shard_map.126.x_ref, bf16[7168,768]{1,0:T(8,128)(2,1)} %shard_map.127.c_ref, ...), custom_call_target="tpu_custom_call" | custom-call | flops 67645734912 | bytes 110100480 | tf_op jit(solution)/shard_map/backward/pallas_call | solution.py:604
  475.8 55.0 %backward.4 = (f32[768,1024]{1,0:T(8,128)}, f32[768,1024]{1,0:T(8,128)}, f32[1024,768]{1,0:T(8,128)}, f32[7168,768]{1,0:T(8,128)}) custom-call(s32[1]{0:T(128)S(6)} %select_n.94.n_ref, s32[9]{0:T(128)} %pad_add_fusion.offset_s, bf16[7168,768]{1,0:T(8,128)(2,1)} %shard_map.126.x_ref, ...), custom_call_target="tpu_custom_call", output_to_operand_aliasing={{3}: (9, {})} | custom-call | flops 67645734912 | bytes 110100480 | tf_op jit(solution)/shard_map/backward/pallas_call | solution.py:604
  530.8 35.5 %collective-permute-start.21 = (bf16[896,768]{1,0:T(8,128)(2,1)}, bf16[896,768]{1,0:T(8,128)(2,1)}, u32[]{:S(2)}, u32[]{:S(2)}) collective-permute-start(bf16[896,768]{1,0:T(8,128)(2,1)} %get-tuple-element.101), channel_id=1, source_target_pairs={{3,0},{2,1},{1,2},{0,3},{7,4},{6,5},{5,6},{4,7},{11,8},{10,9},{9,1... | collective-permute-start | bytes 4128776 | tf_op jit(solution)/shard_map/ppermute | solution.py:474
  566.3 54.8 %backward.5 = (f32[768,1024]{1,0:T(8,128)}, f32[768,1024]{1,0:T(8,128)}, f32[1024,768]{1,0:T(8,128)}, f32[7168,768]{1,0:T(8,128)}) custom-call(s32[1]{0:T(128)S(6)} %select_n.94.n_ref, s32[9]{0:T(128)} %pad_add_fusion.offset_s, bf16[7168,768]{1,0:T(8,128)(2,1)} %shard_map.126.x_ref, ...), custom_call_target="tpu_custom_call", output_to_operand_aliasing={{3}: (9, {})} | custom-call | flops 67645734912 | bytes 110100480 | tf_op jit(solution)/shard_map/backward/pallas_call | solution.py:604
  625.3 42.9 %backward_rows.1 = (bf16[7168,1024]{1,0:T(8,128)(2,1)}, bf16[7168,1024]{1,0:T(8,128)(2,1)}, bf16[7168,1024]{1,0:T(8,128)(2,1)}, bf16[896,768]{1,0:T(8,128)(2,1)}...) custom-call(s32[1]{0:T(128)S(6)} %select_n.94.n_ref, ...), custom_call_target="tpu_custom_call" | custom-call | flops 33822867456 | bytes 110100480 | tf_op jit(solution)/shard_map/backward_rows/pallas_call | solution.py:617
  669.4 20.9 %collective-permute-start.30 = (bf16[896,768]{1,0:T(8,128)(2,1)}, bf16[896,768]{1,0:T(8,128)(2,1)S(1)}, u32[]{:S(2)}, u32[]{:S(2)}) collective-permute-start(bf16[896,768]{1,0:T(8,128)(2,1)} %get-tuple-element.127), channel_id=1, source_target_pairs={{4,0},{9,1},{6,2},{11,3},{0,4},{13,5},{2,6},{15,7},{12,8},{1,9},{1... | collective-permute-start | bytes 4128776 | tf_op jit(solution)/shard_map/ppermute | solution.py:474
  690.3 27.7 %y_combine.1 = (bf16[2048,768]{1,0:T(8,128)(2,1)}, bf16[2048,128]{1,0:T(8,128)(2,1)}, f32[128,768]{1,0:T(8,128)}) custom-call(s32[8]{0:T(128)} %copy-done.15, s32[8,128]{1,0:T(8,128)} %get-tuple-element.82.base_s, s32[8]{0:T(128)} %fusion.2.kept_s, bf16[896,768]{1,0:T(8,128)(2,1)} %get-tuple-element.95.refs_0_, bf16[896,768]{1,0:T(8,128)(2,1)} %copy-done.21, ...), custom_call_target="tpu_custom_call" | custom-call | flops 13690208256 | bytes 22020096 | tf_op jit(solution)/shard_map/y_combine/pallas_call | solution.py:676
  723.0 6.4 collective-permute-start.47
  729.3 3.9 add.263
  733.6 22.1 %collective-permute-done.41 = f32[768,1024]{1,0:T(8,128)} collective-permute-done((f32[768,1024]{1,0:T(8,128)}, f32[768,1024]{1,0:T(8,128)}, u32[]{:S(2)}, u32[]{:S(2)}) %collective-permute-start.41) | collective-permute-done | bytes 3145760 | tf_op jit(solution)/shard_map/ppermute | solution.py:469
  758.8 3.8 collective-permute-start.39
  762.6 50.7 %collective-permute-done.44 = f32[1024,768]{1,0:T(8,128)} collective-permute-done((f32[1024,768]{1,0:T(8,128)}, f32[1024,768]{1,0:T(8,128)}, u32[]{:S(2)}, u32[]{:S(2)}) %collective-permute-start.44) | collective-permute-done | bytes 3145760 | tf_op jit(solution)/shard_map/ppermute | solution.py:469
  813.3 5.8 collective-permute-start.42
  821.6 59.1 %collective-permute-done.40.part_ref = f32[768,1024]{1,0:T(8,128)} collective-permute-done((f32[768,1024]{1,0:T(8,128)S(1)}, f32[768,1024]{1,0:T(8,128)}, u32[]{:S(2)}, u32[]{:S(2)}) %collective-permute-start.40) | collective-permute-done | bytes 3145760 | tf_op jit(solution)/shard_map/ppermute | solution.py:469
  880.7 67.4 %collective-permute-done.43.part_ref = f32[1024,768]{1,0:T(8,128)} collective-permute-done((f32[1024,768]{1,0:T(8,128)S(1)}, f32[1024,768]{1,0:T(8,128)}, u32[]{:S(2)}, u32[]{:S(2)}) %collective-permute-start.43) | collective-permute-done | bytes 3145760 | tf_op jit(solution)/shard_map/ppermute | solution.py:469
  948.1 13.1 %collective-permute-start.34 = (bf16[896,768]{1,0:T(8,128)(2,1)}, bf16[896,768]{1,0:T(8,128)(2,1)}, u32[]{:S(2)}, u32[]{:S(2)}) collective-permute-start(bf16[896,768]{1,0:T(8,128)(2,1)} %get-tuple-element.131), channel_id=1, source_target_pairs={{6,0},{11,1},{4,2},{9,3},{2,4},{15,5},{0,6},{13,7},{14,8},{3,9},{1... | collective-permute-start | bytes 4128776 | tf_op jit(solution)/shard_map/ppermute | solution.py:474
  961.2 9.0 collective-permute-start.35
  970.5 29.6 %weight_grads.1 = (f32[768,1024]{1,0:T(8,128)}, f32[768,1024]{1,0:T(8,128)}, f32[1024,768]{1,0:T(8,128)}) custom-call(s32[1]{0:T(128)S(6)} %select_n.94.n_ref, s32[9]{0:T(128)} %pad_add_fusion.offset_s, bf16[7168,768]{1,0:T(8,128)(2,1)} %shard_map.126.x_ref, bf16[7168,768]{1,0:T(8,128)(2,1)} %shard_map.127.c_ref, ...), custom_call_target="tpu_custom_call" | custom-call | flops 33822867456 | bytes 110100480 | tf_op jit(solution)/shard_map/weight_grads/pallas_call | solution.py:630
  1000.1 8.9 finish.3
  1009.0 8.9 finish.4
  1017.9 8.9 finish.5
  1026.8 6.3 collective-permute-start.50
  1033.7 21.5 %collective-permute-done.35.refs_6_ = bf16[896,768]{1,0:T(8,128)(2,1)} collective-permute-done((bf16[896,768]{1,0:T(8,128)(2,1)}, bf16[896,768]{1,0:T(8,128)(2,1)}, u32[]{:S(2)}, u32[]{:S(2)}) %collective-permute-start.35) | collective-permute-done | bytes 1376288 | tf_op jit(solution)/shard_map/ppermute | solution.py:474
  1055.2 13.6 %collective-permute-done.36.refs_7_ = bf16[896,768]{1,0:T(8,128)(2,1)} collective-permute-done((bf16[896,768]{1,0:T(8,128)(2,1)S(1)}, bf16[896,768]{1,0:T(8,128)(2,1)}, u32[]{:S(2)}, u32[]{:S(2)}) %collective-permute-start.36) | collective-permute-done | bytes 1376288 | tf_op jit(solution)/shard_map/ppermute | solution.py:474
  1068.8 19.0 %dx_combine.1 = bf16[2048,768]{1,0:T(8,128)(2,1)} custom-call(s32[8]{0:T(128)} %copy-done.15, s32[8,128]{1,0:T(8,128)} %get-tuple-element.82.base_s, s32[8]{0:T(128)} %fusion.2.kept_s, bf16[896,768]{1,0:T(8,128)(2,1)} %get-tuple-element.124.refs_0_, bf16[896,768]{1,0:T(8,128)(2,1)} %copy-done.19, bf16[896,768]{1,0:T(8,128)(2,1)} %copy-done.20, ...), custom_call_target="tpu_custom_call" | custom-call | flops 6845104128 | bytes 22020096 | tf_op jit(solution)/shard_map/dx_combine/pallas_call | solution.py:705
  (165 shorter events, 52.2 us)
Async XLA Ops:
  15.4 156.7 %collective-permute-start.11 = (bf16[1024,768]{1,0:T(8,128)(2,1)}, bf16[1024,768]{1,0:T(8,128)(2,1)}, u32[]{:S(2)}, u32[]{:S(2)}) collective-permute-start(bf16[1024,768]{1,0:T(8,128)(2,1)} %get-tuple-element.164), channel_id=1, source_target_pairs={{0,4},{1,9},{2,6},{3,11},{4,0},{5,13},{6,2},{7,15},{8,12},{9,1},{1... | collective-permute-start | bytes 4718600 | tf_op jit(solution)/shard_map/ppermute | solution.py:469
  37.3 34.9 %collective-permute-start = (bf16[896,768]{1,0:T(8,128)(2,1)}, bf16[896,768]{1,0:T(8,128)(2,1)}, u32[]{:S(2)}, u32[]{:S(2)}) collective-permute-start(bf16[896,768]{1,0:T(8,128)(2,1)} %get-tuple-element.84), channel_id=1, source_target_pairs={{0,4},{1,9},{2,6},{3,11},{4,0},{5,13},{6,2},{7,15},{8,12},{9,1},{1... | collective-permute-start | bytes 4128776 | tf_op jit(solution)/shard_map/ppermute | solution.py:474
  38.0 35.8 %collective-permute-start.1 = (bf16[896,768]{1,0:T(8,128)(2,1)}, bf16[896,768]{1,0:T(8,128)(2,1)}, u32[]{:S(2)}, u32[]{:S(2)}) collective-permute-start(bf16[896,768]{1,0:T(8,128)(2,1)} %get-tuple-element.85), channel_id=1, source_target_pairs={{0,1},{1,0},{2,3},{3,2},{4,5},{5,4},{6,7},{7,6},{8,9},{9,8},{10,11... | collective-permute-start | bytes 4128776 | tf_op jit(solution)/shard_map/ppermute | solution.py:474
  38.0 36.2 %collective-permute-start.2 = (bf16[896,768]{1,0:T(8,128)(2,1)}, bf16[896,768]{1,0:T(8,128)(2,1)}, u32[]{:S(2)}, u32[]{:S(2)}) collective-permute-start(bf16[896,768]{1,0:T(8,128)(2,1)} %get-tuple-element.86), channel_id=1, source_target_pairs={{0,9},{1,4},{2,11},{3,6},{4,13},{5,0},{6,15},{7,2},{8,1},{9,12},{1... | collective-permute-start | bytes 4128776 | tf_op jit(solution)/shard_map/ppermute | solution.py:474
  39.5 47.8 %collective-permute-start.3 = (bf16[896,768]{1,0:T(8,128)(2,1)}, bf16[896,768]{1,0:T(8,128)(2,1)}, u32[]{:S(2)}, u32[]{:S(2)}) collective-permute-start(bf16[896,768]{1,0:T(8,128)(2,1)} %get-tuple-element.87), channel_id=1, source_target_pairs={{0,2},{1,3},{2,0},{3,1},{4,6},{5,7},{6,4},{7,5},{8,10},{9,11},{10,... | collective-permute-start | bytes 4128776 | tf_op jit(solution)/shard_map/ppermute | solution.py:474
  73.8 60.4 %collective-permute-start.5 = (bf16[896,768]{1,0:T(8,128)(2,1)}, bf16[896,768]{1,0:T(8,128)(2,1)}, u32[]{:S(2)}, u32[]{:S(2)}) collective-permute-start(bf16[896,768]{1,0:T(8,128)(2,1)} %get-tuple-element.89), channel_id=1, source_target_pairs={{0,3},{1,2},{2,1},{3,0},{4,7},{5,6},{6,5},{7,4},{8,11},{9,10},{10,... | collective-permute-start | bytes 4128776 | tf_op jit(solution)/shard_map/ppermute | solution.py:474
  74.2 88.8 %collective-permute-start.6 = (bf16[896,768]{1,0:T(8,128)(2,1)}, bf16[896,768]{1,0:T(8,128)(2,1)}, u32[]{:S(2)}, u32[]{:S(2)}) collective-permute-start(bf16[896,768]{1,0:T(8,128)(2,1)} %get-tuple-element.90), channel_id=1, source_target_pairs={{0,11},{1,6},{2,9},{3,4},{4,15},{5,2},{6,13},{7,0},{8,3},{9,14},{1... | collective-permute-start | bytes 4128776 | tf_op jit(solution)/shard_map/ppermute | solution.py:474
  87.2 114.6 %collective-permute-start.15 = (bf16[1024,768]{1,0:T(8,128)(2,1)S(1)}, bf16[1024,768]{1,0:T(8,128)(2,1)}, u32[]{:S(2)}, u32[]{:S(2)}) collective-permute-start(bf16[1024,768]{1,0:T(8,128)(2,1)S(1)} %get-tuple-element.163.w2_ref), channel_id=1, source_target_pairs={{0,8},{1,5},{2,10},{3,7},{4,12},{5,1},{6,14},{7,3},{8,0},{9,13},{1... | collective-permute-start | bytes 4718600 | tf_op jit(solution)/shard_map/ppermute | solution.py:469
  106.5 98.6 %collective-permute-start.9 = (bf16[768,1024]{1,0:T(8,128)(2,1)}, bf16[768,1024]{1,0:T(8,128)(2,1)}, u32[]{:S(2)}, u32[]{:S(2)}) collective-permute-start(bf16[768,1024]{1,0:T(8,128)(2,1)} %get-tuple-element.166), channel_id=1, source_target_pairs={{0,4},{1,9},{2,6},{3,11},{4,0},{5,13},{6,2},{7,15},{8,12},{9,1},{1... | collective-permute-start | bytes 4718600 | tf_op jit(solution)/shard_map/ppermute | solution.py:469
  134.2 71.2 %collective-permute-start.14 = (bf16[768,1024]{1,0:T(8,128)(2,1)}, bf16[768,1024]{1,0:T(8,128)(2,1)}, u32[]{:S(2)}, u32[]{:S(2)}) collective-permute-start(bf16[768,1024]{1,0:T(8,128)(2,1)} %get-tuple-element.165.w3_ref), channel_id=1, source_target_pairs={{0,8},{1,5},{2,10},{3,7},{4,12},{5,1},{6,14},{7,3},{8,0},{9,13},{1... | collective-permute-start | bytes 4718600 | tf_op jit(solution)/shard_map/ppermute | solution.py:469
  163.0 43.6 %collective-permute-start.7 = (bf16[768,1024]{1,0:T(8,128)(2,1)}, bf16[768,1024]{1,0:T(8,128)(2,1)}, u32[]{:S(2)}, u32[]{:S(2)}) collective-permute-start(bf16[768,1024]{1,0:T(8,128)(2,1)} %get-tuple-element.168), channel_id=1, source_target_pairs={{0,4},{1,9},{2,6},{3,11},{4,0},{5,13},{6,2},{7,15},{8,12},{9,1},{1... | collective-permute-start | bytes 4718600 | tf_op jit(solution)/shard_map/ppermute | solution.py:469
  172.1 35.3 %collective-permute-start.13 = (bf16[768,1024]{1,0:T(8,128)(2,1)}, bf16[768,1024]{1,0:T(8,128)(2,1)}, u32[]{:S(2)}, u32[]{:S(2)}) collective-permute-start(bf16[768,1024]{1,0:T(8,128)(2,1)} %get-tuple-element.167.w1_ref), channel_id=1, source_target_pairs={{0,8},{1,5},{2,10},{3,7},{4,12},{5,1},{6,14},{7,3},{8,0},{9,13},{1... | collective-permute-start | bytes 4718600 | tf_op jit(solution)/shard_map/ppermute | solution.py:469
  201.9 69.7 %collective-permute-start.23 = (bf16[896,768]{1,0:T(8,128)(2,1)}, bf16[896,768]{1,0:T(8,128)(2,1)S(1)}, u32[]{:S(2)}, u32[]{:S(2)}) collective-permute-start(bf16[896,768]{1,0:T(8,128)(2,1)} %get-tuple-element.106), channel_id=1, source_target_pairs={{0,4},{1,9},{2,6},{3,11},{4,0},{5,13},{6,2},{7,15},{8,12},{9,1},{1... | collective-permute-start | bytes 4128776 | tf_op jit(solution)/shard_map/ppermute | solution.py:474
  205.1 72.8 %collective-permute-start.24 = (bf16[896,768]{1,0:T(8,128)(2,1)}, bf16[896,768]{1,0:T(8,128)(2,1)}, u32[]{:S(2)}, u32[]{:S(2)}) collective-permute-start(bf16[896,768]{1,0:T(8,128)(2,1)} %get-tuple-element.107), channel_id=1, source_target_pairs={{0,1},{1,0},{2,3},{3,2},{4,5},{5,4},{6,7},{7,6},{8,9},{9,8},{10,11... | collective-permute-start | bytes 4128776 | tf_op jit(solution)/shard_map/ppermute | solution.py:474
  205.4 72.6 %collective-permute-start.12 = (bf16[1024,768]{1,0:T(8,128)(2,1)}, bf16[1024,768]{1,0:T(8,128)(2,1)}, u32[]{:S(2)}, u32[]{:S(2)}) collective-permute-start(bf16[1024,768]{1,0:T(8,128)(2,1)} %collective-permute-done.11.w2_ref), channel_id=1, source_target_pairs={{0,8},{1,5},{2,10},{3,7},{4,12},{5,1},{6,14},{7,3},{8,0},{9,13},{1... | collective-permute-start | bytes 4718600 | tf_op jit(solution)/shard_map/ppermute | solution.py:469
  206.5 88.4 %collective-permute-start.10 = (bf16[768,1024]{1,0:T(8,128)(2,1)}, bf16[768,1024]{1,0:T(8,128)(2,1)}, u32[]{:S(2)}, u32[]{:S(2)}) collective-permute-start(bf16[768,1024]{1,0:T(8,128)(2,1)} %collective-permute-done.9.w3_ref), channel_id=1, source_target_pairs={{0,8},{1,5},{2,10},{3,7},{4,12},{5,1},{6,14},{7,3},{8,0},{9,13},{1... | collective-permute-start | bytes 4718600 | tf_op jit(solution)/shard_map/ppermute | solution.py:469
  207.4 87.8 %collective-permute-start.8 = (bf16[768,1024]{1,0:T(8,128)(2,1)}, bf16[768,1024]{1,0:T(8,128)(2,1)}, u32[]{:S(2)}, u32[]{:S(2)}) collective-permute-start(bf16[768,1024]{1,0:T(8,128)(2,1)} %collective-permute-done.7.w1_ref), channel_id=1, source_target_pairs={{0,8},{1,5},{2,10},{3,7},{4,12},{5,1},{6,14},{7,3},{8,0},{9,13},{1... | collective-permute-start | bytes 4718600 | tf_op jit(solution)/shard_map/ppermute | solution.py:469
  271.6 60.4 %collective-permute-start.25 = (bf16[896,768]{1,0:T(8,128)(2,1)}, bf16[896,768]{1,0:T(8,128)(2,1)}, u32[]{:S(2)}, u32[]{:S(2)}) collective-permute-start(bf16[896,768]{1,0:T(8,128)(2,1)} %get-tuple-element.108), channel_id=1, source_target_pairs={{0,9},{1,4},{2,11},{3,6},{4,13},{5,0},{6,15},{7,2},{8,1},{9,12},{1... | collective-permute-start | bytes 4128776 | tf_op jit(solution)/shard_map/ppermute | solution.py:474
  278.0 58.4 %collective-permute-start.26 = (bf16[896,768]{1,0:T(8,128)(2,1)}, bf16[896,768]{1,0:T(8,128)(2,1)}, u32[]{:S(2)}, u32[]{:S(2)}) collective-permute-start(bf16[896,768]{1,0:T(8,128)(2,1)} %get-tuple-element.109), channel_id=1, source_target_pairs={{0,2},{1,3},{2,0},{3,1},{4,6},{5,7},{6,4},{7,5},{8,10},{9,11},{10,... | collective-permute-start | bytes 4128776 | tf_op jit(solution)/shard_map/ppermute | solution.py:474
  278.0 77.7 %collective-permute-start.27 = (bf16[896,768]{1,0:T(8,128)(2,1)}, bf16[896,768]{1,0:T(8,128)(2,1)}, u32[]{:S(2)}, u32[]{:S(2)}) collective-permute-start(bf16[896,768]{1,0:T(8,128)(2,1)} %get-tuple-element.110), channel_id=1, source_target_pairs={{0,6},{1,11},{2,4},{3,9},{4,2},{5,15},{6,0},{7,13},{8,14},{9,3},{1... | collective-permute-start | bytes 4128776 | tf_op jit(solution)/shard_map/ppermute | solution.py:474
  294.9 88.1 %collective-permute-start.28 = (bf16[896,768]{1,0:T(8,128)(2,1)}, bf16[896,768]{1,0:T(8,128)(2,1)}, u32[]{:S(2)}, u32[]{:S(2)}) collective-permute-start(bf16[896,768]{1,0:T(8,128)(2,1)} %get-tuple-element.111), channel_id=1, source_target_pairs={{0,3},{1,2},{2,1},{3,0},{4,7},{5,6},{6,5},{7,4},{8,11},{9,10},{10,... | collective-permute-start | bytes 4128776 | tf_op jit(solution)/shard_map/ppermute | solution.py:474
  295.2 109.0 %collective-permute-start.29 = (bf16[896,768]{1,0:T(8,128)(2,1)}, bf16[896,768]{1,0:T(8,128)(2,1)}, u32[]{:S(2)}, u32[]{:S(2)}) collective-permute-start(bf16[896,768]{1,0:T(8,128)(2,1)} %get-tuple-element.112), channel_id=1, source_target_pairs={{0,11},{1,6},{2,9},{3,4},{4,15},{5,2},{6,13},{7,0},{8,3},{9,14},{1... | collective-permute-start | bytes 4128776 | tf_op jit(solution)/shard_map/ppermute | solution.py:474
  331.9 198.9 %collective-permute-start.16 = (bf16[896,768]{1,0:T(8,128)(2,1)}, bf16[896,768]{1,0:T(8,128)(2,1)S(1)}, u32[]{:S(2)}, u32[]{:S(2)}) collective-permute-start(bf16[896,768]{1,0:T(8,128)(2,1)} %get-tuple-element.96), channel_id=1, source_target_pairs={{4,0},{9,1},{6,2},{11,3},{0,4},{13,5},{2,6},{15,7},{12,8},{1,9},{1... | collective-permute-start | bytes 4128776 | tf_op jit(solution)/shard_map/ppermute | solution.py:474
  336.4 284.8 %collective-permute-start.17 = (bf16[896,768]{1,0:T(8,128)(2,1)}, bf16[896,768]{1,0:T(8,128)(2,1)}, u32[]{:S(2)}, u32[]{:S(2)}) collective-permute-start(bf16[896,768]{1,0:T(8,128)(2,1)} %get-tuple-element.97), channel_id=1, source_target_pairs={{1,0},{0,1},{3,2},{2,3},{5,4},{4,5},{7,6},{6,7},{9,8},{8,9},{11,10... | collective-permute-start | bytes 4128776 | tf_op jit(solution)/shard_map/ppermute | solution.py:474
  355.7 265.5 %collective-permute-start.18 = (bf16[896,768]{1,0:T(8,128)(2,1)}, bf16[896,768]{1,0:T(8,128)(2,1)}, u32[]{:S(2)}, u32[]{:S(2)}) collective-permute-start(bf16[896,768]{1,0:T(8,128)(2,1)} %get-tuple-element.98), channel_id=1, source_target_pairs={{9,0},{4,1},{11,2},{6,3},{13,4},{0,5},{15,6},{2,7},{1,8},{12,9},{3... | collective-permute-start | bytes 4128776 | tf_op jit(solution)/shard_map/ppermute | solution.py:474
  383.0 238.2 %collective-permute-start.19 = (bf16[896,768]{1,0:T(8,128)(2,1)}, bf16[896,768]{1,0:T(8,128)(2,1)}, u32[]{:S(2)}, u32[]{:S(2)}) collective-permute-start(bf16[896,768]{1,0:T(8,128)(2,1)} %get-tuple-element.99), channel_id=1, source_target_pairs={{2,0},{3,1},{0,2},{1,3},{6,4},{7,5},{4,6},{5,7},{10,8},{11,9},{8,1... | collective-permute-start | bytes 4128776 | tf_op jit(solution)/shard_map/ppermute | solution.py:474
  404.2 219.1 %collective-permute-start.20 = (bf16[896,768]{1,0:T(8,128)(2,1)}, bf16[896,768]{1,0:T(8,128)(2,1)}, u32[]{:S(2)}, u32[]{:S(2)}) collective-permute-start(bf16[896,768]{1,0:T(8,128)(2,1)} %get-tuple-element.100), channel_id=1, source_target_pairs={{6,0},{11,1},{4,2},{9,3},{2,4},{15,5},{0,6},{13,7},{14,8},{3,9},{1... | collective-permute-start | bytes 4128776 | tf_op jit(solution)/shard_map/ppermute | solution.py:474
  530.8 92.5 %collective-permute-start.21 = (bf16[896,768]{1,0:T(8,128)(2,1)}, bf16[896,768]{1,0:T(8,128)(2,1)}, u32[]{:S(2)}, u32[]{:S(2)}) collective-permute-start(bf16[896,768]{1,0:T(8,128)(2,1)} %get-tuple-element.101), channel_id=1, source_target_pairs={{3,0},{2,1},{1,2},{0,3},{7,4},{6,5},{5,6},{4,7},{11,8},{10,9},{9,1... | collective-permute-start | bytes 4128776 | tf_op jit(solution)/shard_map/ppermute | solution.py:474
  621.2 47.1 %collective-permute-start.22 = (bf16[896,768]{1,0:T(8,128)(2,1)}, bf16[896,768]{1,0:T(8,128)(2,1)S(1)}, u32[]{:S(2)}, u32[]{:S(2)}) collective-permute-start(bf16[896,768]{1,0:T(8,128)(2,1)} %get-tuple-element.102), channel_id=1, source_target_pairs={{11,0},{6,1},{9,2},{4,3},{15,4},{2,5},{13,6},{0,7},{3,8},{14,9},{1... | collective-permute-start | bytes 4128776 | tf_op jit(solution)/shard_map/ppermute | solution.py:474
  621.2 200.2 %collective-permute-start.37 = (f32[768,1024]{1,0:T(8,128)}, f32[768,1024]{1,0:T(8,128)}, u32[]{:S(2)}, u32[]{:S(2)}) collective-permute-start(f32[768,1024]{1,0:T(8,128)} %get-tuple-element.140), channel_id=1, source_target_pairs={{0,8},{1,5},{2,10},{3,7},{4,12},{5,1},{6,14},{7,3},{8,0},{9,13},{1... | collective-permute-start | bytes 9437192 | tf_op jit(solution)/shard_map/ppermute | solution.py:469
  621.3 101.7 %collective-permute-start.38 = (f32[768,1024]{1,0:T(8,128)}, f32[768,1024]{1,0:T(8,128)}, u32[]{:S(2)}, u32[]{:S(2)}) collective-permute-start(f32[768,1024]{1,0:T(8,128)} %get-tuple-element.142), channel_id=1, source_target_pairs={{0,8},{1,5},{2,10},{3,7},{4,12},{5,1},{6,14},{7,3},{8,0},{9,13},{1... | collective-permute-start | bytes 9437192 | tf_op jit(solution)/shard_map/ppermute | solution.py:469
  623.3 132.5 %collective-permute-start.41 = (f32[768,1024]{1,0:T(8,128)}, f32[768,1024]{1,0:T(8,128)}, u32[]{:S(2)}, u32[]{:S(2)}) collective-permute-start(f32[768,1024]{1,0:T(8,128)} %get-tuple-element.146), channel_id=1, source_target_pairs={{0,8},{1,5},{2,10},{3,7},{4,12},{5,1},{6,14},{7,3},{8,0},{9,13},{1... | collective-permute-start | bytes 9437192 | tf_op jit(solution)/shard_map/ppermute | solution.py:469
  623.4 189.9 %collective-permute-start.44 = (f32[1024,768]{1,0:T(8,128)}, f32[1024,768]{1,0:T(8,128)}, u32[]{:S(2)}, u32[]{:S(2)}) collective-permute-start(f32[1024,768]{1,0:T(8,128)} %get-tuple-element.150), channel_id=1, source_target_pairs={{0,8},{1,5},{2,10},{3,7},{4,12},{5,1},{6,14},{7,3},{8,0},{9,13},{1... | collective-permute-start | bytes 9437192 | tf_op jit(solution)/shard_map/ppermute | solution.py:469
  669.4 52.2 %collective-permute-start.30 = (bf16[896,768]{1,0:T(8,128)(2,1)}, bf16[896,768]{1,0:T(8,128)(2,1)S(1)}, u32[]{:S(2)}, u32[]{:S(2)}) collective-permute-start(bf16[896,768]{1,0:T(8,128)(2,1)} %get-tuple-element.127), channel_id=1, source_target_pairs={{4,0},{9,1},{6,2},{11,3},{0,4},{13,5},{2,6},{15,7},{12,8},{1,9},{1... | collective-permute-start | bytes 4128776 | tf_op jit(solution)/shard_map/ppermute | solution.py:474
  723.0 35.8 %collective-permute-start.47 = (f32[16,768]{1,0:T(8,128)S(1)}, f32[16,768]{1,0:T(8,128)S(1)}, u32[]{:S(2)}, u32[]{:S(2)}) collective-permute-start(f32[16,768]{1,0:T(8,128)S(1)} %fusion.11), channel_id=1, source_target_pairs={{0,2},{1,3},{2,0},{3,1},{4,6},{5,7},{6,4},{7,5},{8,10},{9,11},{10,... | collective-permute-start | bytes 147464 | tf_op jit(solution)/shard_map/ppermute | solution.py:681
  733.3 147.3 %collective-permute-start.40 = (f32[768,1024]{1,0:T(8,128)S(1)}, f32[768,1024]{1,0:T(8,128)}, u32[]{:S(2)}, u32[]{:S(2)}) collective-permute-start(f32[768,1024]{1,0:T(8,128)S(1)} %copy-done.17), channel_id=1, source_target_pairs={{0,8},{1,5},{2,10},{3,7},{4,12},{5,1},{6,14},{7,3},{8,0},{9,13},{1... | collective-permute-start | bytes 9437192 | tf_op jit(solution)/shard_map/ppermute | solution.py:469
  755.8 192.3 %collective-permute-start.43 = (f32[1024,768]{1,0:T(8,128)S(1)}, f32[1024,768]{1,0:T(8,128)}, u32[]{:S(2)}, u32[]{:S(2)}) collective-permute-start(f32[1024,768]{1,0:T(8,128)S(1)} %copy-done.16), channel_id=1, source_target_pairs={{0,8},{1,5},{2,10},{3,7},{4,12},{5,1},{6,14},{7,3},{8,0},{9,13},{1... | collective-permute-start | bytes 9437192 | tf_op jit(solution)/shard_map/ppermute | solution.py:469
  758.8 189.3 %collective-permute-start.39 = (f32[768,1024]{1,0:T(8,128)S(1)}, f32[768,1024]{1,0:T(8,128)}, u32[]{:S(2)}, u32[]{:S(2)}) collective-permute-start(f32[768,1024]{1,0:T(8,128)S(1)} %add.263), channel_id=1, source_target_pairs={{0,4},{1,9},{2,6},{3,11},{4,0},{5,13},{6,2},{7,15},{8,12},{9,1},{1... | collective-permute-start | bytes 9437192 | tf_op jit(solution)/shard_map/ppermute | solution.py:469
  813.3 148.0 %collective-permute-start.42 = (f32[768,1024]{1,0:T(8,128)S(1)}, f32[768,1024]{1,0:T(8,128)}, u32[]{:S(2)}, u32[]{:S(2)}) collective-permute-start(f32[768,1024]{1,0:T(8,128)S(1)} %add.264), channel_id=1, source_target_pairs={{0,4},{1,9},{2,6},{3,11},{4,0},{5,13},{6,2},{7,15},{8,12},{9,1},{1... | collective-permute-start | bytes 9437192 | tf_op jit(solution)/shard_map/ppermute | solution.py:469
  821.5 148.8 %collective-permute-start.45 = (f32[1024,768]{1,0:T(8,128)S(1)}, f32[1024,768]{1,0:T(8,128)}, u32[]{:S(2)}, u32[]{:S(2)}) collective-permute-start(f32[1024,768]{1,0:T(8,128)S(1)} %add.265), channel_id=1, source_target_pairs={{0,4},{1,9},{2,6},{3,11},{4,0},{5,13},{6,2},{7,15},{8,12},{9,1},{1... | collective-permute-start | bytes 9437192 | tf_op jit(solution)/shard_map/ppermute | solution.py:469
  880.7 146.1 %collective-permute-start.32 = (bf16[896,768]{1,0:T(8,128)(2,1)}, bf16[896,768]{1,0:T(8,128)(2,1)}, u32[]{:S(2)}, u32[]{:S(2)}) collective-permute-start(bf16[896,768]{1,0:T(8,128)(2,1)} %get-tuple-element.129), channel_id=1, source_target_pairs={{9,0},{4,1},{11,2},{6,3},{13,4},{0,5},{15,6},{2,7},{1,8},{12,9},{3... | collective-permute-start | bytes 4128776 | tf_op jit(solution)/shard_map/ppermute | solution.py:474
  948.1 85.0 %collective-permute-start.33 = (bf16[896,768]{1,0:T(8,128)(2,1)}, bf16[896,768]{1,0:T(8,128)(2,1)}, u32[]{:S(2)}, u32[]{:S(2)}) collective-permute-start(bf16[896,768]{1,0:T(8,128)(2,1)} %get-tuple-element.130), channel_id=1, source_target_pairs={{2,0},{3,1},{0,2},{1,3},{6,4},{7,5},{4,6},{5,7},{10,8},{11,9},{8,1... | collective-permute-start | bytes 4128776 | tf_op jit(solution)/shard_map/ppermute | solution.py:474
  948.1 85.0 %collective-permute-start.34 = (bf16[896,768]{1,0:T(8,128)(2,1)}, bf16[896,768]{1,0:T(8,128)(2,1)}, u32[]{:S(2)}, u32[]{:S(2)}) collective-permute-start(bf16[896,768]{1,0:T(8,128)(2,1)} %get-tuple-element.131), channel_id=1, source_target_pairs={{6,0},{11,1},{4,2},{9,3},{2,4},{15,5},{0,6},{13,7},{14,8},{3,9},{1... | collective-permute-start | bytes 4128776 | tf_op jit(solution)/shard_map/ppermute | solution.py:474
  961.2 94.0 %collective-permute-start.35 = (bf16[896,768]{1,0:T(8,128)(2,1)}, bf16[896,768]{1,0:T(8,128)(2,1)}, u32[]{:S(2)}, u32[]{:S(2)}) collective-permute-start(bf16[896,768]{1,0:T(8,128)(2,1)} %get-tuple-element.132), channel_id=1, source_target_pairs={{3,0},{2,1},{1,2},{0,3},{7,4},{6,5},{5,6},{4,7},{11,8},{10,9},{9,1... | collective-permute-start | bytes 4128776 | tf_op jit(solution)/shard_map/ppermute | solution.py:474
  970.3 98.5 %collective-permute-start.36 = (bf16[896,768]{1,0:T(8,128)(2,1)S(1)}, bf16[896,768]{1,0:T(8,128)(2,1)}, u32[]{:S(2)}, u32[]{:S(2)}) collective-permute-start(bf16[896,768]{1,0:T(8,128)(2,1)S(1)} %copy-done.18), channel_id=1, source_target_pairs={{11,0},{6,1},{9,2},{4,3},{15,4},{2,5},{13,6},{0,7},{3,8},{14,9},{1... | collective-permute-start | bytes 4128776 | tf_op jit(solution)/shard_map/ppermute | solution.py:474
  1026.8 61.0 %collective-permute-start.50 = (f32[16,768]{1,0:T(8,128)S(1)}, f32[16,768]{1,0:T(8,128)S(1)}, u32[]{:S(2)}, u32[]{:S(2)}) collective-permute-start(f32[16,768]{1,0:T(8,128)S(1)} %add.269), channel_id=1, source_target_pairs={{0,12},{1,13},{2,14},{3,15},{4,8},{5,9},{6,10},{7,11},{8,4},{9,5},... | collective-permute-start | bytes 147464 | tf_op jit(solution)/shard_map/ppermute | solution.py:681
  1033.1 54.7 %collective-permute-start.49 = (f32[16,768]{1,0:T(8,128)S(1)}, f32[16,768]{1,0:T(8,128)S(1)}, u32[]{:S(2)}, u32[]{:S(2)}) collective-permute-start(f32[16,768]{1,0:T(8,128)S(1)} %add.269), channel_id=1, source_target_pairs={{0,8},{1,9},{2,10},{3,11},{4,12},{5,13},{6,14},{7,15},{8,0},{9,1},... | collective-permute-start | bytes 147464 | tf_op jit(solution)/shard_map/ppermute | solution.py:681
  1033.1 54.7 %collective-permute-start.48 = (f32[16,768]{1,0:T(8,128)S(1)}, f32[16,768]{1,0:T(8,128)S(1)}, u32[]{:S(2)}, u32[]{:S(2)}) collective-permute-start(f32[16,768]{1,0:T(8,128)S(1)} %add.269), channel_id=1, source_target_pairs={{0,4},{1,5},{2,6},{3,7},{4,0},{5,1},{6,2},{7,3},{8,12},{9,13},{10,... | collective-permute-start | bytes 147464 | tf_op jit(solution)/shard_map/ppermute | solution.py:681
  (26 other events, 983.0 us)
where the time goes:
time: 1110 us; the launch traced here: 1090 us
  Pallas kernels  507 us (46%)
  waiting for transfers between devices  375 us (34%)
  starting transfers between devices  172 us (15%)
  local copies, waits for them, and re-layouts  16.7 us (2%)
  other arithmetic  16.3 us (1%)
    ppermute x18, waiting for transfers between devices, permute(): return [lax.ppermute(v, dev_axes, pairs) for v in values]  199 us
    ppermute x28, waiting for transfers between devices, exchange(): out.append(lax.ppermute(parts[s], dev_axes, pairs[s]))  174 us
    pallas_call x3, Pallas kernels, backward(): pl.pallas_call(functools.partial(backward_kernel, first=first), grid_spec...  163 us
    ppermute x28, starting transfers between devices, exchange(): out.append(lax.ppermute(parts[s], dev_axes, pairs[s]))  134 us
    pallas_call x4, Pallas kernels, forward(): pl.pallas_call(functools.partial(forward_kernel, first=first, last=last),...  126 us
    pallas_call x1, Pallas kernels, backward_rows(): pl.pallas_call(backward_rows_kernel, grid_spec=pltpu.PrefetchScalarGridSp...  42.9 us
    pallas_call x1, Pallas kernels, weight_grads(): pl.pallas_call(weight_grads_kernel, grid_spec=pltpu.PrefetchScalarGridSpe...  29.6 us
    pallas_call x1, Pallas kernels, layer(): y_combine(order, base, my_kept, *y_recv, after(info, dx_send[0]), hidden,...  27.7 us
  transfers between devices with their start and end apart: 51, of which 14 were waited for; matrix products, arithmetic and copies ran while one was open for 2% of the time, Pallas kernels for 46%

commit v1 on v0

v1 whole, which is shorter than its diff:
```python
import functools
import jax
import jax.numpy as jnp
import numpy as np
from jax import lax
from jax.experimental import pallas as pl
from jax.experimental.pallas import tpu as pltpu
from jax.sharding import PartitionSpec as P


AUX_COEF = 0.01
OUT_SCALE = 2.0
BF16 = jnp.bfloat16
F32 = jnp.float32
I32 = jnp.int32
VMEM_LIMIT = 62 * 1024 * 1024


N_SHIFT = 8
N_LOCAL = 4
TOK_TILE = 256
ROW_TILE = 512
ALIGN = 16
WIN = TOK_TILE + ALIGN


def coords(i):
    return (i >> 3) & 1, (i >> 2) & 1, (i >> 1) & 1, i & 1


def index_of(z, y, x, c):
    return (z << 3) | (y << 2) | (x << 1) | c


def shift_dest(i, s):
    z, y, x, c = coords(i)
    x, c, d = x ^ ((s >> 2) & 1), c ^ ((s >> 1) & 1), s & 1
    return index_of(z, y ^ d, x, c) if c == 0 else index_of(z ^ d, y, x, c)


def split_partner(i):
    z, y, x, c = coords(i)
    return index_of(z, y ^ 1, x, c) if c == 0 else index_of(z ^ 1, y, x, c)


def twin_partner(i):
    z, y, x, c = coords(i)
    return index_of(z ^ 1, y, x, c) if c == 0 else index_of(z, y ^ 1, x, c)


def dot_nn(a, b):
    return lax.dot_general(a, b, (((1,), (0,)), ((), ())), preferred_element_type=F32)


def dot_nt(a, b):
    return lax.dot_general(a, b, (((1,), (1,)), ((), ())), preferred_element_type=F32)


def dot_tn(a, b):
    return lax.dot_general(a, b, (((0,), (0,)), ((), ())), preferred_element_type=F32)


def val(ref):
    return ref[...]


def ones_where(condition):
    return jnp.where(condition, 1.0, 0.0).astype(BF16)


def iota(shape, dim):
    return lax.broadcasted_iota(I32, shape, dim)


def tile_columns(ids_t, starts, n_experts, upper, first=0):
    tokens = ids_t.shape[1]
    e_iota = iota((n_experts, tokens), 0) + first
    hot0 = ids_t[0:1, :] == e_iota
    hot1 = ids_t[1:2, :] == e_iota
    either = ones_where(hot0 | hot1)
    before = dot_nn(either, upper).astype(I32)
    offset = jnp.zeros((n_experts, tokens), I32)
    for e in range(n_experts):
        offset = jnp.where(e_iota == first + e, e * WIN + (starts[e] & (ALIGN - 1)), offset)
    column = before + offset + 1
    return [jnp.sum(jnp.where(hot, column, 0), axis=0, keepdims=True) - 1 for hot in (hot0, hot1)]


def strict_upper(n):
    return ones_where(iota((n, n), 0) < iota((n, n), 1))


def add_windows(buf, value, starts, n_experts):
    for e in range(n_experts):
        rows = pl.ds(pl.multiple_of(starts[e] - (starts[e] & (ALIGN - 1)), ALIGN), WIN)
        buf[e, rows, :] = buf[e, rows, :] + value[e * WIN:(e + 1) * WIN, :]


def slots_out(buf, order_ref, outs, sem, first=0):
    slots = outs[0].shape[0]
    copies = [pltpu.make_async_copy(buf.at[order_ref[s] - first, pl.ds(0, slots), :], out, sem.at[s]) for s, out in enumerate(outs)]
    for copy in copies:
        copy.start()
    for copy in copies:
        copy.wait()


def count_kernel(ids_ref, out_ref):
    tokens = ids_ref.shape[1]
    e_iota = iota((128, tokens), 0)
    hot = (ids_ref[0:1, :] == e_iota) | (ids_ref[1:2, :] == e_iota)
    out_ref[...] = dot_nt(jnp.ones((8, tokens), BF16), ones_where(hot)).astype(I32)


def x_slots_kernel(order_ref, ids_ref, h_ref, base_ref, *rest):
    outs, (buf, base_s, sem, base_sem) = rest[:N_LOCAL], rest[N_LOCAL:]
    n_experts, tokens = base_ref.shape[0], ids_ref.shape[1]
    lowest = order_ref[N_LOCAL]
    e_iota = iota((n_experts, tokens), 0)
    hot = (ids_ref[0:1, :] == e_iota) | (ids_ref[1:2, :] == e_iota)
    earlier = ones_where(iota((tokens, 128), 0) < TOK_TILE * iota((tokens, 128), 1))
    base_ref[...] = dot_nn(ones_where(hot), earlier).astype(I32)
    copy = pltpu.make_async_copy(base_ref, base_s, base_sem)
    copy.start()
    buf[...] = jnp.zeros_like(buf)
    copy.wait()
    upper = strict_upper(TOK_TILE)

    @pl.loop(0, tokens // TOK_TILE)
    def _(t):
        here = pl.ds(pl.multiple_of(t * TOK_TILE, TOK_TILE), TOK_TILE)
        starts = [base_s[lowest + e, t] for e in range(N_LOCAL)]
        col0, col1 = tile_columns(ids_ref[:, here], starts, N_LOCAL, upper, lowest)
        row = iota((N_LOCAL * WIN, TOK_TILE), 0)
        pick = ones_where((row == col0) | (row == col1))
        add_windows(buf, dot_nn(pick, h_ref[here, :]).astype(BF16), starts, N_LOCAL)

    slots_out(buf, order_ref, outs, sem, lowest)


def c_slots_kernel(order_ref, base_s, ids_ref, h_ref, dy_ref, wr3_ref, info_ref, psum_ref, *rest):
    outs, (buf, prob_buf, sem) = rest[:N_SHIFT], rest[N_SHIFT:]
    n_experts, tokens = psum_ref.shape[0], ids_ref.shape[1]
    parts = dot_nt(val(wr3_ref), val(h_ref))
    logits = parts[2 * n_experts:3 * n_experts] + parts[n_experts:2 * n_experts] + parts[0:n_experts]
    top = jnp.max(logits, axis=0, keepdims=True)
    expo = jnp.exp(logits - top)
    prob = expo / jnp.sum(expo, axis=0, keepdims=True)
    prob_buf[...] = prob
    psum_ref[...] = jnp.broadcast_to(jnp.sum(prob, axis=1, keepdims=True), psum_ref.shape)
    buf[...] = jnp.zeros_like(buf)
    upper = strict_upper(TOK_TILE)

    @pl.loop(0, tokens // TOK_TILE)
    def _(t):
        here = pl.ds(pl.multiple_of(t * TOK_TILE, TOK_TILE), TOK_TILE)
        starts = [base_s[e, t] for e in range(n_experts)]
        ids_t = ids_ref[:, here]
        p_t = prob_buf[:, here]
        e_iota = iota((n_experts, TOK_TILE), 0)
        p0 = jnp.sum(jnp.where(ids_t[0:1, :] == e_iota, p_t, 0.0), axis=0, keepdims=True)
        p1 = jnp.sum(jnp.where(ids_t[1:2, :] == e_iota, p_t, 0.0), axis=0, keepdims=True)
        total = p0 + p1
        g0, g1 = p0 / total, p1 / total
        col0, col1 = tile_columns(ids_t, starts, n_experts, upper)
        row = iota((n_experts * WIN, TOK_TILE), 0)
        is0, is1 = row == col0, row == col1
        pick = ones_where(is0 | is1)
        gate = jnp.sum(jnp.where(is0, g0, jnp.where(is1, g1, 0.0)), axis=1, keepdims=True)
        mixed = OUT_SCALE * dot_nn(pick, dy_ref[here, :])
        add_windows(buf, (gate * mixed).astype(BF16), starts, n_experts)
        group = iota((8, TOK_TILE), 0)
        extra = jnp.zeros((8, TOK_TILE), F32)
        for k, v in enumerate((g0, g1, col0.astype(F32), col1.astype(F32), ids_t[0:1, :].astype(F32), ids_t[1:2, :].astype(F32))):
            extra = jnp.where(group == k, v, extra)
        table = jnp.concatenate([p_t] * 6 + [extra, jnp.zeros((128 - 6 * n_experts - 8, TOK_TILE), F32)], axis=0)
        info_ref[here, :] = table.T

    slots_out(buf, order_ref, outs, sem)


def pack_rows(kept_s, offset_s, ins, out_ref, buf, sem, out_sem):
    sizes = [512, 256, 128, 64, 32, 16]

    def for_parts(s, act):
        offset = offset_s[s]
        count = offset_s[s + 1] - offset
        done = jnp.int32(0)
        for j, size in enumerate(sizes):
            has = (count & size) != 0
            start = pl.multiple_of(done, ALIGN)
            dest = pl.multiple_of(offset + done, ALIGN)

            @pl.when(has)
            def _(j=j, size=size, start=start, dest=dest):
                rows = pl.ds(dest, size)
                act(lambda: pltpu.make_async_copy(ins[s].at[pl.ds(start, size), :], buf.at[rows, :], sem.at[s, j]),
                    lambda: pltpu.make_async_copy(buf.at[rows, :], out_ref.at[rows, :], out_sem.at[s, j]))

            done = done + jnp.where(has, size, 0)

    def tail_copy():
        tail = pl.ds(pl.multiple_of(offset_s[N_SHIFT], ALIGN), ROW_TILE)
        return tail, pltpu.make_async_copy(buf.at[tail, :], out_ref.at[tail, :], out_sem.at[N_SHIFT, 0])

    def begin():
        for s in range(N_SHIFT):
            for_parts(s, lambda load, store: load().start())
        tail, copy = tail_copy()
        buf[tail, :] = jnp.zeros((ROW_TILE, buf.shape[1]), buf.dtype)
        for s in range(N_SHIFT):
            for_parts(s, lambda load, store: load().wait())
            extra = kept_s[s] & (ALIGN - 1)

            @pl.when(extra != 0)
            def _(s=s, extra=extra):
                group = pl.ds(pl.multiple_of(offset_s[s] + kept_s[s] - extra, ALIGN), ALIGN)
                rows = buf[group, :]
                buf[group, :] = jnp.where(iota(rows.shape, 0) < extra, rows, jnp.zeros_like(rows))

            for_parts(s, lambda load, store: store().start())
        copy.start()

    def end():
        for s in range(N_SHIFT):
            for_parts(s, lambda load, store: store().wait())
        tail_copy()[1].wait()

    pl.when(pl.program_id(0) == 0)(begin)
    return lambda: pl.when(pl.program_id(0) == pl.num_programs(0) - 1)(end)


def rows_out(buf, offset_s, outs, sem):
    slots = outs[0].shape[0]
    copies = [pltpu.make_async_copy(buf.at[pl.ds(pl.multiple_of(offset_s[s], ALIGN), slots), :], outs[s], sem.at[s]) for s in range(N_SHIFT)]
    for copy in copies:
        copy.start()
    for copy in copies:
        copy.wait()


def clear(refs):
    @pl.when(pl.program_id(0) == 0)
    def _():
        for ref in refs:
            ref[...] = jnp.zeros_like(ref)


def row_tile(buf):
    return buf[pl.ds(pl.multiple_of(pl.program_id(0) * ROW_TILE, ROW_TILE), ROW_TILE), :]


def forward_first_kernel(n_ref, offset_s, kept_s, *refs):
    ins, refs = refs[:N_SHIFT], refs[N_SHIFT:]
    w1_ref, w3_ref, w2_ref, a_ref, b_ref, y_out, rows_ref, buf, sem, out_sem = refs
    end = pack_rows(kept_s, offset_s, ins, rows_ref, buf, sem, out_sem)

    @pl.when(pl.program_id(0) < n_ref[0])
    def _():
        x = row_tile(buf)
        a = dot_nn(x, val(w1_ref))
        b = dot_nn(x, val(w3_ref))
        a_ref[...] = a
        b_ref[...] = b
        y_out[...] = dot_nn((a * jax.nn.sigmoid(a) * b).astype(BF16), val(w2_ref))

    end()


def forward_kernel(n_ref, offset_s, x_ref, w1_ref, w3_ref, w2_ref, y_in, a_ref, b_ref, *rest, last):
    if last:
        outs, (buf, sem) = rest[:N_SHIFT], rest[N_SHIFT:]
    i = pl.program_id(0)

    @pl.when(i < n_ref[0])
    def _():
        a = dot_nn(val(x_ref), val(w1_ref))
        b = dot_nn(val(x_ref), val(w3_ref))
        a_ref[...] = a
        b_ref[...] = b
        y = val(y_in) + dot_nn((a * jax.nn.sigmoid(a) * b).astype(BF16), val(w2_ref))
        if last:
            buf[pl.ds(pl.multiple_of(i * ROW_TILE, ROW_TILE), ROW_TILE), :] = y.astype(BF16)
        else:
            rest[0][...] = y

    if last:
        @pl.when(i == pl.num_programs(0) - 1)
        def _():
            rows_out(buf, offset_s, outs, sem)


def act_grads(du, a, b):
    sig = jax.nn.sigmoid(a)
    silu = a * sig
    da = (du * b * sig * (1.0 + a * (1.0 - sig))).astype(BF16)
    return da, (du * silu).astype(BF16), (silu * b).astype(BF16)


def add_weight_grads(x, c, da, db, u, g1_ref, g3_ref, g2_ref):
    g1_ref[...] += dot_tn(x, da)
    g3_ref[...] += dot_tn(x, db)
    g2_ref[...] += dot_tn(u, c)


def backward_first_kernel(n_ref, offset_s, kept_s, *refs):
    ins, refs = refs[:N_SHIFT], refs[N_SHIFT:]
    x_ref, a_ref, b_ref, w1_ref, w3_ref, w2_ref, g1_ref, g3_ref, g2_ref, dx_out, rows_ref, buf, sem, out_sem = refs
    clear((g1_ref, g3_ref, g2_ref))
    end = pack_rows(kept_s, offset_s, ins, rows_ref, buf, sem, out_sem)

    @pl.when(pl.program_id(0) < n_ref[0])
    def _():
        c = row_tile(buf)
        da, db, u = act_grads(dot_nt(c, val(w2_ref)), val(a_ref), val(b_ref))
        dx_out[...] = dot_nt(da, val(w1_ref)) + dot_nt(db, val(w3_ref))
        add_weight_grads(val(x_ref), c, da, db, u, g1_ref, g3_ref, g2_ref)

    end()


def backward_kernel(n_ref, offset_s, x_ref, c_ref, a_ref, b_ref, w1_ref, w3_ref, w2_ref, dx_in, g1_ref, g3_ref, g2_ref, dx_out):
    clear((g1_ref, g3_ref, g2_ref))

    @pl.when(pl.program_id(0) < n_ref[0])
    def _():
        da, db, u = act_grads(dot_nt(val(c_ref), val(w2_ref)), val(a_ref), val(b_ref))
        dx_out[...] = val(dx_in) + (dot_nt(da, val(w1_ref)) + dot_nt(db, val(w3_ref)))
        add_weight_grads(val(x_ref), val(c_ref), da, db, u, g1_ref, g3_ref, g2_ref)


def both_kernel(n_ref, offset_s, x_ref, c_ref, w1_ref, w3_ref, w2_ref, y_in, dx_in, g1_ref, g3_ref, g2_ref, dx_out, y_out):
    clear((g1_ref, g3_ref, g2_ref))

    @pl.when(pl.program_id(0) < n_ref[0])
    def _():
        x, c = val(x_ref), val(c_ref)
        a = dot_nn(x, val(w1_ref))
        b = dot_nn(x, val(w3_ref))
        da, db, u = act_grads(dot_nt(c, val(w2_ref)), a, b)
        y_out[...] = val(y_in) + dot_nn(u, val(w2_ref))
        dx_out[...] = val(dx_in) + (dot_nt(da, val(w1_ref)) + dot_nt(db, val(w3_ref)))
        add_weight_grads(x, c, da, db, u, g1_ref, g3_ref, g2_ref)


def backward_rows_kernel(n_ref, offset_s, c_ref, a_ref, b_ref, w1_ref, w3_ref, w2_ref, dx_in, *rest):
    outs, (buf, sem) = rest[:N_SHIFT], rest[N_SHIFT:]
    i = pl.program_id(0)

    @pl.when(i < n_ref[0])
    def _():
        da, db, _ = act_grads(dot_nt(val(c_ref), val(w2_ref)), val(a_ref), val(b_ref))
        dx = val(dx_in) + (dot_nt(da, val(w1_ref)) + dot_nt(db, val(w3_ref)))
        buf[pl.ds(pl.multiple_of(i * ROW_TILE, ROW_TILE), ROW_TILE), :] = dx.astype(BF16)

    @pl.when(i == pl.num_programs(0) - 1)
    def _():
        rows_out(buf, offset_s, outs, sem)


def weight_grads_kernel(n_ref, offset_s, x_ref, c_ref, a_ref, b_ref, w2_ref, g1_ref, g3_ref, g2_ref):
    clear((g1_ref, g3_ref, g2_ref))

    @pl.when(pl.program_id(0) < n_ref[0])
    def _():
        da, db, u = act_grads(dot_nt(val(c_ref), val(w2_ref)), val(a_ref), val(b_ref))
        add_weight_grads(val(x_ref), val(c_ref), da, db, u, g1_ref, g3_ref, g2_ref)


def load_slots(order_ref, ins, buf, sem):
    slots = ins[0].shape[0]
    copies = [pltpu.make_async_copy(ins[s], buf.at[order_ref[s], pl.ds(0, slots), :], sem.at[s]) for s in range(N_SHIFT)]
    for copy in copies:
        copy.start()
    for copy in copies:
        copy.wait()


def gather_windows(buf, window, base_s, kept_s, t, n_experts):
    for e in range(n_experts):
        start = base_s[e, t] - (base_s[e, t] & (ALIGN - 1))
        rows = buf[e, pl.ds(pl.multiple_of(start, ALIGN), WIN), :]
        valid = iota(rows.shape, 0) < kept_s[e] - start
        window[e * WIN:(e + 1) * WIN, :] = jnp.where(valid, rows, jnp.zeros_like(rows))


def y_combine_kernel(order_ref, base_s, kept_s, *refs):
    ins, refs = refs[:N_SHIFT], refs[N_SHIFT:]
    info_ref, h_ref, dy_ref, w_ref, out_ref, dz_ref, dwr_ref, buf, window, sem = refs
    n_experts = buf.shape[0]
    t = pl.program_id(0)

    @pl.when(t == 0)
    def _():
        load_slots(order_ref, ins, buf, sem)
        dwr_ref[...] = jnp.zeros_like(dwr_ref)

    gather_windows(buf, window, base_s, kept_s, t, n_experts)
    info = val(info_ref)
    k0 = 6 * n_experts
    g0, g1, col0, col1, e0, e1 = [info[:, k0 + k:k0 + k + 1] for k in range(6)]
    col = iota((TOK_TILE, n_experts * WIN), 1)
    pick0 = ones_where(col == col0.astype(I32))
    pick1 = ones_where(col == col1.astype(I32))
    y0 = dot_nn(pick0, val(window))
    y1 = dot_nn(pick1, val(window))
    h = val(h_ref)
    mix = OUT_SCALE * val(dy_ref).astype(F32)
    out_ref[...] = (h.astype(F32) + OUT_SCALE * (g0 * y0 + g1 * y1)).astype(BF16)
    dg0 = jnp.sum(mix * y0, axis=1, keepdims=True)
    dg1 = jnp.sum(mix * y1, axis=1, keepdims=True)
    lane = iota(info.shape, 1)
    prob = jnp.where(lane < k0, info, 0.0)
    weight = val(w_ref)
    mean_w = jnp.sum(jnp.where(lane < n_experts, prob * weight, 0.0), axis=1, keepdims=True)
    expert = (lane & (n_experts - 1)).astype(F32)
    sign = jnp.where(expert == e0, 1.0, 0.0) - jnp.where(expert == e1, 1.0, 0.0)
    dz = prob * (weight - mean_w) + g0 * g1 * (dg0 - dg1) * jnp.where(lane < k0, sign, 0.0)
    d1 = dz.astype(BF16)
    rem1 = dz - d1.astype(F32)
    d2 = rem1.astype(BF16)
    d3 = (rem1 - d2.astype(F32)).astype(BF16)
    group = lane // n_experts
    first = (group == 0) | (group == 1) | (group == 3)
    second = (group == 2) | (group == 4)
    dzp = jnp.where(first, d1.astype(F32), jnp.where(second, d2.astype(F32), d3.astype(F32))).astype(BF16)
    dz_ref[...] = dzp
    dwr_ref[...] += dot_tn(dzp, h)


def dx_combine_kernel(order_ref, base_s, kept_s, *refs):
    ins, refs = refs[:N_SHIFT], refs[N_SHIFT:]
    info_ref, dz_ref, dy_ref, wr_ref, out_ref, buf, window, sem = refs
    n_experts = buf.shape[0]
    t = pl.program_id(0)

    @pl.when(t == 0)
    def _():
        load_slots(order_ref, ins, buf, sem)

    gather_windows(buf, window, base_s, kept_s, t, n_experts)
    info = val(info_ref)
    k0 = 6 * n_experts
    col0, col1 = info[:, k0 + 2:k0 + 3].astype(I32), info[:, k0 + 3:k0 + 4].astype(I32)
    col = iota((TOK_TILE, n_experts * WIN), 1)
    pick = ones_where((col == col0) | (col == col1))
    total = val(dy_ref).astype(F32) + dot_nn(pick, val(window)) + dot_nn(val(dz_ref), val(wr_ref))
    out_ref[...] = total.astype(BF16)


def finish_own_kernel(j_ref, own_ref, part_0_ref, part_1_ref, out_ref):
    for piece, part_ref in enumerate((part_0_ref, part_1_ref)):
        @pl.when(pl.program_id(0) == piece)
        def _(part_ref=part_ref):
            out_ref[0] = val(own_ref) + val(part_ref)


def finish_other_kernel(j_ref, other_ref, _, out_ref):
    out_ref[0] = val(other_ref)


def params(*semantics):
    return pltpu.CompilerParams(dimension_semantics=semantics or None, vmem_limit_bytes=VMEM_LIMIT)


def hbm():
    return pl.BlockSpec(memory_space=pl.ANY)


def smem():
    return pl.BlockSpec(memory_space=pltpu.SMEM)


def vmem():
    return pl.BlockSpec(memory_space=pltpu.VMEM)


def cost(flops, nbytes):
    return pl.CostEstimate(flops=int(flops), bytes_accessed=int(nbytes), transcendentals=0)


def split3(v):
    p1 = v.astype(BF16)
    r1 = v - p1.astype(F32)
    p2 = r1.astype(BF16)
    return p1, p2, (r1 - p2.astype(F32)).astype(BF16)


def solution(mesh):
    ep_size = mesh.shape["ep"]
    etp_size = mesh.shape["etp"]
    n_dev = ep_size * etp_size
    all_axes = ("ep", "etp")
    dev_axes = ("etp", "ep")
    tok_spec = P(all_axes, None)
    gate_spec = P("ep", None, "etp")
    down_spec = P("ep", "etp", None)

    def layer(hidden, w_router, expert_ids, d_out, w_gate, w_up, w_down):
        tok_rows, d_model = hidden.shape
        n_experts = w_router.shape[1]
        n_tokens = tok_rows * n_dev
        capacity = (5 * n_tokens + 2 * n_experts - 1) // (2 * n_experts)
        slots = 7 * tok_rows // (2 * n_experts)
        width = w_gate.shape[2]
        rows = N_SHIFT * slots
        buf_rows = slots + WIN + ALIGN
        etp, ep = lax.axis_index("etp"), lax.axis_index("ep")
        z, y, x, c = etp >> 1, etp & 1, ep >> 1, ep & 1
        mine = jnp.where(c == 0, y, z)

        def permute(values, pairs):
            return [lax.ppermute(v, dev_axes, pairs) for v in values]

        def exchange(parts, pairs):
            out = [parts[0]]
            for s in range(1, len(parts)):
                out.append(lax.ppermute(parts[s], dev_axes, pairs[s]))
            return out

        def after(value, earlier):
            return lax.optimization_barrier((value, earlier))[0]

        forth = [[(i, shift_dest(i, s)) for i in range(n_dev)] for s in range(N_SHIFT)]
        back = [[(b, a) for a, b in pairs] for pairs in forth]
        split_pairs = [(i, split_partner(i)) for i in range(n_dev)]
        twin_pairs = [(i, twin_partner(i)) for i in range(n_dev)]

        order = []
        source = []
        for s in range(N_SHIFT):
            dx, dc, d = (s >> 2) & 1, (s >> 1) & 1, s & 1
            order.append(4 * (x ^ dx) + 2 * (c ^ dc) + (jnp.where((c ^ dc) == 0, y, z) ^ d))
            sx, sc = x ^ dx, c ^ dc
            sz = jnp.where(c == 0, z, z ^ d)
            sy = jnp.where(c == 0, y ^ d, y)
            source.append((sx * 2 + sc) * etp_size + sz * 2 + sy)
        order = jnp.stack(order).astype(I32)
        source = jnp.stack(source).astype(I32)

        ids_t = expert_ids.T
        slot_shape = jax.ShapeDtypeStruct((slots, d_model), BF16)
        slot_buf = pltpu.VMEM((n_experts, buf_rows, d_model), BF16)
        dma8 = pltpu.SemaphoreType.DMA((N_SHIFT,))
        spread_flops = 2 * tok_rows * n_experts * WIN * d_model

        def flip(value, bits):
            return lax.ppermute(value, dev_axes, [(i, i ^ bits) for i in range(n_dev)])

        steps = (2, 4, 8, 1)
        table = pl.pallas_call(
            count_kernel, in_specs=[vmem()], out_specs=vmem(), out_shape=jax.ShapeDtypeStruct((8, 128), I32), compiler_params=params(),
        )(ids_t)[:1]
        table = jnp.concatenate([table, flip(table, 2)])
        table = jnp.concatenate([table, flip(table, 4), flip(table, 8), flip(table, 12)])
        table = jnp.concatenate([table, flip(table, 1)])
        ids_peer, h_peer = flip(ids_t, 2), flip(hidden, 2)

        local_order = jnp.concatenate([order[:N_LOCAL], (4 * x)[None]])
        x_slots = pl.pallas_call(
            x_slots_kernel,
            in_specs=[smem(), vmem(), vmem()],
            out_specs=[vmem()] + [hbm()] * N_LOCAL,
            out_shape=[jax.ShapeDtypeStruct((n_experts, 128), I32)] + [slot_shape] * N_LOCAL,
            scratch_shapes=[pltpu.VMEM((N_LOCAL, buf_rows, d_model), BF16), pltpu.SMEM((n_experts, 128), I32), pltpu.SemaphoreType.DMA((N_LOCAL,)), pltpu.SemaphoreType.DMA],
            compiler_params=params(), cost_estimate=cost(spread_flops // 2, rows * d_model),
        )
        base, *x_own = x_slots(local_order, ids_t, hidden)
        _, *x_peer = x_slots(local_order, ids_peer, h_peer)
        x_recv = exchange(x_own, forth) + exchange(x_peer, forth)

        device = np.arange(n_dev)
        place = np.zeros(n_dev, np.int32)
        for step, bits in enumerate(steps):
            place += ((device & bits) != 0) << step
        by_block = [t * ep_size + o for o in range(ep_size) for t in range(etp_size)]
        me = etp * ep_size + ep
        count_table = jnp.take(table[:, :n_experts], jnp.take(jnp.asarray(place), jnp.asarray(by_block, I32) ^ me), axis=0)
        running = jnp.cumsum(count_table, axis=0) - count_table
        total_count = jnp.sum(count_table, axis=0)
        block_idx = ep * etp_size + etp
        limit = jnp.clip(capacity - running, 0, None)
        kept_table = jnp.minimum(count_table, limit)
        my_kept = kept_table[block_idx]
        my_expert = order[0]
        kept = kept_table[source, my_expert]
        part = (kept + ALIGN - 1) // ALIGN * ALIGN
        offset = jnp.concatenate([jnp.zeros((1,), I32), jnp.cumsum(part)]).astype(I32)
        n_tiles = (offset[N_SHIFT:] + ROW_TILE - 1) // ROW_TILE

        wr_t = split3(w_router.T)
        wr3 = jnp.concatenate(wr_t + (jnp.zeros_like(wr_t[0]),), axis=0)
        wr6 = jnp.concatenate([wr_t[0], wr_t[1], wr_t[0], wr_t[2], wr_t[1], wr_t[0], jnp.zeros((128 - 6 * n_experts, d_model), BF16)], axis=0)
        c_slots = pl.pallas_call(
            c_slots_kernel,
            in_specs=[smem()] * 2 + [vmem()] * 4,
            out_specs=[vmem()] * 2 + [hbm()] * N_SHIFT,
            out_shape=[jax.ShapeDtypeStruct((tok_rows, 128), F32), jax.ShapeDtypeStruct((n_experts, 128), F32)] + [slot_shape] * N_SHIFT,
            scratch_shapes=[slot_buf, pltpu.VMEM((n_experts, tok_rows), F32), dma8],
            compiler_params=params(), cost_estimate=cost(spread_flops, 2 * rows * d_model),
        )
        info, prob_sum, *c_send = c_slots(order, base, ids_t, hidden, d_out, wr3)

        def take(w, j):
            return lax.dynamic_index_in_dim(w, j, 0, keepdims=False)

        weights = (w_gate, w_up, w_down)
        q_own = [take(w, mine) for w in weights]
        q_twin = permute(q_own[:1], twin_pairs) + permute(q_own[1:], twin_pairs)
        q_split = permute([take(w, 1 - mine) for w in weights], split_pairs)
        q_far = permute(q_split, twin_pairs)

        c_recv = exchange(c_send, forth)

        def row_spec(w):
            return pl.BlockSpec((ROW_TILE, w), lambda i, n, *_: (jnp.clip(n[0] - 1, 0, i), 0))

        def full_spec(shape):
            return pl.BlockSpec(shape, lambda i, *_: (0, 0), pipeline_mode=pl.Buffered(1))

        grid = (rows // ROW_TILE,)
        up_shape, down_shape = (d_model, width), (width, d_model)
        row_f32 = jax.ShapeDtypeStruct((rows, d_model), F32)
        act_shape = jax.ShapeDtypeStruct((rows, width), F32)
        row_buf = pltpu.VMEM((rows + slots, d_model), BF16)
        mm = 2 * rows * d_model * width

        grad_shapes = [jax.ShapeDtypeStruct(up_shape, F32)] * 2 + [jax.ShapeDtypeStruct(down_shape, F32)]
        full = [full_spec(up_shape), full_spec(up_shape), full_spec(down_shape)]

        def rows_call(kernel, matmuls, ins, outs, shapes, scratch, aliases, *args, scalars=2):
            return pl.pallas_call(
                kernel,
                grid_spec=pltpu.PrefetchScalarGridSpec(num_scalar_prefetch=scalars, grid=grid, in_specs=ins, out_specs=outs, scratch_shapes=scratch),
                out_shape=shapes, input_output_aliases=aliases,
                compiler_params=params("arbitrary"), cost_estimate=cost(matmuls * mm, 20 * rows * d_model),
            )(n_tiles, offset, *args)

        slots_outs, slots_shapes, slots_scratch = [hbm()] * N_SHIFT, [slot_shape] * N_SHIFT, [row_buf, dma8]

        packed = jax.ShapeDtypeStruct((rows + ROW_TILE, d_model), BF16)
        pack_scratch = [pltpu.VMEM((rows + ROW_TILE, d_model), BF16), pltpu.SemaphoreType.DMA((N_SHIFT, 6)), pltpu.SemaphoreType.DMA((N_SHIFT + 1, 6))]

        def forward_first(quarter, parts):
            out = rows_call(
                forward_first_kernel, 3, [hbm()] * N_SHIFT + full, [row_spec(width)] * 2 + [row_spec(d_model), hbm()],
                [act_shape] * 2 + [row_f32, packed], pack_scratch, {}, kept, *parts, *quarter, scalars=3)
            return out[:2], out[2], out[3]

        def forward(quarter, y_acc, last=False):
            out = rows_call(
                functools.partial(forward_kernel, last=last), 3,
                [row_spec(d_model)] + full + [row_spec(d_model)], [row_spec(width)] * 2 + (slots_outs if last else [row_spec(d_model)]),
                [act_shape] * 2 + (slots_shapes if last else [row_f32]), slots_scratch if last else [], {} if last else {6: 2},
                x_rows, *quarter, y_acc)
            return out[:2], (out[2:] if last else out[2])

        def half(piece, pieces):
            w = width // pieces
            shapes = [(d_model, w), (d_model, w), (w, d_model)]
            act_spec = pl.BlockSpec((ROW_TILE, w), lambda i, n, *_: (jnp.clip(n[0] - 1, 0, i), piece))
            at = [(0, piece), (0, piece), (piece, 0)]
            w_specs = [pl.BlockSpec(shape, lambda i, *_, at=at: at, pipeline_mode=pl.Buffered(1)) for shape, at in zip(shapes, at)]
            return act_spec, w_specs, [full_spec(shape) for shape in shapes], [jax.ShapeDtypeStruct(shape, F32) for shape in shapes]

        def backward_first(quarter, acts, parts):
            act_spec, w_specs, g_specs, g_shapes = half(0, 2)
            out = rows_call(
                backward_first_kernel, 3, [hbm()] * N_SHIFT + [row_spec(d_model)] + [act_spec] * 2 + w_specs,
                g_specs + [row_spec(d_model), hbm()], g_shapes + [row_f32, packed], pack_scratch, {}, kept, *parts, x_rows, *acts, *quarter, scalars=3)
            return out[:3], out[3], out[4]

        def backward(quarter, acts, dx_acc, piece, pieces):
            act_spec, w_specs, g_specs, g_shapes = half(piece, pieces)
            out = rows_call(
                backward_kernel, 6 // pieces, [row_spec(d_model)] * 2 + [act_spec] * 2 + w_specs + [row_spec(d_model)],
                g_specs + [row_spec(d_model)], g_shapes + [row_f32], [], {9: 3}, x_rows, c_rows, *acts, *quarter, dx_acc)
            return out[:3], out[3]

        def both(quarter, y_acc, dx_acc):
            out = rows_call(
                both_kernel, 9, [row_spec(d_model)] * 2 + full + [row_spec(d_model)] * 2, full + [row_spec(d_model)] * 2,
                grad_shapes + [row_f32] * 2, [], {8: 3, 7: 4}, x_rows, c_rows, *quarter, y_acc, dx_acc)
            return out[:3], out[3], out[4]

        def backward_rows(quarter, acts, dx_acc):
            return rows_call(
                backward_rows_kernel, 3, [row_spec(d_model)] + [row_spec(width)] * 2 + full + [row_spec(d_model)], slots_outs,
                slots_shapes, slots_scratch, {}, c_rows, *acts, *quarter, dx_acc)

        def weight_grads(quarter, acts):
            return rows_call(
                weight_grads_kernel, 4, [row_spec(d_model)] * 2 + [row_spec(width)] * 2 + full[2:], full,
                grad_shapes, [], {}, x_rows, c_rows, *acts, quarter[2])

        act_own, acc_y, x_rows = forward_first(q_own, x_recv)
        act_twin, acc_y = forward(q_twin, acc_y)
        g_twin_0, acc_dx, c_rows = backward_first(q_twin, act_twin, [after(c_recv[0], acc_y)] + c_recv[1:])
        g_twin_0 = permute(g_twin_0, twin_pairs)
        g_twin_1, acc_dx = backward(q_twin, act_twin, acc_dx, 1, 2)
        g_twin_1 = permute(g_twin_1, twin_pairs)
        g_far, acc_dx, acc_y = both(q_far, acc_y, acc_dx)
        g_far = permute(g_far, twin_pairs)
        act_split, y_send = forward(q_split, acc_y, True)
        y_recv = exchange(y_send, back)
        g_split, acc_dx = backward(q_split, [after(act_split[0], acc_dx), act_split[1]], acc_dx, 0, 1)
        got_split = permute([g_split[0] + g_far[0]], split_pairs)
        dx_send = backward_rows(q_own, act_own, acc_dx)
        dx_recv = exchange(dx_send, back)

        g_split = got_split + permute([after(a, dx_send[0]) + b for a, b in zip(g_split[1:], g_far[1:])], split_pairs)
        g_own = weight_grads(q_own, [after(act_own[0], dx_send[0]), act_own[1]])
        route_frac = total_count.astype(F32) / (2 * n_tokens)
        aux_weight = (AUX_COEF * n_experts / n_tokens) * route_frac
        weight_row = jnp.concatenate([jnp.tile(aux_weight, 6), jnp.zeros((128 - 6 * n_experts,), F32)])[None, :]

        def tok_block(w):
            return pl.BlockSpec((TOK_TILE, w), lambda t: (t, 0))

        def whole(shape):
            return pl.BlockSpec(shape, lambda t: (0, 0))

        combine_scratch = [slot_buf, pltpu.VMEM((n_experts * WIN, d_model), BF16), dma8]
        y_combine = pl.pallas_call(
            y_combine_kernel, grid=(tok_rows // TOK_TILE,),
            in_specs=[smem()] * 3 + [hbm()] * N_SHIFT + [tok_block(128), tok_block(d_model), tok_block(d_model), whole((1, 128))],
            out_specs=[tok_block(d_model), tok_block(128), whole((128, d_model))],
            out_shape=[jax.ShapeDtypeStruct((tok_rows, d_model), BF16), jax.ShapeDtypeStruct((tok_rows, 128), BF16), jax.ShapeDtypeStruct((128, d_model), F32)],
            scratch_shapes=combine_scratch,
            compiler_params=params("arbitrary"), cost_estimate=cost(2 * spread_flops, 4 * rows * d_model),
        )
        output, dz, dwr = y_combine(order, base, my_kept, *y_recv, after(info, g_own[0]), hidden, d_out, weight_row)
        dwr_t = dwr[0:n_experts] + dwr[2 * n_experts:3 * n_experts] + dwr[5 * n_experts:6 * n_experts]
        shared = jnp.concatenate([dwr_t, jnp.pad(prob_sum, ((0, 0), (0, d_model - 128)))], axis=0)

        shared = shared + flip(shared, 1)
        across_x = flip(shared, 2)

        def finish_other(other, aliased):
            r, w = other.shape
            return pl.pallas_call(
                finish_other_kernel,
                grid_spec=pltpu.PrefetchScalarGridSpec(
                    num_scalar_prefetch=1, grid=(2,), in_specs=[pl.BlockSpec((r // 2, w), lambda i, j: (i, 0)), hbm()],
                    out_specs=pl.BlockSpec((1, r // 2, w), lambda i, j: (j[0] ^ 1, i, 0))),
                out_shape=jax.ShapeDtypeStruct((2, r, w), F32), input_output_aliases={2: 0},
                compiler_params=params("arbitrary"), cost_estimate=cost(10**9, 12 * r * w),
            )(mine[None].astype(I32), other, aliased)

        def finish_own(own, got_0, got_1):
            r, w = own.shape
            block = (r // 2, w) if got_0.shape[0] != r else (r, w // 2)
            place = (lambda i: (i, 0)) if got_0.shape[0] != r else (lambda i: (0, i))
            spec = pl.BlockSpec(block, lambda i, j: (0, 0), pipeline_mode=pl.Buffered(1))
            return pl.pallas_call(
                finish_own_kernel,
                grid_spec=pltpu.PrefetchScalarGridSpec(
                    num_scalar_prefetch=1, grid=(2,), in_specs=[pl.BlockSpec(block, lambda i, j: place(i)), spec, spec],
                    out_specs=pl.BlockSpec((1,) + block, lambda i, j: (j[0],) + place(i))),
                out_shape=jax.ShapeDtypeStruct((2, r, w), F32),
                compiler_params=params("arbitrary"), cost_estimate=cost(10**9, 12 * r * w),
            )(mine[None].astype(I32), own, got_0, got_1)

        halves = [finish_own(after(own, shared), got_0, got_1) for own, got_0, got_1 in zip(g_own, g_twin_0, g_twin_1)]
        d_hidden = pl.pallas_call(
            dx_combine_kernel, grid=(tok_rows // TOK_TILE,),
            in_specs=[smem()] * 3 + [hbm()] * N_SHIFT + [tok_block(128), tok_block(128), tok_block(d_model), whole((128, d_model))],
            out_specs=tok_block(d_model),
            out_shape=jax.ShapeDtypeStruct((tok_rows, d_model), BF16),
            scratch_shapes=combine_scratch,
            compiler_params=params("arbitrary"), cost_estimate=cost(spread_flops, 4 * rows * d_model),
        )(order, base, my_kept, *dx_recv, after(info, halves), dz, d_out, wr6)

        shared = shared + after(across_x, d_hidden)
        across = [flip(shared, bits) for bits in (4, 8, 12)]
        done = d_hidden
        outputs = []
        for other, half in zip(g_split, halves):
            done = finish_other(after(other, done), half)
            outputs.append(done)
        d_gate, d_up, d_down = outputs
        across = [after(v, d_down) for v in across]
        shared = (shared + across[0]) + (across[1] + across[2])
        d_router = shared[:n_experts].T
        prob_total = shared[n_experts:, 0]
        aux_loss = AUX_COEF * n_experts * jnp.sum(route_frac * (prob_total / n_tokens))
        return output, d_hidden, d_router, aux_loss, d_gate, d_up, d_down

    return jax.shard_map(layer, mesh=mesh, in_specs=(tok_spec, P(), tok_spec, tok_spec, gate_spec, gate_spec, down_spec), out_specs=(tok_spec, tok_spec, P(), P(), gate_spec, gate_spec, down_spec), check_vma=False)
```

time: 1110 us -> 1070 us (0.964)
  waiting for transfers between devices: 375 us -> 335 us
    ppermute x28 -> x27, waiting for transfers between devices: 174 us -> 101 us  [exchange(): out.append(lax.ppermute(parts[s], dev_axes, pairs[s]))]
    ppermute x18 -> x21, waiting for transfers between devices: 199 us -> 225 us  [permute(): return [lax.ppermute(v, dev_axes, pairs) for v in values]]
    ppermute x18 -> x21, starting transfers between devices: 24.7 us -> 32.6 us  [permute(): return [lax.ppermute(v, dev_axes, pairs) for v in values]]
    ppermute x28 -> x27, starting transfers between devices: 134 us -> 126 us  [exchange(): out.append(lax.ppermute(parts[s], dev_axes, pairs[s]))]
    pallas_call x18 -> x20, Pallas kernels: 488 us -> 480 us  [the longest x9 375 us: rows_call(): pl.pallas_call(kernel, grid_spec=pltpu.PrefetchScalarGridSpec(num_scalar_...]
  transfers between devices with their start and end apart: 51 -> 60, of which waited for: 14 -> 18; matrix products, arithmetic and copies ran while one was open for 2% -> 3% of each run, Pallas kernels for 46% -> 37%
where the time goes in v1:
time: 1070 us; the launch traced here: 1050 us
  Pallas kernels  499 us (47%)
  waiting for transfers between devices  335 us (31%)
  starting transfers between devices  175 us (16%)
  local copies, waits for them, and re-layouts  18.3 us (2%)
  other arithmetic  17.6 us (2%)
    pallas_call x9, Pallas kernels, rows_call(): pl.pallas_call(kernel, grid_spec=pltpu.PrefetchScalarGridSpec(num_scalar_...  375 us
    ppermute x21, waiting for transfers between devices, permute(): return [lax.ppermute(v, dev_axes, pairs) for v in values]  225 us
    ppermute x27, starting transfers between devices, exchange(): out.append(lax.ppermute(parts[s], dev_axes, pairs[s]))  126 us
    ppermute x27, waiting for transfers between devices, exchange(): out.append(lax.ppermute(parts[s], dev_axes, pairs[s]))  101 us
    ppermute x21, starting transfers between devices, permute(): return [lax.ppermute(v, dev_axes, pairs) for v in values]  32.6 us
    pallas_call x1, Pallas kernels, layer(): y_combine(order, base, my_kept, *y_recv, after(info, g_own[0]), hidden, d...  27.7 us
    pallas_call x1, Pallas kernels, layer(): info, prob_sum, *c_send = c_slots(order, base, ids_t, hidden, d_out, wr3)  27.5 us
  transfers between devices with their start and end apart: 60, of which 18 were waited for; matrix products, arithmetic and copies ran while one was open for 3% of the time, Pallas kernels for 37%

profile of v1, /device:TPU:0, one launch (start us, length us, event | category | flops | bytes accessed | tf_op | source)
XLA Modules:
  0.0 1049.5 jit_solution(9596621658117678187)
XLA Ops:
  0.6 3.2 collective-permute-start.8
  14.3 13.1 %shard_map.144 = (s32[8,128]{1,0:T(8,128)}, bf16[896,768]{1,0:T(8,128)(2,1)}, bf16[896,768]{1,0:T(8,128)(2,1)}, bf16[896,768]{1,0:T(8,128)(2,1)}, bf16[896,768]{1,0:T(8,128)(2,1)}) custom-call(s32[5]{0:T(128)} %concatenate.53.order_ref, s32[2,2048]{1,0:T(2,128)} %bitcast.65, bf16[2048,768]{1,0:T(8,128)(2,1)} %refs_9_.1), custom_call_target="tpu_custom_call" | custom-call | flops 3422552064 | bytes 5505024 | tf_op jit(solution)/shard_map/pallas_call | solution.py:568
  31.7 27.5 %shard_map.148 = (f32[2048,128]{1,0:T(8,128)}, f32[8,128]{1,0:T(8,128)}, bf16[896,768]{1,0:T(8,128)(2,1)}, bf16[896,768]{1,0:T(8,128)(2,1)}, bf16[896,768]{1,0:T...) custom-call(s32[8]{0:T(128)} %stack.62.order_ref, ...), custom_call_target="tpu_custom_call" | custom-call | flops 6845104128 | bytes 11010048 | tf_op jit(solution)/shard_map/pallas_call | solution.py:602
  63.7 3.4 dynamic-slice_bitcast_fusion
  69.3 6.8 collective-permute-done.9.h_ref
  76.1 13.1 %shard_map.146 = (s32[8,128]{1,0:T(8,128)}, bf16[896,768]{1,0:T(8,128)(2,1)}, bf16[896,768]{1,0:T(8,128)(2,1)}, bf16[896,768]{1,0:T(8,128)(2,1)}, bf16[896,768]{1,0:T(8,128)(2,1)}) custom-call(s32[5]{0:T(128)} %concatenate.53.order_ref, s32[2,2048]{1,0:T(2,128)} %copy-done.21, bf16[2048,768]{1,0:T(8,128)(2,1)} %collective-permute-done.9.h_ref), custom_call_target="tpu_custom_call" | custom-call | flops 3422552064 | bytes 5505024 | tf_op jit(solution)/shard_map/pallas_call | solution.py:569
  95.5 24.2 %collective-permute-done.19.refs_1_ = bf16[896,768]{1,0:T(8,128)(2,1)} collective-permute-done((bf16[896,768]{1,0:T(8,128)(2,1)}, bf16[896,768]{1,0:T(8,128)(2,1)}, u32[]{:S(2)}, u32[]{:S(2)}) %collective-permute-start.19) | collective-permute-done | bytes 1376288 | tf_op jit(solution)/shard_map/ppermute | solution.py:518
  119.7 3.8 dynamic-slice_bitcast_fusion.2
  130.8 18.4 %collective-permute-done.10.refs_5_ = bf16[896,768]{1,0:T(8,128)(2,1)} collective-permute-done((bf16[896,768]{1,0:T(8,128)(2,1)}, bf16[896,768]{1,0:T(8,128)(2,1)}, u32[]{:S(2)}, u32[]{:S(2)}) %collective-permute-start.10) | collective-permute-done | bytes 1376288 | tf_op jit(solution)/shard_map/ppermute | solution.py:518
  152.9 33.7 %shard_map.147 = (f32[7168,1024]{1,0:T(8,128)}, f32[7168,1024]{1,0:T(8,128)}, f32[7168,768]{1,0:T(8,128)}, bf16[7680,768]{1,0:T(8,128)(2,1)}) custom-call(s32[1]{0:T(128)S(6)} %select_n.119.n_ref, s32[9]{0:T(128)} %pad_add_fusion.1.offset_s, s32[8]{0:T(128)} %copy-done.13, bf16[896,768]{1,0:T(8,128)(2,1)} %get-tuple-element.93.refs_0_, ...), custom_call_target="tpu_custom_call" | custom-call | flops 33822867456 | bytes 110100480 | tf_op jit(solution)/shard_map/pallas_call | solution.py:632
  186.6 9.3 collective-permute-start.24
  195.9 17.7 %collective-permute-done.23.refs_5_ = bf16[896,768]{1,0:T(8,128)(2,1)} collective-permute-done((bf16[896,768]{1,0:T(8,128)(2,1)}, bf16[896,768]{1,0:T(8,128)(2,1)}, u32[]{:S(2)}, u32[]{:S(2)}) %collective-permute-start.23) | collective-permute-done | bytes 1376288 | tf_op jit(solution)/shard_map/ppermute | solution.py:518
  217.1 31.5 %shard_map.149 = (f32[7168,1024]{1,0:T(8,128)}, f32[7168,1024]{1,0:T(8,128)}, f32[7168,768]{1,0:T(8,128)}) custom-call(s32[1]{0:T(128)S(6)} %select_n.119.n_ref, s32[9]{0:T(128)} %pad_add_fusion.1.offset_s, bf16[7680,768]{1,0:T(8,128)(2,1)} %get-tuple-element.101.x_ref.refs_8_, ...), custom_call_target="tpu_custom_call", output_to_operand_aliasing={{2}: (6, {})} | custom-call | flops 33822867456 | bytes 110100480 | tf_op jit(solution)/shard_map/pallas_call | solution.py:632
  248.7 3.5 collective-permute-start.26
  252.2 29.9 %collective-permute-done.14.w3_ref = bf16[768,1024]{1,0:T(8,128)(2,1)} collective-permute-done((bf16[768,1024]{1,0:T(8,128)(2,1)}, bf16[768,1024]{1,0:T(8,128)(2,1)}, u32[]{:S(2)}, u32[]{:S(2)}) %collective-permute-start.14) | collective-permute-done | bytes 1572896 | tf_op jit(solution)/shard_map/ppermute | solution.py:513
  282.1 33.7 %collective-permute-done.15.w2_ref = bf16[1024,768]{1,0:T(8,128)(2,1)} collective-permute-done((bf16[1024,768]{1,0:T(8,128)(2,1)}, bf16[1024,768]{1,0:T(8,128)(2,1)}, u32[]{:S(2)}, u32[]{:S(2)}) %collective-permute-start.15) | collective-permute-done | bytes 1572896 | tf_op jit(solution)/shard_map/ppermute | solution.py:513
  315.8 35.4 %shard_map.150 = (f32[768,512]{1,0:T(8,128)}, f32[768,512]{1,0:T(8,128)}, f32[512,768]{1,0:T(8,128)}, f32[7168,768]{1,0:T(8,128)}, bf16[7680,768]{1,0:T(8,128)(2,1)}) custom-call(s32[1]{0:T(128)S(6)} %select_n.119.n_ref, s32[9]{0:T(128)} %pad_add_fusion.1.offset_s, s32[8]{0:T(128)} %copy-done.13, bf16[896,768]{1,0:T(8,128)(2,1)} %get-tuple-element.105.refs_0_, ...), custom_call_target="tpu_custom_call" | custom-call | flops 33822867456 | bytes 110100480 | tf_op jit(solution)/shard_map/pallas_call | solution.py:632
  351.2 32.0 %shard_map.151 = (f32[768,512]{1,0:T(8,128)}, f32[768,512]{1,0:T(8,128)}, f32[512,768]{1,0:T(8,128)}, f32[7168,768]{1,0:T(8,128)}) custom-call(s32[1]{0:T(128)S(6)} %select_n.119.n_ref, s32[9]{0:T(128)} %pad_add_fusion.1.offset_s, bf16[7680,768]{1,0:T(8,128)(2,1)} %get-tuple-element.101.x_ref.refs_8_, ...), custom_call_target="tpu_custom_call", output_to_operand_aliasing={{3}: (9, {})} | custom-call | flops 33822867456 | bytes 110100480 | tf_op jit(solution)/shard_map/pallas_call | solution.py:632
  383.2 73.0 %shard_map.152 = (f32[768,1024]{1,0:T(8,128)}, f32[768,1024]{1,0:T(8,128)}, f32[1024,768]{1,0:T(8,128)}, f32[7168,768]{1,0:T(8,128)}, f32[7168,768]{1,0:T(8,128)}) custom-call(s32[1]{0:T(128)S(6)} %select_n.119.n_ref, s32[9]{0:T(128)} %pad_add_fusion.1.offset_s, ...), custom_call_target="tpu_custom_call", output_to_operand_aliasing={{3}: (8, {}), {4}: (7, {})} | custom-call | flops 101468602368 | bytes 110100480 | tf_op jit(solution)/shard_map/pallas_call | solution.py:632
  456.2 34.2 %shard_map.153 = (f32[7168,1024]{1,0:T(8,128)}, f32[7168,1024]{1,0:T(8,128)}, bf16[896,768]{1,0:T(8,128)(2,1)}, bf16[896,768]{1,0:T(8,128)(2,1)}, bf16[896,768]{...) custom-call(s32[1]{0:T(128)S(6)} %select_n.119.n_ref, ...), custom_call_target="tpu_custom_call" | custom-call | flops 33822867456 | bytes 110100480 | tf_op jit(solution)/shard_map/pallas_call | solution.py:632
  490.5 19.5 %collective-permute-start.29 = (bf16[896,768]{1,0:T(8,128)(2,1)}, bf16[896,768]{1,0:T(8,128)(2,1)S(1)}, u32[]{:S(2)}, u32[]{:S(2)}) collective-permute-start(bf16[896,768]{1,0:T(8,128)(2,1)} %get-tuple-element.120), channel_id=1, source_target_pairs={{4,0},{9,1},{6,2},{11,3},{0,4},{13,5},{2,6},{15,7},{12,8},{1,9},{1... | collective-permute-start | bytes 4128776 | tf_op jit(solution)/shard_map/ppermute | solution.py:518
  510.1 26.9 %collective-permute-start.32 = (bf16[896,768]{1,0:T(8,128)(2,1)}, bf16[896,768]{1,0:T(8,128)(2,1)}, u32[]{:S(2)}, u32[]{:S(2)}) collective-permute-start(bf16[896,768]{1,0:T(8,128)(2,1)} %get-tuple-element.123), channel_id=1, source_target_pairs={{2,0},{3,1},{0,2},{1,3},{6,4},{7,5},{4,6},{5,7},{10,8},{11,9},{8,1... | collective-permute-start | bytes 4128776 | tf_op jit(solution)/shard_map/ppermute | solution.py:518
  538.4 55.2 %shard_map.154 = (f32[768,1024]{1,0:T(8,128)}, f32[768,1024]{1,0:T(8,128)}, f32[1024,768]{1,0:T(8,128)}, f32[7168,768]{1,0:T(8,128)}) custom-call(s32[1]{0:T(128)S(6)} %select_n.119.n_ref, s32[9]{0:T(128)} %pad_add_fusion.1.offset_s, bf16[7680,768]{1,0:T(8,128)(2,1)} %get-tuple-element.101.x_ref.refs_8_, ...), custom_call_target="tpu_custom_call", output_to_operand_aliasing={{3}: (9, {})} | custom-call | flops 67645734912 | bytes 110100480 | tf_op jit(solution)/shard_map/pallas_call | solution.py:632
  593.6 38.8 %shard_map.155 = (bf16[896,768]{1,0:T(8,128)(2,1)}, bf16[896,768]{1,0:T(8,128)(2,1)}, bf16[896,768]{1,0:T(8,128)(2,1)}, bf16[896,768]{1,0:T(8,128)(2,1)}, bf16[8...) custom-call(s32[1]{0:T(128)S(6)} %select_n.119.n_ref, ...), custom_call_target="tpu_custom_call" | custom-call | flops 33822867456 | bytes 110100480 | tf_op jit(solution)/shard_map/pallas_call | solution.py:632
  632.5 27.5 %collective-permute-start.34 = (bf16[896,768]{1,0:T(8,128)(2,1)}, bf16[896,768]{1,0:T(8,128)(2,1)}, u32[]{:S(2)}, u32[]{:S(2)}) collective-permute-start(bf16[896,768]{1,0:T(8,128)(2,1)} %get-tuple-element.125), channel_id=1, source_target_pairs={{3,0},{2,1},{1,2},{0,3},{7,4},{6,5},{5,6},{4,7},{11,8},{10,9},{9,1... | collective-permute-start | bytes 4128776 | tf_op jit(solution)/shard_map/ppermute | solution.py:518
  662.1 41.3 %shard_map.156 = (f32[768,1024]{1,0:T(8,128)}, f32[768,1024]{1,0:T(8,128)}, f32[1024,768]{1,0:T(8,128)}) custom-call(s32[1]{0:T(128)S(6)} %select_n.119.n_ref, s32[9]{0:T(128)} %pad_add_fusion.1.offset_s, bf16[7680,768]{1,0:T(8,128)(2,1)} %get-tuple-element.101.x_ref.refs_8_, bf16[7680,768]{1,0:T(8,128)(2,1)} %get-tuple-element.115.c_ref, ...), custom_call_target="tpu_custom_call" | custom-call | flops 45097156608 | bytes 110100480 | tf_op jit(solution)/shard_map/pallas_call | solution.py:632
  703.4 4.4 collective-permute-start.56
  707.9 11.9 %collective-permute-start.40 = (bf16[896,768]{1,0:T(8,128)(2,1)}, bf16[896,768]{1,0:T(8,128)(2,1)}, u32[]{:S(2)}, u32[]{:S(2)}) collective-permute-start(bf16[896,768]{1,0:T(8,128)(2,1)} %get-tuple-element.144), channel_id=1, source_target_pairs={{6,0},{11,1},{4,2},{9,3},{2,4},{15,5},{0,6},{13,7},{14,8},{3,9},{1... | collective-permute-start | bytes 4128776 | tf_op jit(solution)/shard_map/ppermute | solution.py:518
  719.8 27.7 %shard_map.157 = (bf16[2048,768]{1,0:T(8,128)(2,1)}, bf16[2048,128]{1,0:T(8,128)(2,1)}, f32[128,768]{1,0:T(8,128)}) custom-call(s32[8]{0:T(128)} %stack.62.order_ref, s32[8,128]{1,0:T(8,128)} %get-tuple-element.92.base_s, s32[8]{0:T(128)} %fusion.2.kept_s, bf16[896,768]{1,0:T(8,128)(2,1)} %get-tuple-element.119.refs_0_, bf16[896,768]{1,0:T(8,128)(2,1)} %copy-done.20, ...), custom_call_target="tpu_custom_call" | custom-call | flops 13690208256 | bytes 22020096 | tf_op jit(solution)/shard_map/pallas_call | solution.py:732
  750.4 28.3 %collective-permute-done.40.refs_5_ = bf16[896,768]{1,0:T(8,128)(2,1)} collective-permute-done((bf16[896,768]{1,0:T(8,128)(2,1)}, bf16[896,768]{1,0:T(8,128)(2,1)}, u32[]{:S(2)}, u32[]{:S(2)}) %collective-permute-start.40) | collective-permute-done | bytes 1376288 | tf_op jit(solution)/shard_map/ppermute | solution.py:518
  781.9 77.2 %collective-permute-done.48.part_0_ref = f32[512,768]{1,0:T(8,128)S(1)} collective-permute-done((f32[512,768]{1,0:T(8,128)}, f32[512,768]{1,0:T(8,128)S(1)}, u32[]{:S(2)}, u32[]{:S(2)}) %collective-permute-start.48) | collective-permute-done | bytes 1572896 | tf_op jit(solution)/shard_map/ppermute | solution.py:513
  861.2 14.8 %collective-permute-done.47.part_1_ref = f32[768,512]{1,0:T(8,128)S(1)} collective-permute-done((f32[768,512]{1,0:T(8,128)}, f32[768,512]{1,0:T(8,128)S(1)}, u32[]{:S(2)}, u32[]{:S(2)}) %collective-permute-start.47) | collective-permute-done | bytes 1572896 | tf_op jit(solution)/shard_map/ppermute | solution.py:513
  878.1 5.6 add.261
  891.7 7.5 collective-permute-done.46.part_0_ref
  899.2 5.5 collective-permute-start.53
  904.7 28.2 %collective-permute-done.45.part_1_ref = f32[768,512]{1,0:T(8,128)} collective-permute-done((f32[768,512]{1,0:T(8,128)}, f32[768,512]{1,0:T(8,128)}, u32[]{:S(2)}, u32[]{:S(2)}) %collective-permute-start.45) | collective-permute-done | bytes 1572896 | tf_op jit(solution)/shard_map/ppermute | solution.py:513
  932.9 9.3 collective-permute-start.41
  942.2 24.4 %collective-permute-done.44.part_0_ref = f32[768,512]{1,0:T(8,128)} collective-permute-done((f32[768,512]{1,0:T(8,128)}, f32[768,512]{1,0:T(8,128)}, u32[]{:S(2)}, u32[]{:S(2)}) %collective-permute-start.44) | collective-permute-done | bytes 1572896 | tf_op jit(solution)/shard_map/ppermute | solution.py:513
  966.6 8.3 collective-permute-start.42
  976.7 4.2 shard_map.160._
  980.9 4.2 shard_map.159._
  985.1 4.2 shard_map.158._
  989.3 10.2 collective-permute-done.42.refs_7_
  999.5 19.0 %shard_map.161 = bf16[2048,768]{1,0:T(8,128)(2,1)} custom-call(s32[8]{0:T(128)} %stack.62.order_ref, s32[8,128]{1,0:T(8,128)} %get-tuple-element.92.base_s, s32[8]{0:T(128)} %fusion.2.kept_s, bf16[896,768]{1,0:T(8,128)(2,1)} %get-tuple-element.135.refs_0_, bf16[896,768]{1,0:T(8,128)(2,1)} %collective-permute-done.36.refs_1_, ...), custom_call_target="tpu_custom_call" | custom-call | flops 6845104128 | bytes 22020096 | tf_op jit(solution)/shard_map/pallas_call | solution.py:765
  1018.6 6.1 collective-permute-start.51
  1029.3 3.2 shard_map.163
  1032.5 9.5 collective-permute-done.53.other_ref
  1042.0 3.2 shard_map.164
  (188 shorter events, 72.4 us)
Async XLA Ops:
  0.6 61.8 %collective-permute-start.8 = (s32[2,2048]{1,0:T(2,128)}, s32[2,2048]{1,0:T(2,128)S(1)}, u32[]{:S(2)}, u32[]{:S(2)}) collective-permute-start(s32[2,2048]{1,0:T(2,128)} %bitcast.63), channel_id=1, source_target_pairs={{0,2},{1,3},{2,0},{3,1},{4,6},{5,7},{6,4},{7,5},{8,10},{9,11},{10,... | collective-permute-start | bytes 49160 | tf_op jit(solution)/shard_map/ppermute | solution.py:548
  6.2 69.9 %collective-permute-start.9 = (bf16[2048,768]{1,0:T(8,128)(2,1)}, bf16[2048,768]{1,0:T(8,128)(2,1)}, u32[]{:S(2)}, u32[]{:S(2)}) collective-permute-start(bf16[2048,768]{1,0:T(8,128)(2,1)} %refs_9_.1), channel_id=1, source_target_pairs={{0,2},{1,3},{2,0},{3,1},{4,6},{5,7},{6,4},{7,5},{8,10},{9,11},{10,... | collective-permute-start | bytes 9437192 | tf_op jit(solution)/shard_map/ppermute | solution.py:548
  59.2 32.4 %collective-permute-start.5 = (bf16[896,768]{1,0:T(8,128)(2,1)}, bf16[896,768]{1,0:T(8,128)(2,1)}, u32[]{:S(2)}, u32[]{:S(2)}) collective-permute-start(bf16[896,768]{1,0:T(8,128)(2,1)} %get-tuple-element.94), channel_id=1, source_target_pairs={{0,4},{1,9},{2,6},{3,11},{4,0},{5,13},{6,2},{7,15},{8,12},{9,1},{1... | collective-permute-start | bytes 4128776 | tf_op jit(solution)/shard_map/ppermute | solution.py:518
  60.8 33.3 %collective-permute-start.7 = (bf16[896,768]{1,0:T(8,128)(2,1)}, bf16[896,768]{1,0:T(8,128)(2,1)}, u32[]{:S(2)}, u32[]{:S(2)}) collective-permute-start(bf16[896,768]{1,0:T(8,128)(2,1)} %get-tuple-element.96), channel_id=1, source_target_pairs={{0,9},{1,4},{2,11},{3,6},{4,13},{5,0},{6,15},{7,2},{8,1},{9,12},{1... | collective-permute-start | bytes 4128776 | tf_op jit(solution)/shard_map/ppermute | solution.py:518
  62.4 57.3 %collective-permute-start.19 = (bf16[896,768]{1,0:T(8,128)(2,1)}, bf16[896,768]{1,0:T(8,128)(2,1)}, u32[]{:S(2)}, u32[]{:S(2)}) collective-permute-start(bf16[896,768]{1,0:T(8,128)(2,1)} %get-tuple-element.106), channel_id=1, source_target_pairs={{0,4},{1,9},{2,6},{3,11},{4,0},{5,13},{6,2},{7,15},{8,12},{9,1},{1... | collective-permute-start | bytes 4128776 | tf_op jit(solution)/shard_map/ppermute | solution.py:518
  89.3 38.9 %collective-permute-start.20 = (bf16[896,768]{1,0:T(8,128)(2,1)}, bf16[896,768]{1,0:T(8,128)(2,1)S(1)}, u32[]{:S(2)}, u32[]{:S(2)}) collective-permute-start(bf16[896,768]{1,0:T(8,128)(2,1)} %get-tuple-element.107), channel_id=1, source_target_pairs={{0,1},{1,0},{2,3},{3,2},{4,5},{5,4},{6,7},{7,6},{8,9},{9,8},{10,11... | collective-permute-start | bytes 4128776 | tf_op jit(solution)/shard_map/ppermute | solution.py:518
  91.6 38.1 %collective-permute-start.21 = (bf16[896,768]{1,0:T(8,128)(2,1)}, bf16[896,768]{1,0:T(8,128)(2,1)}, u32[]{:S(2)}, u32[]{:S(2)}) collective-permute-start(bf16[896,768]{1,0:T(8,128)(2,1)} %get-tuple-element.108), channel_id=1, source_target_pairs={{0,9},{1,4},{2,11},{3,6},{4,13},{5,0},{6,15},{7,2},{8,1},{9,12},{1... | collective-permute-start | bytes 4128776 | tf_op jit(solution)/shard_map/ppermute | solution.py:518
  91.6 57.6 %collective-permute-start.10 = (bf16[896,768]{1,0:T(8,128)(2,1)}, bf16[896,768]{1,0:T(8,128)(2,1)}, u32[]{:S(2)}, u32[]{:S(2)}) collective-permute-start(bf16[896,768]{1,0:T(8,128)(2,1)} %get-tuple-element.98), channel_id=1, source_target_pairs={{0,4},{1,9},{2,6},{3,11},{4,0},{5,13},{6,2},{7,15},{8,12},{9,1},{1... | collective-permute-start | bytes 4128776 | tf_op jit(solution)/shard_map/ppermute | solution.py:518
  94.1 56.7 %collective-permute-start.11 = (bf16[896,768]{1,0:T(8,128)(2,1)}, bf16[896,768]{1,0:T(8,128)(2,1)}, u32[]{:S(2)}, u32[]{:S(2)}) collective-permute-start(bf16[896,768]{1,0:T(8,128)(2,1)} %get-tuple-element.99), channel_id=1, source_target_pairs={{0,1},{1,0},{2,3},{3,2},{4,5},{5,4},{6,7},{7,6},{8,9},{9,8},{10,11... | collective-permute-start | bytes 4128776 | tf_op jit(solution)/shard_map/ppermute | solution.py:518
  128.1 85.5 %collective-permute-start.18 = (bf16[1024,768]{1,0:T(8,128)(2,1)S(1)}, bf16[1024,768]{1,0:T(8,128)(2,1)}, u32[]{:S(2)}, u32[]{:S(2)}) collective-permute-start(bf16[1024,768]{1,0:T(8,128)(2,1)S(1)} %get-tuple-element.188.refs_10_.w2_ref), channel_id=1, source_target_pairs={{0,8},{1,5},{2,10},{3,7},{4,12},{5,1},{6,14},{7,3},{8,0},{9,13},{1... | collective-permute-start | bytes 4718600 | tf_op jit(solution)/shard_map/ppermute | solution.py:513
  129.7 85.4 %collective-permute-start.16 = (bf16[768,1024]{1,0:T(8,128)(2,1)}, bf16[768,1024]{1,0:T(8,128)(2,1)}, u32[]{:S(2)}, u32[]{:S(2)}) collective-permute-start(bf16[768,1024]{1,0:T(8,128)(2,1)} %get-tuple-element.192.refs_8_.w1_ref), channel_id=1, source_target_pairs={{0,8},{1,5},{2,10},{3,7},{4,12},{5,1},{6,14},{7,3},{8,0},{9,13},{1... | collective-permute-start | bytes 4718600 | tf_op jit(solution)/shard_map/ppermute | solution.py:513
  149.2 66.4 %collective-permute-start.17 = (bf16[768,1024]{1,0:T(8,128)(2,1)}, bf16[768,1024]{1,0:T(8,128)(2,1)}, u32[]{:S(2)}, u32[]{:S(2)}) collective-permute-start(bf16[768,1024]{1,0:T(8,128)(2,1)} %get-tuple-element.190.refs_9_.w3_ref), channel_id=1, source_target_pairs={{0,8},{1,5},{2,10},{3,7},{4,12},{5,1},{6,14},{7,3},{8,0},{9,13},{1... | collective-permute-start | bytes 4718600 | tf_op jit(solution)/shard_map/ppermute | solution.py:513
  150.8 35.8 %collective-permute-start.22 = (bf16[896,768]{1,0:T(8,128)(2,1)}, bf16[896,768]{1,0:T(8,128)(2,1)}, u32[]{:S(2)}, u32[]{:S(2)}) collective-permute-start(bf16[896,768]{1,0:T(8,128)(2,1)} %get-tuple-element.109), channel_id=1, source_target_pairs={{0,2},{1,3},{2,0},{3,1},{4,6},{5,7},{6,4},{7,5},{8,10},{9,11},{10,... | collective-permute-start | bytes 4128776 | tf_op jit(solution)/shard_map/ppermute | solution.py:518
  151.5 62.1 %collective-permute-start.23 = (bf16[896,768]{1,0:T(8,128)(2,1)}, bf16[896,768]{1,0:T(8,128)(2,1)}, u32[]{:S(2)}, u32[]{:S(2)}) collective-permute-start(bf16[896,768]{1,0:T(8,128)(2,1)} %get-tuple-element.110), channel_id=1, source_target_pairs={{0,6},{1,11},{2,4},{3,9},{4,2},{5,15},{6,0},{7,13},{8,14},{9,3},{1... | collective-permute-start | bytes 4128776 | tf_op jit(solution)/shard_map/ppermute | solution.py:518
  186.6 129.2 %collective-permute-start.24 = (bf16[896,768]{1,0:T(8,128)(2,1)}, bf16[896,768]{1,0:T(8,128)(2,1)}, u32[]{:S(2)}, u32[]{:S(2)}) collective-permute-start(bf16[896,768]{1,0:T(8,128)(2,1)} %get-tuple-element.111), channel_id=1, source_target_pairs={{0,3},{1,2},{2,1},{3,0},{4,7},{5,6},{6,5},{7,4},{8,11},{9,10},{10,... | collective-permute-start | bytes 4128776 | tf_op jit(solution)/shard_map/ppermute | solution.py:518
  213.6 102.2 %collective-permute-start.25 = (bf16[896,768]{1,0:T(8,128)(2,1)}, bf16[896,768]{1,0:T(8,128)(2,1)}, u32[]{:S(2)}, u32[]{:S(2)}) collective-permute-start(bf16[896,768]{1,0:T(8,128)(2,1)} %get-tuple-element.112), channel_id=1, source_target_pairs={{0,11},{1,6},{2,9},{3,4},{4,15},{5,2},{6,13},{7,0},{8,3},{9,14},{1... | collective-permute-start | bytes 4128776 | tf_op jit(solution)/shard_map/ppermute | solution.py:518
  213.6 35.0 %collective-permute-start.13 = (bf16[768,1024]{1,0:T(8,128)(2,1)}, bf16[768,1024]{1,0:T(8,128)(2,1)S(1)}, u32[]{:S(2)}, u32[]{:S(2)}) collective-permute-start(bf16[768,1024]{1,0:T(8,128)(2,1)} %get-tuple-element.191), channel_id=1, source_target_pairs={{0,4},{1,9},{2,6},{3,11},{4,0},{5,13},{6,2},{7,15},{8,12},{9,1},{1... | collective-permute-start | bytes 4718600 | tf_op jit(solution)/shard_map/ppermute | solution.py:513
  215.1 66.9 %collective-permute-start.14 = (bf16[768,1024]{1,0:T(8,128)(2,1)}, bf16[768,1024]{1,0:T(8,128)(2,1)}, u32[]{:S(2)}, u32[]{:S(2)}) collective-permute-start(bf16[768,1024]{1,0:T(8,128)(2,1)} %get-tuple-element.189), channel_id=1, source_target_pairs={{0,4},{1,9},{2,6},{3,11},{4,0},{5,13},{6,2},{7,15},{8,12},{9,1},{1... | collective-permute-start | bytes 4718600 | tf_op jit(solution)/shard_map/ppermute | solution.py:513
  215.7 100.1 %collective-permute-start.15 = (bf16[1024,768]{1,0:T(8,128)(2,1)}, bf16[1024,768]{1,0:T(8,128)(2,1)}, u32[]{:S(2)}, u32[]{:S(2)}) collective-permute-start(bf16[1024,768]{1,0:T(8,128)(2,1)} %get-tuple-element.187), channel_id=1, source_target_pairs={{0,4},{1,9},{2,6},{3,11},{4,0},{5,13},{6,2},{7,15},{8,12},{9,1},{1... | collective-permute-start | bytes 4718600 | tf_op jit(solution)/shard_map/ppermute | solution.py:513
  248.7 134.5 %collective-permute-start.26 = (bf16[768,1024]{1,0:T(8,128)(2,1)S(1)}, bf16[768,1024]{1,0:T(8,128)(2,1)}, u32[]{:S(2)}, u32[]{:S(2)}) collective-permute-start(bf16[768,1024]{1,0:T(8,128)(2,1)S(1)} %collective-permute-done.13.w1_ref), channel_id=1, source_target_pairs={{0,8},{1,5},{2,10},{3,7},{4,12},{5,1},{6,14},{7,3},{8,0},{9,13},{1... | collective-permute-start | bytes 4718600 | tf_op jit(solution)/shard_map/ppermute | solution.py:513
  282.1 101.1 %collective-permute-start.27 = (bf16[768,1024]{1,0:T(8,128)(2,1)}, bf16[768,1024]{1,0:T(8,128)(2,1)}, u32[]{:S(2)}, u32[]{:S(2)}) collective-permute-start(bf16[768,1024]{1,0:T(8,128)(2,1)} %collective-permute-done.14.w3_ref), channel_id=1, source_target_pairs={{0,8},{1,5},{2,10},{3,7},{4,12},{5,1},{6,14},{7,3},{8,0},{9,13},{1... | collective-permute-start | bytes 4718600 | tf_op jit(solution)/shard_map/ppermute | solution.py:513
  315.8 67.4 %collective-permute-start.28 = (bf16[1024,768]{1,0:T(8,128)(2,1)}, bf16[1024,768]{1,0:T(8,128)(2,1)}, u32[]{:S(2)}, u32[]{:S(2)}) collective-permute-start(bf16[1024,768]{1,0:T(8,128)(2,1)} %collective-permute-done.15.w2_ref), channel_id=1, source_target_pairs={{0,8},{1,5},{2,10},{3,7},{4,12},{5,1},{6,14},{7,3},{8,0},{9,13},{1... | collective-permute-start | bytes 4718600 | tf_op jit(solution)/shard_map/ppermute | solution.py:513
  490.5 142.0 %collective-permute-start.29 = (bf16[896,768]{1,0:T(8,128)(2,1)}, bf16[896,768]{1,0:T(8,128)(2,1)S(1)}, u32[]{:S(2)}, u32[]{:S(2)}) collective-permute-start(bf16[896,768]{1,0:T(8,128)(2,1)} %get-tuple-element.120), channel_id=1, source_target_pairs={{4,0},{9,1},{6,2},{11,3},{0,4},{13,5},{2,6},{15,7},{12,8},{1,9},{1... | collective-permute-start | bytes 4128776 | tf_op jit(solution)/shard_map/ppermute | solution.py:518
  509.9 150.0 %collective-permute-start.30 = (bf16[896,768]{1,0:T(8,128)(2,1)}, bf16[896,768]{1,0:T(8,128)(2,1)}, u32[]{:S(2)}, u32[]{:S(2)}) collective-permute-start(bf16[896,768]{1,0:T(8,128)(2,1)} %get-tuple-element.121), channel_id=1, source_target_pairs={{1,0},{0,1},{3,2},{2,3},{5,4},{4,5},{7,6},{6,7},{9,8},{8,9},{11,10... | collective-permute-start | bytes 4128776 | tf_op jit(solution)/shard_map/ppermute | solution.py:518
  509.9 150.0 %collective-permute-start.31 = (bf16[896,768]{1,0:T(8,128)(2,1)}, bf16[896,768]{1,0:T(8,128)(2,1)}, u32[]{:S(2)}, u32[]{:S(2)}) collective-permute-start(bf16[896,768]{1,0:T(8,128)(2,1)} %get-tuple-element.122), channel_id=1, source_target_pairs={{9,0},{4,1},{11,2},{6,3},{13,4},{0,5},{15,6},{2,7},{1,8},{12,9},{3... | collective-permute-start | bytes 4128776 | tf_op jit(solution)/shard_map/ppermute | solution.py:518
  510.1 151.4 %collective-permute-start.32 = (bf16[896,768]{1,0:T(8,128)(2,1)}, bf16[896,768]{1,0:T(8,128)(2,1)}, u32[]{:S(2)}, u32[]{:S(2)}) collective-permute-start(bf16[896,768]{1,0:T(8,128)(2,1)} %get-tuple-element.123), channel_id=1, source_target_pairs={{2,0},{3,1},{0,2},{1,3},{6,4},{7,5},{4,6},{5,7},{10,8},{11,9},{8,1... | collective-permute-start | bytes 4128776 | tf_op jit(solution)/shard_map/ppermute | solution.py:518
  537.0 124.5 %collective-permute-start.33 = (bf16[896,768]{1,0:T(8,128)(2,1)}, bf16[896,768]{1,0:T(8,128)(2,1)}, u32[]{:S(2)}, u32[]{:S(2)}) collective-permute-start(bf16[896,768]{1,0:T(8,128)(2,1)} %get-tuple-element.124), channel_id=1, source_target_pairs={{6,0},{11,1},{4,2},{9,3},{2,4},{15,5},{0,6},{13,7},{14,8},{3,9},{1... | collective-permute-start | bytes 4128776 | tf_op jit(solution)/shard_map/ppermute | solution.py:518
  632.5 71.0 %collective-permute-start.34 = (bf16[896,768]{1,0:T(8,128)(2,1)}, bf16[896,768]{1,0:T(8,128)(2,1)}, u32[]{:S(2)}, u32[]{:S(2)}) collective-permute-start(bf16[896,768]{1,0:T(8,128)(2,1)} %get-tuple-element.125), channel_id=1, source_target_pairs={{3,0},{2,1},{1,2},{0,3},{7,4},{6,5},{5,6},{4,7},{11,8},{10,9},{9,1... | collective-permute-start | bytes 4128776 | tf_op jit(solution)/shard_map/ppermute | solution.py:518
  659.9 47.9 %collective-permute-start.35 = (bf16[896,768]{1,0:T(8,128)(2,1)}, bf16[896,768]{1,0:T(8,128)(2,1)}, u32[]{:S(2)}, u32[]{:S(2)}) collective-permute-start(bf16[896,768]{1,0:T(8,128)(2,1)} %get-tuple-element.126), channel_id=1, source_target_pairs={{11,0},{6,1},{9,2},{4,3},{15,4},{2,5},{13,6},{0,7},{3,8},{14,9},{1... | collective-permute-start | bytes 4128776 | tf_op jit(solution)/shard_map/ppermute | solution.py:518
  659.9 47.9 %collective-permute-start.36 = (bf16[896,768]{1,0:T(8,128)(2,1)}, bf16[896,768]{1,0:T(8,128)(2,1)}, u32[]{:S(2)}, u32[]{:S(2)}) collective-permute-start(bf16[896,768]{1,0:T(8,128)(2,1)} %get-tuple-element.140), channel_id=1, source_target_pairs={{4,0},{9,1},{6,2},{11,3},{0,4},{13,5},{2,6},{15,7},{12,8},{1,9},{1... | collective-permute-start | bytes 4128776 | tf_op jit(solution)/shard_map/ppermute | solution.py:518
  661.5 46.4 %collective-permute-start.37 = (bf16[896,768]{1,0:T(8,128)(2,1)}, bf16[896,768]{1,0:T(8,128)(2,1)}, u32[]{:S(2)}, u32[]{:S(2)}) collective-permute-start(bf16[896,768]{1,0:T(8,128)(2,1)} %get-tuple-element.141), channel_id=1, source_target_pairs={{1,0},{0,1},{3,2},{2,3},{5,4},{4,5},{7,6},{6,7},{9,8},{8,9},{11,10... | collective-permute-start | bytes 4128776 | tf_op jit(solution)/shard_map/ppermute | solution.py:518
  661.5 86.0 %collective-permute-start.38 = (bf16[896,768]{1,0:T(8,128)(2,1)}, bf16[896,768]{1,0:T(8,128)(2,1)}, u32[]{:S(2)}, u32[]{:S(2)}) collective-permute-start(bf16[896,768]{1,0:T(8,128)(2,1)} %get-tuple-element.142), channel_id=1, source_target_pairs={{9,0},{4,1},{11,2},{6,3},{13,4},{0,5},{15,6},{2,7},{1,8},{12,9},{3... | collective-permute-start | bytes 4128776 | tf_op jit(solution)/shard_map/ppermute | solution.py:518
  703.4 174.6 %collective-permute-start.56 = (f32[768,1024]{1,0:T(8,128)}, f32[768,1024]{1,0:T(8,128)}, u32[]{:S(2)}, u32[]{:S(2)}) collective-permute-start(f32[768,1024]{1,0:T(8,128)} %get-tuple-element.170), channel_id=1, source_target_pairs={{0,8},{1,5},{2,10},{3,7},{4,12},{5,1},{6,14},{7,3},{8,0},{9,13},{1... | collective-permute-start | bytes 9437192 | tf_op jit(solution)/shard_map/ppermute | solution.py:513
  707.8 72.1 %collective-permute-start.49 = (f32[512,768]{1,0:T(8,128)}, f32[512,768]{1,0:T(8,128)S(1)}, u32[]{:S(2)}, u32[]{:S(2)}) collective-permute-start(f32[512,768]{1,0:T(8,128)} %get-tuple-element.159), channel_id=1, source_target_pairs={{0,8},{1,5},{2,10},{3,7},{4,12},{5,1},{6,14},{7,3},{8,0},{9,13},{1... | collective-permute-start | bytes 4718600 | tf_op jit(solution)/shard_map/ppermute | solution.py:513
  707.9 40.4 %collective-permute-start.39 = (bf16[896,768]{1,0:T(8,128)(2,1)}, bf16[896,768]{1,0:T(8,128)(2,1)}, u32[]{:S(2)}, u32[]{:S(2)}) collective-permute-start(bf16[896,768]{1,0:T(8,128)(2,1)} %get-tuple-element.143), channel_id=1, source_target_pairs={{2,0},{3,1},{0,2},{1,3},{6,4},{7,5},{4,6},{5,7},{10,8},{11,9},{8,1... | collective-permute-start | bytes 4128776 | tf_op jit(solution)/shard_map/ppermute | solution.py:518
  707.9 70.8 %collective-permute-start.40 = (bf16[896,768]{1,0:T(8,128)(2,1)}, bf16[896,768]{1,0:T(8,128)(2,1)}, u32[]{:S(2)}, u32[]{:S(2)}) collective-permute-start(bf16[896,768]{1,0:T(8,128)(2,1)} %get-tuple-element.144), channel_id=1, source_target_pairs={{6,0},{11,1},{4,2},{9,3},{2,4},{15,5},{0,6},{13,7},{14,8},{3,9},{1... | collective-permute-start | bytes 4128776 | tf_op jit(solution)/shard_map/ppermute | solution.py:518
  747.5 136.2 %collective-permute-start.54 = (f32[768,1024]{1,0:T(8,128)}, f32[768,1024]{1,0:T(8,128)S(1)}, u32[]{:S(2)}, u32[]{:S(2)}) collective-permute-start(f32[768,1024]{1,0:T(8,128)} %get-tuple-element.168), channel_id=1, source_target_pairs={{0,8},{1,5},{2,10},{3,7},{4,12},{5,1},{6,14},{7,3},{8,0},{9,13},{1... | collective-permute-start | bytes 9437192 | tf_op jit(solution)/shard_map/ppermute | solution.py:513
  748.3 141.1 %collective-permute-start.52 = (f32[1024,768]{1,0:T(8,128)}, f32[1024,768]{1,0:T(8,128)S(1)}, u32[]{:S(2)}, u32[]{:S(2)}) collective-permute-start(f32[1024,768]{1,0:T(8,128)} %get-tuple-element.165), channel_id=1, source_target_pairs={{0,8},{1,5},{2,10},{3,7},{4,12},{5,1},{6,14},{7,3},{8,0},{9,13},{1... | collective-permute-start | bytes 9437192 | tf_op jit(solution)/shard_map/ppermute | solution.py:513
  779.9 79.2 %collective-permute-start.48 = (f32[512,768]{1,0:T(8,128)}, f32[512,768]{1,0:T(8,128)S(1)}, u32[]{:S(2)}, u32[]{:S(2)}) collective-permute-start(f32[512,768]{1,0:T(8,128)} %get-tuple-element.158), channel_id=1, source_target_pairs={{0,8},{1,5},{2,10},{3,7},{4,12},{5,1},{6,14},{7,3},{8,0},{9,13},{1... | collective-permute-start | bytes 4718600 | tf_op jit(solution)/shard_map/ppermute | solution.py:513
  779.9 96.1 %collective-permute-start.47 = (f32[768,512]{1,0:T(8,128)}, f32[768,512]{1,0:T(8,128)S(1)}, u32[]{:S(2)}, u32[]{:S(2)}) collective-permute-start(f32[768,512]{1,0:T(8,128)} %get-tuple-element.155), channel_id=1, source_target_pairs={{0,8},{1,5},{2,10},{3,7},{4,12},{5,1},{6,14},{7,3},{8,0},{9,13},{1... | collective-permute-start | bytes 4718600 | tf_op jit(solution)/shard_map/ppermute | solution.py:513
  859.1 40.0 %collective-permute-start.46 = (f32[768,512]{1,0:T(8,128)}, f32[768,512]{1,0:T(8,128)}, u32[]{:S(2)}, u32[]{:S(2)}) collective-permute-start(f32[768,512]{1,0:T(8,128)} %get-tuple-element.154), channel_id=1, source_target_pairs={{0,8},{1,5},{2,10},{3,7},{4,12},{5,1},{6,14},{7,3},{8,0},{9,13},{1... | collective-permute-start | bytes 4718600 | tf_op jit(solution)/shard_map/ppermute | solution.py:513
  876.0 56.9 %collective-permute-start.45 = (f32[768,512]{1,0:T(8,128)}, f32[768,512]{1,0:T(8,128)}, u32[]{:S(2)}, u32[]{:S(2)}) collective-permute-start(f32[768,512]{1,0:T(8,128)} %get-tuple-element.151), channel_id=1, source_target_pairs={{0,8},{1,5},{2,10},{3,7},{4,12},{5,1},{6,14},{7,3},{8,0},{9,13},{1... | collective-permute-start | bytes 4718600 | tf_op jit(solution)/shard_map/ppermute | solution.py:513
  878.0 88.6 %collective-permute-start.44 = (f32[768,512]{1,0:T(8,128)}, f32[768,512]{1,0:T(8,128)}, u32[]{:S(2)}, u32[]{:S(2)}) collective-permute-start(f32[768,512]{1,0:T(8,128)} %get-tuple-element.150), channel_id=1, source_target_pairs={{0,8},{1,5},{2,10},{3,7},{4,12},{5,1},{6,14},{7,3},{8,0},{9,13},{1... | collective-permute-start | bytes 4718600 | tf_op jit(solution)/shard_map/ppermute | solution.py:513
  883.7 141.0 %collective-permute-start.57 = (f32[768,1024]{1,0:T(8,128)}, f32[768,1024]{1,0:T(8,128)}, u32[]{:S(2)}, u32[]{:S(2)}) collective-permute-start(f32[768,1024]{1,0:T(8,128)} %add.261), channel_id=1, source_target_pairs={{0,4},{1,9},{2,6},{3,11},{4,0},{5,13},{6,2},{7,15},{8,12},{9,1},{1... | collective-permute-start | bytes 9437192 | tf_op jit(solution)/shard_map/ppermute | solution.py:513
  889.5 139.9 %collective-permute-start.55 = (f32[768,1024]{1,0:T(8,128)}, f32[768,1024]{1,0:T(8,128)}, u32[]{:S(2)}, u32[]{:S(2)}) collective-permute-start(f32[768,1024]{1,0:T(8,128)} %add.260), channel_id=1, source_target_pairs={{0,4},{1,9},{2,6},{3,11},{4,0},{5,13},{6,2},{7,15},{8,12},{9,1},{1... | collective-permute-start | bytes 9437192 | tf_op jit(solution)/shard_map/ppermute | solution.py:513
  899.2 142.8 %collective-permute-start.53 = (f32[1024,768]{1,0:T(8,128)}, f32[1024,768]{1,0:T(8,128)}, u32[]{:S(2)}, u32[]{:S(2)}) collective-permute-start(f32[1024,768]{1,0:T(8,128)} %add.259), channel_id=1, source_target_pairs={{0,4},{1,9},{2,6},{3,11},{4,0},{5,13},{6,2},{7,15},{8,12},{9,1},{1... | collective-permute-start | bytes 9437192 | tf_op jit(solution)/shard_map/ppermute | solution.py:513
  932.9 56.4 %collective-permute-start.41 = (bf16[896,768]{1,0:T(8,128)(2,1)}, bf16[896,768]{1,0:T(8,128)(2,1)}, u32[]{:S(2)}, u32[]{:S(2)}) collective-permute-start(bf16[896,768]{1,0:T(8,128)(2,1)} %get-tuple-element.145), channel_id=1, source_target_pairs={{3,0},{2,1},{1,2},{0,3},{7,4},{6,5},{5,6},{4,7},{11,8},{10,9},{9,1... | collective-permute-start | bytes 4128776 | tf_op jit(solution)/shard_map/ppermute | solution.py:518
  966.6 33.0 %collective-permute-start.42 = (bf16[896,768]{1,0:T(8,128)(2,1)S(1)}, bf16[896,768]{1,0:T(8,128)(2,1)}, u32[]{:S(2)}, u32[]{:S(2)}) collective-permute-start(bf16[896,768]{1,0:T(8,128)(2,1)S(1)} %copy-done.19), channel_id=1, source_target_pairs={{11,0},{6,1},{9,2},{4,3},{15,4},{2,5},{13,6},{0,7},{3,8},{14,9},{1... | collective-permute-start | bytes 4128776 | tf_op jit(solution)/shard_map/ppermute | solution.py:518
  (34 other events, 1133.3 us)

commit v2 on v1

--- a/solution.py
+++ b/solution.py
@@ -250,26 +250,32 @@
     return buf[pl.ds(pl.multiple_of(pl.program_id(0) * ROW_TILE, ROW_TILE), ROW_TILE), :]
 
 
-def forward_first_kernel(n_ref, offset_s, kept_s, *refs):
+def forward_first_kernel(n_ref, offset_s, kept_s, *refs, quarters):
     ins, refs = refs[:N_SHIFT], refs[N_SHIFT:]
-    w1_ref, w3_ref, w2_ref, a_ref, b_ref, y_out, rows_ref, buf, sem, out_sem = refs
+    weights, refs = refs[:3 * quarters], refs[3 * quarters:]
+    acts, refs = refs[:2 * quarters], refs[2 * quarters:]
+    y_out, rows_ref, buf, sem, out_sem = refs
     end = pack_rows(kept_s, offset_s, ins, rows_ref, buf, sem, out_sem)
 
     @pl.when(pl.program_id(0) < n_ref[0])
     def _():
         x = row_tile(buf)
-        a = dot_nn(x, val(w1_ref))
-        b = dot_nn(x, val(w3_ref))
-        a_ref[...] = a
-        b_ref[...] = b
-        y_out[...] = dot_nn((a * jax.nn.sigmoid(a) * b).astype(BF16), val(w2_ref))
+        total = None
+        for q in range(quarters):
+            w1_ref, w3_ref, w2_ref = weights[3 * q:3 * q + 3]
+            a = dot_nn(x, val(w1_ref))
+            b = dot_nn(x, val(w3_ref))
+            acts[2 * q][...] = a
+            acts[2 * q + 1][...] = b
+            y = dot_nn((a * jax.nn.sigmoid(a) * b).astype(BF16), val(w2_ref))
+            total = y if total is None else total + y
+        y_out[...] = total
 
     end()
 
 
-def forward_kernel(n_ref, offset_s, x_ref, w1_ref, w3_ref, w2_ref, y_in, a_ref, b_ref, *rest, last):
-    if last:
-        outs, (buf, sem) = rest[:N_SHIFT], rest[N_SHIFT:]
+def forward_last_kernel(n_ref, offset_s, x_ref, w1_ref, w3_ref, w2_ref, y_in, a_ref, b_ref, *rest):
+    outs, (buf, sem) = rest[:N_SHIFT], rest[N_SHIFT:]
     i = pl.program_id(0)
 
     @pl.when(i < n_ref[0])
@@ -279,15 +285,11 @@
         a_ref[...] = a
         b_ref[...] = b
         y = val(y_in) + dot_nn((a * jax.nn.sigmoid(a) * b).astype(BF16), val(w2_ref))
-        if last:
-            buf[pl.ds(pl.multiple_of(i * ROW_TILE, ROW_TILE), ROW_TILE), :] = y.astype(BF16)
-        else:
-            rest[0][...] = y
-
-    if last:
-        @pl.when(i == pl.num_programs(0) - 1)
-        def _():
-            rows_out(buf, offset_s, outs, sem)
+        buf[pl.ds(pl.multiple_of(i * ROW_TILE, ROW_TILE), ROW_TILE), :] = y.astype(BF16)
+
+    @pl.when(i == pl.num_programs(0) - 1)
+    def _():
+        rows_out(buf, offset_s, outs, sem)
 
 
 def act_grads(du, a, b):
@@ -606,9 +608,10 @@
 
         weights = (w_gate, w_up, w_down)
         q_own = [take(w, mine) for w in weights]
-        q_twin = permute(q_own[:1], twin_pairs) + permute(q_own[1:], twin_pairs)
-        q_split = permute([take(w, 1 - mine) for w in weights], split_pairs)
-        q_far = permute(q_split, twin_pairs)
+        q_twin = permute(q_own, twin_pairs)
+        q_other = [take(w, 1 - mine) for w in weights]
+        q_split = permute(q_other[:1], split_pairs) + permute(q_other[1:], split_pairs)
+        q_far = permute(q_split[:1], twin_pairs) + permute(q_split[1:], twin_pairs)
 
         c_recv = exchange(c_send, forth)
 
@@ -641,19 +644,19 @@
         packed = jax.ShapeDtypeStruct((rows + ROW_TILE, d_model), BF16)
         pack_scratch = [pltpu.VMEM((rows + ROW_TILE, d_model), BF16), pltpu.SemaphoreType.DMA((N_SHIFT, 6)), pltpu.SemaphoreType.DMA((N_SHIFT + 1, 6))]
 
-        def forward_first(quarter, parts):
+        def forward_first(quarters, parts):
+            k = len(quarters)
+            flat = [w for quarter in quarters for w in quarter]
             out = rows_call(
-                forward_first_kernel, 3, [hbm()] * N_SHIFT + full, [row_spec(width)] * 2 + [row_spec(d_model), hbm()],
-                [act_shape] * 2 + [row_f32, packed], pack_scratch, {}, kept, *parts, *quarter, scalars=3)
-            return out[:2], out[2], out[3]
-
-        def forward(quarter, y_acc, last=False):
+                functools.partial(forward_first_kernel, quarters=k), 3 * k, [hbm()] * N_SHIFT + full * k, [row_spec(width)] * (2 * k) + [row_spec(d_model), hbm()],
+                [act_shape] * (2 * k) + [row_f32, packed], pack_scratch, {}, kept, *parts, *flat, scalars=3)
+            return [out[2 * q:2 * q + 2] for q in range(k)], out[-2], out[-1]
+
+        def forward_last(quarter, y_acc):
             out = rows_call(
-                functools.partial(forward_kernel, last=last), 3,
-                [row_spec(d_model)] + full + [row_spec(d_model)], [row_spec(width)] * 2 + (slots_outs if last else [row_spec(d_model)]),
-                [act_shape] * 2 + (slots_shapes if last else [row_f32]), slots_scratch if last else [], {} if last else {6: 2},
-                x_rows, *quarter, y_acc)
-            return out[:2], (out[2:] if last else out[2])
+                forward_last_kernel, 3, [row_spec(d_model)] + full + [row_spec(d_model)], [row_spec(width)] * 2 + slots_outs,
+                [act_shape] * 2 + slots_shapes, slots_scratch, {}, x_rows, *quarter, y_acc)
+            return out[:2], out[2:]
 
         def half(piece, pieces):
             w = width // pieces
@@ -693,15 +696,14 @@
                 weight_grads_kernel, 4, [row_spec(d_model)] * 2 + [row_spec(width)] * 2 + full[2:], full,
                 grad_shapes, [], {}, x_rows, c_rows, *acts, quarter[2])
 
-        act_own, acc_y, x_rows = forward_first(q_own, x_recv)
-        act_twin, acc_y = forward(q_twin, acc_y)
+        (act_own, act_twin), acc_y, x_rows = forward_first([q_own, q_twin], x_recv)
         g_twin_0, acc_dx, c_rows = backward_first(q_twin, act_twin, [after(c_recv[0], acc_y)] + c_recv[1:])
         g_twin_0 = permute(g_twin_0, twin_pairs)
         g_twin_1, acc_dx = backward(q_twin, act_twin, acc_dx, 1, 2)
         g_twin_1 = permute(g_twin_1, twin_pairs)
         g_far, acc_dx, acc_y = both(q_far, acc_y, acc_dx)
-        g_far = permute(g_far, twin_pairs)
-        act_split, y_send = forward(q_split, acc_y, True)
+        g_far = permute(g_far[:1], twin_pairs) + permute(g_far[1:], twin_pairs)
+        act_split, y_send = forward_last(q_split, acc_y)
         y_recv = exchange(y_send, back)
         g_split, acc_dx = backward(q_split, [after(act_split[0], acc_dx), act_split[1]], acc_dx, 0, 1)
         got_split = permute([g_split[0] + g_far[0]], split_pairs)
@@ -762,6 +764,8 @@
             )(mine[None].astype(I32), own, got_0, got_1)
 
         halves = [finish_own(after(own, shared), got_0, got_1) for own, got_0, got_1 in zip(g_own, g_twin_0, g_twin_1)]
+        d_gate = finish_other(g_split[0], halves[0])
+
         d_hidden = pl.pallas_call(
             dx_combine_kernel, grid=(tok_rows // TOK_TILE,),
             in_specs=[smem()] * 3 + [hbm()] * N_SHIFT + [tok_block(128), tok_block(128), tok_block(d_model), whole((128, d_model))],
@@ -769,16 +773,11 @@
             out_shape=jax.ShapeDtypeStruct((tok_rows, d_model), BF16),
             scratch_shapes=combine_scratch,
             compiler_params=params("arbitrary"), cost_estimate=cost(spread_flops, 4 * rows * d_model),
-        )(order, base, my_kept, *dx_recv, after(info, halves), dz, d_out, wr6)
+        )(order, base, my_kept, *dx_recv, after(info, d_gate), dz, d_out, wr6)
 
         shared = shared + after(across_x, d_hidden)
         across = [flip(shared, bits) for bits in (4, 8, 12)]
-        done = d_hidden
-        outputs = []
-        for other, half in zip(g_split, halves):
-            done = finish_other(after(other, done), half)
-            outputs.append(done)
-        d_gate, d_up, d_down = outputs
+        d_up, d_down = [finish_other(after(other, d_hidden), part) for other, part in zip(g_split[1:], halves[1:])]
         across = [after(v, d_down) for v in across]
         shared = (shared + across[0]) + (across[1] + across[2])
         d_router = shared[:n_experts].T

time: 1070 us -> 1090 us (1.019); the launches traced: 1050 us -> 1080 us
  waiting for transfers between devices: 335 us -> 395 us
  starting transfers between devices: 175 us -> 156 us
    ppermute x27, waiting for transfers between devices: 101 us -> 132 us  [exchange(): out.append(lax.ppermute(parts[s], dev_axes, pairs[s]))]
    ppermute x21, waiting for transfers between devices: 225 us -> 250 us  [permute(): return [lax.ppermute(v, dev_axes, pairs) for v in values]]
    pallas_call x9 -> x8, Pallas kernels: 375 us -> 371 us  [rows_call(): pl.pallas_call(kernel, grid_spec=pltpu.PrefetchScalarGridSpec(num_scalar_...]
  transfers between devices with their start and end apart: 60 -> 60, of which waited for: 18 -> 16; matrix products, arithmetic and copies ran while one was open for 3% -> 3% of each run, Pallas kernels for 37% -> 36%
where the time goes in v2:
time: 1090 us; the launch traced here: 1080 us
  Pallas kernels  495 us (45%)
  waiting for transfers between devices  395 us (36%)
  starting transfers between devices  156 us (14%)
  local copies, waits for them, and re-layouts  19.1 us (2%)
  other arithmetic  15.8 us (1%)
    pallas_call x8, Pallas kernels, rows_call(): pl.pallas_call(kernel, grid_spec=pltpu.PrefetchScalarGridSpec(num_scalar_...  371 us
    ppermute x21, waiting for transfers between devices, permute(): return [lax.ppermute(v, dev_axes, pairs) for v in values]  250 us
    ppermute x27, waiting for transfers between devices, exchange(): out.append(lax.ppermute(parts[s], dev_axes, pairs[s]))  132 us
    ppermute x27, starting transfers between devices, exchange(): out.append(lax.ppermute(parts[s], dev_axes, pairs[s]))  117 us
    pallas_call x1, Pallas kernels, layer(): y_combine(order, base, my_kept, *y_recv, after(info, g_own[0]), hidden, d...  27.7 us
    pallas_call x1, Pallas kernels, layer(): info, prob_sum, *c_send = c_slots(order, base, ids_t, hidden, d_out, wr3)  27.4 us
    ppermute x21, starting transfers between devices, permute(): return [lax.ppermute(v, dev_axes, pairs) for v in values]  25.1 us
  transfers between devices with their start and end apart: 60, of which 16 were waited for; matrix products, arithmetic and copies ran while one was open for 3% of the time, Pallas kernels for 36%

profile of v2, /device:TPU:0, one launch (start us, length us, event | category | flops | bytes accessed | tf_op | source)
XLA Modules:
  0.0 1084.4 jit_solution(11331018386264758674)
XLA Ops:
  0.6 3.2 collective-permute-start.8
  6.8 13.2 %shard_map.144 = (s32[8,128]{1,0:T(8,128)}, bf16[896,768]{1,0:T(8,128)(2,1)}, bf16[896,768]{1,0:T(8,128)(2,1)}, bf16[896,768]{1,0:T(8,128)(2,1)}, bf16[896,768]{1,0:T(8,128)(2,1)}) custom-call(s32[5]{0:T(128)} %concatenate.53.order_ref, s32[2,2048]{1,0:T(2,128)} %bitcast.65, bf16[2048,768]{1,0:T(8,128)(2,1)} %refs_9_.1), custom_call_target="tpu_custom_call" | custom-call | flops 3422552064 | bytes 5505024 | tf_op jit(solution)/shard_map/pallas_call | solution.py:570
  28.1 10.5 collective-permute-done.1
  45.5 27.4 %shard_map.148 = (f32[2048,128]{1,0:T(8,128)}, f32[8,128]{1,0:T(8,128)}, bf16[896,768]{1,0:T(8,128)(2,1)}, bf16[896,768]{1,0:T(8,128)(2,1)}, bf16[896,768]{1,0:T...) custom-call(s32[8]{0:T(128)} %stack.62.order_ref, ...), custom_call_target="tpu_custom_call" | custom-call | flops 6845104128 | bytes 11010048 | tf_op jit(solution)/shard_map/pallas_call | solution.py:604
  75.8 3.9 dynamic-slice_bitcast_fusion
  81.2 23.2 %collective-permute-done.19.refs_1_ = bf16[896,768]{1,0:T(8,128)(2,1)} collective-permute-done((bf16[896,768]{1,0:T(8,128)(2,1)}, bf16[896,768]{1,0:T(8,128)(2,1)}, u32[]{:S(2)}, u32[]{:S(2)}) %collective-permute-start.19) | collective-permute-done | bytes 1376288 | tf_op jit(solution)/shard_map/ppermute | solution.py:520
  104.9 3.4 collective-permute-start.23
  116.2 13.3 %shard_map.146 = (s32[8,128]{1,0:T(8,128)}, bf16[896,768]{1,0:T(8,128)(2,1)}, bf16[896,768]{1,0:T(8,128)(2,1)}, bf16[896,768]{1,0:T(8,128)(2,1)}, bf16[896,768]{1,0:T(8,128)(2,1)}) custom-call(s32[5]{0:T(128)} %concatenate.53.order_ref, s32[2,2048]{1,0:T(2,128)} %copy-done.32, bf16[2048,768]{1,0:T(8,128)(2,1)} %collective-permute-done.9.h_ref), custom_call_target="tpu_custom_call" | custom-call | flops 3422552064 | bytes 5505024 | tf_op jit(solution)/shard_map/pallas_call | solution.py:571
  129.5 8.2 collective-permute-done.22.refs_4_
  137.8 2.5 collective-permute-start.10
  140.2 24.7 %collective-permute-done.23.refs_5_ = bf16[896,768]{1,0:T(8,128)(2,1)} collective-permute-done((bf16[896,768]{1,0:T(8,128)(2,1)}, bf16[896,768]{1,0:T(8,128)(2,1)}, u32[]{:S(2)}, u32[]{:S(2)}) %collective-permute-start.23) | collective-permute-done | bytes 1376288 | tf_op jit(solution)/shard_map/ppermute | solution.py:520
  172.1 13.7 %collective-permute-done.14.refs_12_.w3_ref = bf16[768,1024]{1,0:T(8,128)(2,1)} collective-permute-done((bf16[768,1024]{1,0:T(8,128)(2,1)}, bf16[768,1024]{1,0:T(8,128)(2,1)}, u32[]{:S(2)}, u32[]{:S(2)}) %collective-permute-start.14) | collective-permute-done | bytes 1572896 | tf_op jit(solution)/shard_map/ppermute | solution.py:515
  188.3 30.7 %collective-permute-done.12.refs_7_ = bf16[896,768]{1,0:T(8,128)(2,1)} collective-permute-done((bf16[896,768]{1,0:T(8,128)(2,1)}, bf16[896,768]{1,0:T(8,128)(2,1)}, u32[]{:S(2)}, u32[]{:S(2)}) %collective-permute-start.12) | collective-permute-done | bytes 1376288 | tf_op jit(solution)/shard_map/ppermute | solution.py:520
  220.5 60.9 %shard_map.147 = (f32[7168,1024]{1,0:T(8,128)}, f32[7168,1024]{1,0:T(8,128)}, f32[7168,1024]{1,0:T(8,128)}, f32[7168,1024]{1,0:T(8,128)}, f32[7168,768]{1,0:T(8,128)}, /*index=5*/bf16[7680,768]{1,0:T(8,128)(2,1)}) custom-call(s32[1]{0:T(128)S(6)} %select_n.119.n_ref, s32[9]{0:T(128)} %pad_add_fusion.1.offset_s, s32[8]{0:T(128)} %copy-done.20, ...), custom_call_target="tpu_custom_call" | custom-call | flops 67645734912 | bytes 110100480 | tf_op jit(solution)/shard_map/pallas_call | solution.py:635
  281.4 5.2 collective-permute-start.26
  288.7 35.2 %shard_map.149 = (f32[768,512]{1,0:T(8,128)}, f32[768,512]{1,0:T(8,128)}, f32[512,768]{1,0:T(8,128)}, f32[7168,768]{1,0:T(8,128)}, bf16[7680,768]{1,0:T(8,128)(2,1)}) custom-call(s32[1]{0:T(128)S(6)} %select_n.119.n_ref, s32[9]{0:T(128)} %pad_add_fusion.1.offset_s, s32[8]{0:T(128)} %copy-done.20, bf16[896,768]{1,0:T(8,128)(2,1)} %get-tuple-element.102.refs_0_, ...), custom_call_target="tpu_custom_call" | custom-call | flops 33822867456 | bytes 110100480 | tf_op jit(solution)/shard_map/pallas_call | solution.py:635
  323.9 32.0 %shard_map.150 = (f32[768,512]{1,0:T(8,128)}, f32[768,512]{1,0:T(8,128)}, f32[512,768]{1,0:T(8,128)}, f32[7168,768]{1,0:T(8,128)}) custom-call(s32[1]{0:T(128)S(6)} %select_n.119.n_ref, s32[9]{0:T(128)} %pad_add_fusion.1.offset_s, bf16[7680,768]{1,0:T(8,128)(2,1)} %get-tuple-element.99.refs_8_.x_ref, ...), custom_call_target="tpu_custom_call", output_to_operand_aliasing={{3}: (9, {})} | custom-call | flops 33822867456 | bytes 110100480 | tf_op jit(solution)/shard_map/pallas_call | solution.py:635
  357.1 73.0 %shard_map.151 = (f32[768,1024]{1,0:T(8,128)}, f32[768,1024]{1,0:T(8,128)}, f32[1024,768]{1,0:T(8,128)}, f32[7168,768]{1,0:T(8,128)}, f32[7168,768]{1,0:T(8,128)}) custom-call(s32[1]{0:T(128)S(6)} %select_n.119.n_ref, s32[9]{0:T(128)} %pad_add_fusion.1.offset_s, ...), custom_call_target="tpu_custom_call", output_to_operand_aliasing={{3}: (8, {}), {4}: (7, {})} | custom-call | flops 101468602368 | bytes 110100480 | tf_op jit(solution)/shard_map/pallas_call | solution.py:635
  430.1 34.3 %shard_map.152 = (f32[7168,1024]{1,0:T(8,128)}, f32[7168,1024]{1,0:T(8,128)}, bf16[896,768]{1,0:T(8,128)(2,1)}, bf16[896,768]{1,0:T(8,128)(2,1)}, bf16[896,768]{...) custom-call(s32[1]{0:T(128)S(6)} %select_n.119.n_ref, ...), custom_call_target="tpu_custom_call" | custom-call | flops 33822867456 | bytes 110100480 | tf_op jit(solution)/shard_map/pallas_call | solution.py:635
  464.3 18.5 %collective-permute-start.29 = (bf16[896,768]{1,0:T(8,128)(2,1)}, bf16[896,768]{1,0:T(8,128)(2,1)S(1)}, u32[]{:S(2)}, u32[]{:S(2)}) collective-permute-start(bf16[896,768]{1,0:T(8,128)(2,1)} %get-tuple-element.117), channel_id=1, source_target_pairs={{4,0},{9,1},{6,2},{11,3},{0,4},{13,5},{2,6},{15,7},{12,8},{1,9},{1... | collective-permute-start | bytes 4128776 | tf_op jit(solution)/shard_map/ppermute | solution.py:520
  483.9 42.5 %collective-permute-start.32 = (bf16[896,768]{1,0:T(8,128)(2,1)}, bf16[896,768]{1,0:T(8,128)(2,1)}, u32[]{:S(2)}, u32[]{:S(2)}) collective-permute-start(bf16[896,768]{1,0:T(8,128)(2,1)} %get-tuple-element.120), channel_id=1, source_target_pairs={{2,0},{3,1},{0,2},{1,3},{6,4},{7,5},{4,6},{5,7},{10,8},{11,9},{8,1... | collective-permute-start | bytes 4128776 | tf_op jit(solution)/shard_map/ppermute | solution.py:520
  527.8 55.2 %shard_map.153 = (f32[768,1024]{1,0:T(8,128)}, f32[768,1024]{1,0:T(8,128)}, f32[1024,768]{1,0:T(8,128)}, f32[7168,768]{1,0:T(8,128)}) custom-call(s32[1]{0:T(128)S(6)} %select_n.119.n_ref, s32[9]{0:T(128)} %pad_add_fusion.1.offset_s, bf16[7680,768]{1,0:T(8,128)(2,1)} %get-tuple-element.99.refs_8_.x_ref, ...), custom_call_target="tpu_custom_call", output_to_operand_aliasing={{3}: (9, {})} | custom-call | flops 67645734912 | bytes 110100480 | tf_op jit(solution)/shard_map/pallas_call | solution.py:635
  583.1 38.9 %shard_map.154 = (bf16[896,768]{1,0:T(8,128)(2,1)}, bf16[896,768]{1,0:T(8,128)(2,1)}, bf16[896,768]{1,0:T(8,128)(2,1)}, bf16[896,768]{1,0:T(8,128)(2,1)}, bf16[8...) custom-call(s32[1]{0:T(128)S(6)} %select_n.119.n_ref, ...), custom_call_target="tpu_custom_call" | custom-call | flops 33822867456 | bytes 110100480 | tf_op jit(solution)/shard_map/pallas_call | solution.py:635
  622.0 27.5 %collective-permute-start.34 = (bf16[896,768]{1,0:T(8,128)(2,1)}, bf16[896,768]{1,0:T(8,128)(2,1)}, u32[]{:S(2)}, u32[]{:S(2)}) collective-permute-start(bf16[896,768]{1,0:T(8,128)(2,1)} %get-tuple-element.122), channel_id=1, source_target_pairs={{3,0},{2,1},{1,2},{0,3},{7,4},{6,5},{5,6},{4,7},{11,8},{10,9},{9,1... | collective-permute-start | bytes 4128776 | tf_op jit(solution)/shard_map/ppermute | solution.py:520
  651.6 41.2 %shard_map.155 = (f32[768,1024]{1,0:T(8,128)}, f32[768,1024]{1,0:T(8,128)}, f32[1024,768]{1,0:T(8,128)}) custom-call(s32[1]{0:T(128)S(6)} %select_n.119.n_ref, s32[9]{0:T(128)} %pad_add_fusion.1.offset_s, bf16[7680,768]{1,0:T(8,128)(2,1)} %get-tuple-element.99.refs_8_.x_ref, bf16[7680,768]{1,0:T(8,128)(2,1)} %get-tuple-element.112.c_ref, ...), custom_call_target="tpu_custom_call" | custom-call | flops 45097156608 | bytes 110100480 | tf_op jit(solution)/shard_map/pallas_call | solution.py:635
  692.8 5.6 collective-permute-start.59
  698.5 3.5 collective-permute-start.38
  702.0 5.6 collective-permute-start.39
  707.7 27.7 %shard_map.156 = (bf16[2048,768]{1,0:T(8,128)(2,1)}, bf16[2048,128]{1,0:T(8,128)(2,1)}, f32[128,768]{1,0:T(8,128)}) custom-call(s32[8]{0:T(128)} %stack.62.order_ref, s32[8,128]{1,0:T(8,128)} %get-tuple-element.90.base_s, s32[8]{0:T(128)} %fusion.2.kept_s, bf16[896,768]{1,0:T(8,128)(2,1)} %get-tuple-element.116.refs_0_, bf16[896,768]{1,0:T(8,128)(2,1)} %copy-done.30, ...), custom_call_target="tpu_custom_call" | custom-call | flops 13690208256 | bytes 22020096 | tf_op jit(solution)/shard_map/pallas_call | solution.py:734
  736.3 2.2 collective-permute-done.39.refs_4_
  740.5 3.9 add.255
  744.5 3.5 collective-permute-done.59.part_1_ref
  748.3 117.6 %collective-permute-done.58.part_0_ref = f32[768,512]{1,0:T(8,128)S(1)} collective-permute-done((f32[768,512]{1,0:T(8,128)}, f32[768,512]{1,0:T(8,128)S(1)}, u32[]{:S(2)}, u32[]{:S(2)}) %collective-permute-start.58) | collective-permute-done | bytes 1572896 | tf_op jit(solution)/shard_map/ppermute | solution.py:515
  866.1 16.7 %collective-permute-done.47.part_1_ref = f32[768,512]{1,0:T(8,128)S(1)} collective-permute-done((f32[768,512]{1,0:T(8,128)}, f32[768,512]{1,0:T(8,128)S(1)}, u32[]{:S(2)}, u32[]{:S(2)}) %collective-permute-start.47) | collective-permute-done | bytes 1572896 | tf_op jit(solution)/shard_map/ppermute | solution.py:515
  884.8 4.7 add.264
  892.0 16.7 %collective-permute-done.46.part_0_ref = f32[768,512]{1,0:T(8,128)S(1)} collective-permute-done((f32[768,512]{1,0:T(8,128)S(1)}, f32[768,512]{1,0:T(8,128)S(1)}, u32[]{:S(2)}, u32[]{:S(2)}) %collective-permute-start.46) | collective-permute-done | bytes 1572896 | tf_op jit(solution)/shard_map/ppermute | solution.py:515
  908.8 33.7 %collective-permute-done.53.part_1_ref = f32[512,768]{1,0:T(8,128)S(1)} collective-permute-done((f32[512,768]{1,0:T(8,128)S(1)}, f32[512,768]{1,0:T(8,128)S(1)}, u32[]{:S(2)}, u32[]{:S(2)}) %collective-permute-start.53) | collective-permute-done | bytes 1572896 | tf_op jit(solution)/shard_map/ppermute | solution.py:515
  942.5 48.4 %collective-permute-done.52.part_0_ref = f32[512,768]{1,0:T(8,128)S(1)} collective-permute-done((f32[512,768]{1,0:T(8,128)S(1)}, f32[512,768]{1,0:T(8,128)S(1)}, u32[]{:S(2)}, u32[]{:S(2)}) %collective-permute-start.52) | collective-permute-done | bytes 1572896 | tf_op jit(solution)/shard_map/ppermute | solution.py:515
  992.2 4.2 shard_map.162._
  996.4 4.2 shard_map.157._
  1000.6 4.2 shard_map.160._
  1004.8 3.2 shard_map.158
  1008.5 15.3 %collective-permute-done.41.refs_6_ = bf16[896,768]{1,0:T(8,128)(2,1)} collective-permute-done((bf16[896,768]{1,0:T(8,128)(2,1)}, bf16[896,768]{1,0:T(8,128)(2,1)}, u32[]{:S(2)}, u32[]{:S(2)}) %collective-permute-start.41) | collective-permute-done | bytes 1376288 | tf_op jit(solution)/shard_map/ppermute | solution.py:520
  1023.7 28.0 %collective-permute-done.42.refs_7_ = bf16[896,768]{1,0:T(8,128)(2,1)} collective-permute-done((bf16[896,768]{1,0:T(8,128)(2,1)}, bf16[896,768]{1,0:T(8,128)(2,1)}, u32[]{:S(2)}, u32[]{:S(2)}) %collective-permute-start.42) | collective-permute-done | bytes 1376288 | tf_op jit(solution)/shard_map/ppermute | solution.py:520
  1051.8 19.0 %shard_map.159 = bf16[2048,768]{1,0:T(8,128)(2,1)} custom-call(s32[8]{0:T(128)} %stack.62.order_ref, s32[8,128]{1,0:T(8,128)} %get-tuple-element.90.base_s, s32[8]{0:T(128)} %fusion.2.kept_s, bf16[896,768]{1,0:T(8,128)(2,1)} %get-tuple-element.132.refs_0_, bf16[896,768]{1,0:T(8,128)(2,1)} %collective-permute-done.36.refs_1_, ...), custom_call_target="tpu_custom_call" | custom-call | flops 6845104128 | bytes 22020096 | tf_op jit(solution)/shard_map/pallas_call | solution.py:769
  1071.8 3.0 collective-permute-start.55
  1074.7 3.2 shard_map.163
  1077.9 3.2 shard_map.161
  (209 shorter events, 61.0 us)
Async XLA Ops:
  0.6 72.3 %collective-permute-start.8 = (s32[2,2048]{1,0:T(2,128)}, s32[2,2048]{1,0:T(2,128)S(1)}, u32[]{:S(2)}, u32[]{:S(2)}) collective-permute-start(s32[2,2048]{1,0:T(2,128)} %bitcast.63), channel_id=1, source_target_pairs={{0,2},{1,3},{2,0},{3,1},{4,6},{5,7},{6,4},{7,5},{8,10},{9,11},{10,... | collective-permute-start | bytes 49160 | tf_op jit(solution)/shard_map/ppermute | solution.py:550
  20.0 54.5 %collective-permute-start.5 = (bf16[896,768]{1,0:T(8,128)(2,1)}, bf16[896,768]{1,0:T(8,128)(2,1)S(1)}, u32[]{:S(2)}, u32[]{:S(2)}) collective-permute-start(bf16[896,768]{1,0:T(8,128)(2,1)} %get-tuple-element.92), channel_id=1, source_target_pairs={{0,4},{1,9},{2,6},{3,11},{4,0},{5,13},{6,2},{7,15},{8,12},{9,1},{1... | collective-permute-start | bytes 4128776 | tf_op jit(solution)/shard_map/ppermute | solution.py:520
  38.7 75.9 %collective-permute-start.9 = (bf16[2048,768]{1,0:T(8,128)(2,1)}, bf16[2048,768]{1,0:T(8,128)(2,1)}, u32[]{:S(2)}, u32[]{:S(2)}) collective-permute-start(bf16[2048,768]{1,0:T(8,128)(2,1)} %refs_9_.1), channel_id=1, source_target_pairs={{0,2},{1,3},{2,0},{3,1},{4,6},{5,7},{6,4},{7,5},{8,10},{9,11},{10,... | collective-permute-start | bytes 9437192 | tf_op jit(solution)/shard_map/ppermute | solution.py:550
  40.7 33.9 %collective-permute-start.6 = (bf16[896,768]{1,0:T(8,128)(2,1)}, bf16[896,768]{1,0:T(8,128)(2,1)}, u32[]{:S(2)}, u32[]{:S(2)}) collective-permute-start(bf16[896,768]{1,0:T(8,128)(2,1)} %get-tuple-element.93), channel_id=1, source_target_pairs={{0,1},{1,0},{2,3},{3,2},{4,5},{5,4},{6,7},{7,6},{8,9},{9,8},{10,11... | collective-permute-start | bytes 4128776 | tf_op jit(solution)/shard_map/ppermute | solution.py:520
  44.1 35.6 %collective-permute-start.7 = (bf16[896,768]{1,0:T(8,128)(2,1)}, bf16[896,768]{1,0:T(8,128)(2,1)}, u32[]{:S(2)}, u32[]{:S(2)}) collective-permute-start(bf16[896,768]{1,0:T(8,128)(2,1)} %get-tuple-element.94), channel_id=1, source_target_pairs={{0,9},{1,4},{2,11},{3,6},{4,13},{5,0},{6,15},{7,2},{8,1},{9,12},{1... | collective-permute-start | bytes 4128776 | tf_op jit(solution)/shard_map/ppermute | solution.py:520
  75.6 38.5 %collective-permute-start.21 = (bf16[896,768]{1,0:T(8,128)(2,1)}, bf16[896,768]{1,0:T(8,128)(2,1)}, u32[]{:S(2)}, u32[]{:S(2)}) collective-permute-start(bf16[896,768]{1,0:T(8,128)(2,1)} %get-tuple-element.105), channel_id=1, source_target_pairs={{0,9},{1,4},{2,11},{3,6},{4,13},{5,0},{6,15},{7,2},{8,1},{9,12},{1... | collective-permute-start | bytes 4128776 | tf_op jit(solution)/shard_map/ppermute | solution.py:520
  79.7 86.6 %collective-permute-start.15 = (bf16[1024,768]{1,0:T(8,128)(2,1)}, bf16[1024,768]{1,0:T(8,128)(2,1)}, u32[]{:S(2)}, u32[]{:S(2)}) collective-permute-start(bf16[1024,768]{1,0:T(8,128)(2,1)} %get-tuple-element.184.refs_10_.w2_ref), channel_id=1, source_target_pairs={{0,8},{1,5},{2,10},{3,7},{4,12},{5,1},{6,14},{7,3},{8,0},{9,13},{1... | collective-permute-start | bytes 4718600 | tf_op jit(solution)/shard_map/ppermute | solution.py:515
  104.4 33.4 %collective-permute-start.22 = (bf16[896,768]{1,0:T(8,128)(2,1)}, bf16[896,768]{1,0:T(8,128)(2,1)}, u32[]{:S(2)}, u32[]{:S(2)}) collective-permute-start(bf16[896,768]{1,0:T(8,128)(2,1)} %get-tuple-element.106), channel_id=1, source_target_pairs={{0,2},{1,3},{2,0},{3,1},{4,6},{5,7},{6,4},{7,5},{8,10},{9,11},{10,... | collective-permute-start | bytes 4128776 | tf_op jit(solution)/shard_map/ppermute | solution.py:520
  104.9 60.0 %collective-permute-start.23 = (bf16[896,768]{1,0:T(8,128)(2,1)}, bf16[896,768]{1,0:T(8,128)(2,1)}, u32[]{:S(2)}, u32[]{:S(2)}) collective-permute-start(bf16[896,768]{1,0:T(8,128)(2,1)} %get-tuple-element.107), channel_id=1, source_target_pairs={{0,6},{1,11},{2,4},{3,9},{4,2},{5,15},{6,0},{7,13},{8,14},{9,3},{1... | collective-permute-start | bytes 4128776 | tf_op jit(solution)/shard_map/ppermute | solution.py:520
  114.1 58.0 %collective-permute-start.13 = (bf16[768,1024]{1,0:T(8,128)(2,1)}, bf16[768,1024]{1,0:T(8,128)(2,1)}, u32[]{:S(2)}, u32[]{:S(2)}) collective-permute-start(bf16[768,1024]{1,0:T(8,128)(2,1)} %get-tuple-element.188.refs_8_.w1_ref), channel_id=1, source_target_pairs={{0,8},{1,5},{2,10},{3,7},{4,12},{5,1},{6,14},{7,3},{8,0},{9,13},{1... | collective-permute-start | bytes 4718600 | tf_op jit(solution)/shard_map/ppermute | solution.py:515
  114.5 71.2 %collective-permute-start.14 = (bf16[768,1024]{1,0:T(8,128)(2,1)}, bf16[768,1024]{1,0:T(8,128)(2,1)}, u32[]{:S(2)}, u32[]{:S(2)}) collective-permute-start(bf16[768,1024]{1,0:T(8,128)(2,1)} %get-tuple-element.186.refs_9_.w3_ref), channel_id=1, source_target_pairs={{0,8},{1,5},{2,10},{3,7},{4,12},{5,1},{6,14},{7,3},{8,0},{9,13},{1... | collective-permute-start | bytes 4718600 | tf_op jit(solution)/shard_map/ppermute | solution.py:515
  137.8 48.5 %collective-permute-start.10 = (bf16[896,768]{1,0:T(8,128)(2,1)}, bf16[896,768]{1,0:T(8,128)(2,1)S(1)}, u32[]{:S(2)}, u32[]{:S(2)}) collective-permute-start(bf16[896,768]{1,0:T(8,128)(2,1)} %get-tuple-element.96), channel_id=1, source_target_pairs={{0,4},{1,9},{2,6},{3,11},{4,0},{5,13},{6,2},{7,15},{8,12},{9,1},{1... | collective-permute-start | bytes 4128776 | tf_op jit(solution)/shard_map/ppermute | solution.py:520
  166.3 52.7 %collective-permute-start.12 = (bf16[896,768]{1,0:T(8,128)(2,1)}, bf16[896,768]{1,0:T(8,128)(2,1)}, u32[]{:S(2)}, u32[]{:S(2)}) collective-permute-start(bf16[896,768]{1,0:T(8,128)(2,1)} %get-tuple-element.98), channel_id=1, source_target_pairs={{0,9},{1,4},{2,11},{3,6},{4,13},{5,0},{6,15},{7,2},{8,1},{9,12},{1... | collective-permute-start | bytes 4128776 | tf_op jit(solution)/shard_map/ppermute | solution.py:520
  172.1 116.5 %collective-permute-start.24 = (bf16[896,768]{1,0:T(8,128)(2,1)}, bf16[896,768]{1,0:T(8,128)(2,1)}, u32[]{:S(2)}, u32[]{:S(2)}) collective-permute-start(bf16[896,768]{1,0:T(8,128)(2,1)} %get-tuple-element.108), channel_id=1, source_target_pairs={{0,3},{1,2},{2,1},{3,0},{4,7},{5,6},{6,5},{7,4},{8,11},{9,10},{10,... | collective-permute-start | bytes 4128776 | tf_op jit(solution)/shard_map/ppermute | solution.py:520
  185.8 102.9 %collective-permute-start.25 = (bf16[896,768]{1,0:T(8,128)(2,1)}, bf16[896,768]{1,0:T(8,128)(2,1)}, u32[]{:S(2)}, u32[]{:S(2)}) collective-permute-start(bf16[896,768]{1,0:T(8,128)(2,1)} %get-tuple-element.109), channel_id=1, source_target_pairs={{0,11},{1,6},{2,9},{3,4},{4,15},{5,2},{6,13},{7,0},{8,3},{9,14},{1... | collective-permute-start | bytes 4128776 | tf_op jit(solution)/shard_map/ppermute | solution.py:520
  186.2 95.2 %collective-permute-start.16 = (bf16[768,1024]{1,0:T(8,128)(2,1)}, bf16[768,1024]{1,0:T(8,128)(2,1)}, u32[]{:S(2)}, u32[]{:S(2)}) collective-permute-start(bf16[768,1024]{1,0:T(8,128)(2,1)} %get-tuple-element.187), channel_id=1, source_target_pairs={{0,4},{1,9},{2,6},{3,11},{4,0},{5,13},{6,2},{7,15},{8,12},{9,1},{1... | collective-permute-start | bytes 4718600 | tf_op jit(solution)/shard_map/ppermute | solution.py:515
  188.0 98.6 %collective-permute-start.17 = (bf16[768,1024]{1,0:T(8,128)(2,1)}, bf16[768,1024]{1,0:T(8,128)(2,1)}, u32[]{:S(2)}, u32[]{:S(2)}) collective-permute-start(bf16[768,1024]{1,0:T(8,128)(2,1)} %get-tuple-element.185), channel_id=1, source_target_pairs={{0,4},{1,9},{2,6},{3,11},{4,0},{5,13},{6,2},{7,15},{8,12},{9,1},{1... | collective-permute-start | bytes 4718600 | tf_op jit(solution)/shard_map/ppermute | solution.py:515
  219.0 67.7 %collective-permute-start.18 = (bf16[1024,768]{1,0:T(8,128)(2,1)S(1)}, bf16[1024,768]{1,0:T(8,128)(2,1)}, u32[]{:S(2)}, u32[]{:S(2)}) collective-permute-start(bf16[1024,768]{1,0:T(8,128)(2,1)S(1)} %copy-done.11), channel_id=1, source_target_pairs={{0,4},{1,9},{2,6},{3,11},{4,0},{5,13},{6,2},{7,15},{8,12},{9,1},{1... | collective-permute-start | bytes 4718600 | tf_op jit(solution)/shard_map/ppermute | solution.py:515
  281.4 74.5 %collective-permute-start.26 = (bf16[768,1024]{1,0:T(8,128)(2,1)}, bf16[768,1024]{1,0:T(8,128)(2,1)}, u32[]{:S(2)}, u32[]{:S(2)}) collective-permute-start(bf16[768,1024]{1,0:T(8,128)(2,1)} %collective-permute-done.16.w1_ref), channel_id=1, source_target_pairs={{0,8},{1,5},{2,10},{3,7},{4,12},{5,1},{6,14},{7,3},{8,0},{9,13},{1... | collective-permute-start | bytes 4718600 | tf_op jit(solution)/shard_map/ppermute | solution.py:515
  286.6 69.3 %collective-permute-start.27 = (bf16[768,1024]{1,0:T(8,128)(2,1)}, bf16[768,1024]{1,0:T(8,128)(2,1)}, u32[]{:S(2)}, u32[]{:S(2)}) collective-permute-start(bf16[768,1024]{1,0:T(8,128)(2,1)} %collective-permute-done.17.w3_ref), channel_id=1, source_target_pairs={{0,8},{1,5},{2,10},{3,7},{4,12},{5,1},{6,14},{7,3},{8,0},{9,13},{1... | collective-permute-start | bytes 4718600 | tf_op jit(solution)/shard_map/ppermute | solution.py:515
  286.7 69.2 %collective-permute-start.28 = (bf16[1024,768]{1,0:T(8,128)(2,1)}, bf16[1024,768]{1,0:T(8,128)(2,1)S(1)}, u32[]{:S(2)}, u32[]{:S(2)}) collective-permute-start(bf16[1024,768]{1,0:T(8,128)(2,1)} %collective-permute-done.18.w2_ref), channel_id=1, source_target_pairs={{0,8},{1,5},{2,10},{3,7},{4,12},{5,1},{6,14},{7,3},{8,0},{9,13},{1... | collective-permute-start | bytes 4718600 | tf_op jit(solution)/shard_map/ppermute | solution.py:515
  464.3 157.6 %collective-permute-start.29 = (bf16[896,768]{1,0:T(8,128)(2,1)}, bf16[896,768]{1,0:T(8,128)(2,1)S(1)}, u32[]{:S(2)}, u32[]{:S(2)}) collective-permute-start(bf16[896,768]{1,0:T(8,128)(2,1)} %get-tuple-element.117), channel_id=1, source_target_pairs={{4,0},{9,1},{6,2},{11,3},{0,4},{13,5},{2,6},{15,7},{12,8},{1,9},{1... | collective-permute-start | bytes 4128776 | tf_op jit(solution)/shard_map/ppermute | solution.py:520
  482.8 166.7 %collective-permute-start.30 = (bf16[896,768]{1,0:T(8,128)(2,1)}, bf16[896,768]{1,0:T(8,128)(2,1)}, u32[]{:S(2)}, u32[]{:S(2)}) collective-permute-start(bf16[896,768]{1,0:T(8,128)(2,1)} %get-tuple-element.118), channel_id=1, source_target_pairs={{1,0},{0,1},{3,2},{2,3},{5,4},{4,5},{7,6},{6,7},{9,8},{8,9},{11,10... | collective-permute-start | bytes 4128776 | tf_op jit(solution)/shard_map/ppermute | solution.py:520
  482.8 166.7 %collective-permute-start.31 = (bf16[896,768]{1,0:T(8,128)(2,1)}, bf16[896,768]{1,0:T(8,128)(2,1)}, u32[]{:S(2)}, u32[]{:S(2)}) collective-permute-start(bf16[896,768]{1,0:T(8,128)(2,1)} %get-tuple-element.119), channel_id=1, source_target_pairs={{9,0},{4,1},{11,2},{6,3},{13,4},{0,5},{15,6},{2,7},{1,8},{12,9},{3... | collective-permute-start | bytes 4128776 | tf_op jit(solution)/shard_map/ppermute | solution.py:520
  483.9 165.6 %collective-permute-start.32 = (bf16[896,768]{1,0:T(8,128)(2,1)}, bf16[896,768]{1,0:T(8,128)(2,1)}, u32[]{:S(2)}, u32[]{:S(2)}) collective-permute-start(bf16[896,768]{1,0:T(8,128)(2,1)} %get-tuple-element.120), channel_id=1, source_target_pairs={{2,0},{3,1},{0,2},{1,3},{6,4},{7,5},{4,6},{5,7},{10,8},{11,9},{8,1... | collective-permute-start | bytes 4128776 | tf_op jit(solution)/shard_map/ppermute | solution.py:520
  526.4 124.6 %collective-permute-start.33 = (bf16[896,768]{1,0:T(8,128)(2,1)}, bf16[896,768]{1,0:T(8,128)(2,1)}, u32[]{:S(2)}, u32[]{:S(2)}) collective-permute-start(bf16[896,768]{1,0:T(8,128)(2,1)} %get-tuple-element.121), channel_id=1, source_target_pairs={{6,0},{11,1},{4,2},{9,3},{2,4},{15,5},{0,6},{13,7},{14,8},{3,9},{1... | collective-permute-start | bytes 4128776 | tf_op jit(solution)/shard_map/ppermute | solution.py:520
  622.0 70.8 %collective-permute-start.34 = (bf16[896,768]{1,0:T(8,128)(2,1)}, bf16[896,768]{1,0:T(8,128)(2,1)}, u32[]{:S(2)}, u32[]{:S(2)}) collective-permute-start(bf16[896,768]{1,0:T(8,128)(2,1)} %get-tuple-element.122), channel_id=1, source_target_pairs={{3,0},{2,1},{1,2},{0,3},{7,4},{6,5},{5,6},{4,7},{11,8},{10,9},{9,1... | collective-permute-start | bytes 4128776 | tf_op jit(solution)/shard_map/ppermute | solution.py:520
  649.5 49.0 %collective-permute-start.35 = (bf16[896,768]{1,0:T(8,128)(2,1)}, bf16[896,768]{1,0:T(8,128)(2,1)}, u32[]{:S(2)}, u32[]{:S(2)}) collective-permute-start(bf16[896,768]{1,0:T(8,128)(2,1)} %get-tuple-element.123), channel_id=1, source_target_pairs={{11,0},{6,1},{9,2},{4,3},{15,4},{2,5},{13,6},{0,7},{3,8},{14,9},{1... | collective-permute-start | bytes 4128776 | tf_op jit(solution)/shard_map/ppermute | solution.py:520
  649.5 91.0 %collective-permute-start.43 = (f32[768,1024]{1,0:T(8,128)}, f32[768,1024]{1,0:T(8,128)}, u32[]{:S(2)}, u32[]{:S(2)}) collective-permute-start(f32[768,1024]{1,0:T(8,128)} %get-tuple-element.145), channel_id=1, source_target_pairs={{0,8},{1,5},{2,10},{3,7},{4,12},{5,1},{6,14},{7,3},{8,0},{9,13},{1... | collective-permute-start | bytes 9437192 | tf_op jit(solution)/shard_map/ppermute | solution.py:515
  649.5 49.0 %collective-permute-start.36 = (bf16[896,768]{1,0:T(8,128)(2,1)}, bf16[896,768]{1,0:T(8,128)(2,1)}, u32[]{:S(2)}, u32[]{:S(2)}) collective-permute-start(bf16[896,768]{1,0:T(8,128)(2,1)} %get-tuple-element.137), channel_id=1, source_target_pairs={{4,0},{9,1},{6,2},{11,3},{0,4},{13,5},{2,6},{15,7},{12,8},{1,9},{1... | collective-permute-start | bytes 4128776 | tf_op jit(solution)/shard_map/ppermute | solution.py:520
  651.0 51.0 %collective-permute-start.37 = (bf16[896,768]{1,0:T(8,128)(2,1)}, bf16[896,768]{1,0:T(8,128)(2,1)}, u32[]{:S(2)}, u32[]{:S(2)}) collective-permute-start(bf16[896,768]{1,0:T(8,128)(2,1)} %get-tuple-element.138), channel_id=1, source_target_pairs={{1,0},{0,1},{3,2},{2,3},{5,4},{4,5},{7,6},{6,7},{9,8},{8,9},{11,10... | collective-permute-start | bytes 4128776 | tf_op jit(solution)/shard_map/ppermute | solution.py:520
  692.8 55.2 %collective-permute-start.59 = (f32[768,512]{1,0:T(8,128)}, f32[768,512]{1,0:T(8,128)S(1)}, u32[]{:S(2)}, u32[]{:S(2)}) collective-permute-start(f32[768,512]{1,0:T(8,128)} %get-tuple-element.172), channel_id=1, source_target_pairs={{0,8},{1,5},{2,10},{3,7},{4,12},{5,1},{6,14},{7,3},{8,0},{9,13},{1... | collective-permute-start | bytes 4718600 | tf_op jit(solution)/shard_map/ppermute | solution.py:515
  698.4 184.5 %collective-permute-start.56 = (f32[768,1024]{1,0:T(8,128)}, f32[768,1024]{1,0:T(8,128)}, u32[]{:S(2)}, u32[]{:S(2)}) collective-permute-start(f32[768,1024]{1,0:T(8,128)} %get-tuple-element.167), channel_id=1, source_target_pairs={{0,8},{1,5},{2,10},{3,7},{4,12},{5,1},{6,14},{7,3},{8,0},{9,13},{1... | collective-permute-start | bytes 9437192 | tf_op jit(solution)/shard_map/ppermute | solution.py:515
  698.5 37.7 %collective-permute-start.38 = (bf16[896,768]{1,0:T(8,128)(2,1)}, bf16[896,768]{1,0:T(8,128)(2,1)}, u32[]{:S(2)}, u32[]{:S(2)}) collective-permute-start(bf16[896,768]{1,0:T(8,128)(2,1)} %get-tuple-element.139), channel_id=1, source_target_pairs={{9,0},{4,1},{11,2},{6,3},{13,4},{0,5},{15,6},{2,7},{1,8},{12,9},{3... | collective-permute-start | bytes 4128776 | tf_op jit(solution)/shard_map/ppermute | solution.py:520
  702.0 36.4 %collective-permute-start.39 = (bf16[896,768]{1,0:T(8,128)(2,1)}, bf16[896,768]{1,0:T(8,128)(2,1)}, u32[]{:S(2)}, u32[]{:S(2)}) collective-permute-start(bf16[896,768]{1,0:T(8,128)(2,1)} %get-tuple-element.140), channel_id=1, source_target_pairs={{2,0},{3,1},{0,2},{1,3},{6,4},{7,5},{4,6},{5,7},{10,8},{11,9},{8,1... | collective-permute-start | bytes 4128776 | tf_op jit(solution)/shard_map/ppermute | solution.py:520
  738.4 151.1 %collective-permute-start.50 = (f32[1024,768]{1,0:T(8,128)}, f32[1024,768]{1,0:T(8,128)S(1)}, u32[]{:S(2)}, u32[]{:S(2)}) collective-permute-start(f32[1024,768]{1,0:T(8,128)} %get-tuple-element.156), channel_id=1, source_target_pairs={{0,8},{1,5},{2,10},{3,7},{4,12},{5,1},{6,14},{7,3},{8,0},{9,13},{1... | collective-permute-start | bytes 9437192 | tf_op jit(solution)/shard_map/ppermute | solution.py:515
  738.4 127.5 %collective-permute-start.58 = (f32[768,512]{1,0:T(8,128)}, f32[768,512]{1,0:T(8,128)S(1)}, u32[]{:S(2)}, u32[]{:S(2)}) collective-permute-start(f32[768,512]{1,0:T(8,128)} %get-tuple-element.171), channel_id=1, source_target_pairs={{0,8},{1,5},{2,10},{3,7},{4,12},{5,1},{6,14},{7,3},{8,0},{9,13},{1... | collective-permute-start | bytes 4718600 | tf_op jit(solution)/shard_map/ppermute | solution.py:515
  740.5 142.3 %collective-permute-start.47 = (f32[768,512]{1,0:T(8,128)}, f32[768,512]{1,0:T(8,128)S(1)}, u32[]{:S(2)}, u32[]{:S(2)}) collective-permute-start(f32[768,512]{1,0:T(8,128)} %get-tuple-element.150), channel_id=1, source_target_pairs={{0,8},{1,5},{2,10},{3,7},{4,12},{5,1},{6,14},{7,3},{8,0},{9,13},{1... | collective-permute-start | bytes 4718600 | tf_op jit(solution)/shard_map/ppermute | solution.py:515
  748.0 243.0 %collective-permute-start.44 = (f32[768,1024]{1,0:T(8,128)S(1)}, f32[768,1024]{1,0:T(8,128)}, u32[]{:S(2)}, u32[]{:S(2)}) collective-permute-start(f32[768,1024]{1,0:T(8,128)S(1)} %add.255), channel_id=1, source_target_pairs={{0,4},{1,9},{2,6},{3,11},{4,0},{5,13},{6,2},{7,15},{8,12},{9,1},{1... | collective-permute-start | bytes 9437192 | tf_op jit(solution)/shard_map/ppermute | solution.py:515
  865.9 42.8 %collective-permute-start.46 = (f32[768,512]{1,0:T(8,128)S(1)}, f32[768,512]{1,0:T(8,128)S(1)}, u32[]{:S(2)}, u32[]{:S(2)}) collective-permute-start(f32[768,512]{1,0:T(8,128)S(1)} %copy-done.25), channel_id=1, source_target_pairs={{0,8},{1,5},{2,10},{3,7},{4,12},{5,1},{6,14},{7,3},{8,0},{9,13},{1... | collective-permute-start | bytes 4718600 | tf_op jit(solution)/shard_map/ppermute | solution.py:515
  882.8 59.7 %collective-permute-start.53 = (f32[512,768]{1,0:T(8,128)S(1)}, f32[512,768]{1,0:T(8,128)S(1)}, u32[]{:S(2)}, u32[]{:S(2)}) collective-permute-start(f32[512,768]{1,0:T(8,128)S(1)} %copy-done.26), channel_id=1, source_target_pairs={{0,8},{1,5},{2,10},{3,7},{4,12},{5,1},{6,14},{7,3},{8,0},{9,13},{1... | collective-permute-start | bytes 4718600 | tf_op jit(solution)/shard_map/ppermute | solution.py:515
  882.9 108.0 %collective-permute-start.52 = (f32[512,768]{1,0:T(8,128)S(1)}, f32[512,768]{1,0:T(8,128)S(1)}, u32[]{:S(2)}, u32[]{:S(2)}) collective-permute-start(f32[512,768]{1,0:T(8,128)S(1)} %copy-done.24), channel_id=1, source_target_pairs={{0,8},{1,5},{2,10},{3,7},{4,12},{5,1},{6,14},{7,3},{8,0},{9,13},{1... | collective-permute-start | bytes 4718600 | tf_op jit(solution)/shard_map/ppermute | solution.py:515
  889.5 185.2 %collective-permute-start.57 = (f32[768,1024]{1,0:T(8,128)}, f32[768,1024]{1,0:T(8,128)}, u32[]{:S(2)}, u32[]{:S(2)}) collective-permute-start(f32[768,1024]{1,0:T(8,128)} %add.264), channel_id=1, source_target_pairs={{0,4},{1,9},{2,6},{3,11},{4,0},{5,13},{6,2},{7,15},{8,12},{9,1},{1... | collective-permute-start | bytes 9437192 | tf_op jit(solution)/shard_map/ppermute | solution.py:515
  908.8 166.0 %collective-permute-start.51 = (f32[1024,768]{1,0:T(8,128)}, f32[1024,768]{1,0:T(8,128)}, u32[]{:S(2)}, u32[]{:S(2)}) collective-permute-start(f32[1024,768]{1,0:T(8,128)} %add.260), channel_id=1, source_target_pairs={{0,4},{1,9},{2,6},{3,11},{4,0},{5,13},{6,2},{7,15},{8,12},{9,1},{1... | collective-permute-start | bytes 9437192 | tf_op jit(solution)/shard_map/ppermute | solution.py:515
  942.5 65.5 %collective-permute-start.40 = (bf16[896,768]{1,0:T(8,128)(2,1)}, bf16[896,768]{1,0:T(8,128)(2,1)S(1)}, u32[]{:S(2)}, u32[]{:S(2)}) collective-permute-start(bf16[896,768]{1,0:T(8,128)(2,1)} %get-tuple-element.141), channel_id=1, source_target_pairs={{6,0},{11,1},{4,2},{9,3},{2,4},{15,5},{0,6},{13,7},{14,8},{3,9},{1... | collective-permute-start | bytes 4128776 | tf_op jit(solution)/shard_map/ppermute | solution.py:520
  990.9 32.8 %collective-permute-start.41 = (bf16[896,768]{1,0:T(8,128)(2,1)}, bf16[896,768]{1,0:T(8,128)(2,1)}, u32[]{:S(2)}, u32[]{:S(2)}) collective-permute-start(bf16[896,768]{1,0:T(8,128)(2,1)} %get-tuple-element.142), channel_id=1, source_target_pairs={{3,0},{2,1},{1,2},{0,3},{7,4},{6,5},{5,6},{4,7},{11,8},{10,9},{9,1... | collective-permute-start | bytes 4128776 | tf_op jit(solution)/shard_map/ppermute | solution.py:520
  991.0 60.8 %collective-permute-start.42 = (bf16[896,768]{1,0:T(8,128)(2,1)}, bf16[896,768]{1,0:T(8,128)(2,1)}, u32[]{:S(2)}, u32[]{:S(2)}) collective-permute-start(bf16[896,768]{1,0:T(8,128)(2,1)} %get-tuple-element.143), channel_id=1, source_target_pairs={{11,0},{6,1},{9,2},{4,3},{15,4},{2,5},{13,6},{0,7},{3,8},{14,9},{1... | collective-permute-start | bytes 4128776 | tf_op jit(solution)/shard_map/ppermute | solution.py:520
  1008.0 62.8 %collective-permute-start.48 = (f32[16,768]{1,0:T(8,128)S(1)}, f32[16,768]{1,0:T(8,128)S(1)}, u32[]{:S(2)}, u32[]{:S(2)}) collective-permute-start(f32[16,768]{1,0:T(8,128)S(1)} %fusion.8), channel_id=1, source_target_pairs={{0,2},{1,3},{2,0},{3,1},{4,6},{5,7},{6,4},{7,5},{8,10},{9,11},{10,... | collective-permute-start | bytes 147464 | tf_op jit(solution)/shard_map/ppermute | solution.py:550
  (45 other events, 1899.3 us)
